TPU v7x, 32 devices: a whole 2x2x4 slice. The times are simulated.
32 devices in a mesh: fsdp: 2 (over x), ctx: 4 (over z), tp: 4 (over y, core).
Axes of the slice: x: 2, y: 2, z: 4, core: 2. Of those that a mesh axis runs over, the one named last changes fastest.
Arguments:
- tokens: bfloat16 [2, 2048, 3072], P('fsdp', 'ctx'), may hold values from -6 to 6
- segments: int32 [2, 2048], P('fsdp'), may hold values from 0 to 5, never falling along the last dimension, each value on 1 to 1024 neighbouring positions
- w_qkv: bfloat16 [3, 3072, 3072], P(None, ('fsdp', 'ctx'), 'tp'), may hold values from -1 to 1
- w_out: bfloat16 [3072, 3072], P('tp', ('fsdp', 'ctx')), may hold values from -1.75 to 1.75
- w_gate_up: bfloat16 [2, 3072, 8192], P(None, ('fsdp', 'ctx'), 'tp'), may hold values from -0.109375 to 0.109375
- w_down: bfloat16 [8192, 3072], P('tp', ('fsdp', 'ctx')), may hold values from -0.0625 to 0.0625
- norm_attn: bfloat16 [3072], P(('fsdp', 'ctx')), may hold values from 0.099609375 to 1.8984375
- norm_mlp: bfloat16 [3072], P(('fsdp', 'ctx')), may hold values from 0.099609375 to 1.8984375
- cotangent: bfloat16 [2, 2048, 3072], P('fsdp', 'ctx'), may hold values from -6 to 6
Outputs:
- output: bfloat16 [2, 2048, 3072], P('fsdp', 'ctx')
- grad_tokens: bfloat16 [2, 2048, 3072], P('fsdp', 'ctx')
- grad_qkv: float32 [3, 3072, 3072], P(None, ('fsdp', 'ctx'), 'tp')
- grad_out: float32 [3072, 3072], P('tp', ('fsdp', 'ctx'))
- grad_gate_up: float32 [2, 3072, 8192], P(None, ('fsdp', 'ctx'), 'tp')
- grad_down: float32 [8192, 3072], P('tp', ('fsdp', 'ctx'))
- grad_norm_attn: float32 [3072], P(('fsdp', 'ctx'))
- grad_norm_mlp: float32 [3072], P(('fsdp', 'ctx'))
Inputs may be any that keep to these rules, and one draw needn't show every extreme that they name: `segments`: document numbers never fall along a sequence and begin at 0; every one of the 6 numbers is used, each document has 1 to 1024 tokens and one has exactly 1024.
All inputs are finite; a program needn't handle non-finite values.
Results may differ from a plain program's by a relative error of at most 0.014.
Values may be sent and summed in bfloat16 or wider, within the bound.
A program may use at most 384 MiB of HBM per device.

v0:
```python
import math

import jax
import jax.numpy as jnp
from jax import lax
from jax.sharding import PartitionSpec as P

HD = 96


EPSILON = 1e-05
MASK_FILL = -1e30
ROPE_BASE = 10000.0


def doc_positions(segment_row):
    places = jnp.arange(segment_row.shape[0], dtype=jnp.int32)
    starts = jnp.concatenate([jnp.ones((1,), dtype=jnp.bool_), segment_row[1:] != segment_row[:-1]])
    first = lax.cummax(jnp.where(starts, places, jnp.zeros_like(places)), axis=0)
    return places - first


def rope_tables(positions, head_dim):
    half = head_dim // 2
    freqs = ROPE_BASE ** (-(jnp.arange(half, dtype=jnp.float32) * 2.0 / head_dim))
    angles = positions.astype(jnp.float32)[..., None] * freqs
    cosine = jnp.cos(angles)
    sine = jnp.sin(angles)
    return (jnp.concatenate([cosine, cosine], axis=-1), jnp.concatenate([sine, sine], axis=-1))


def rotate(values_in, cosine, sine):
    half = values_in.shape[-1] // 2
    turned = jnp.concatenate([-values_in[..., half:], values_in[..., :half]], axis=-1)
    return values_in * cosine[..., None, :] + turned * sine[..., None, :]


def unrotate(grads_in, cosine, sine):
    half = grads_in.shape[-1] // 2
    weighted = grads_in * sine[..., None, :]
    turned = jnp.concatenate([weighted[..., half:], -weighted[..., :half]], axis=-1)
    return grads_in * cosine[..., None, :] + turned


def rms_scale(values_in):
    return lax.rsqrt(jnp.mean(values_in * values_in, axis=-1, keepdims=True) + EPSILON)


def score_block(query_blk, keys_all, seg_query, seg_keys, start, scale):
    scores = (
        jnp.einsum("qhd,khd->hqk", query_blk, keys_all, preferred_element_type=jnp.float32) * scale
    )
    query_pos = start + jnp.arange(query_blk.shape[0], dtype=jnp.int32)
    key_pos = jnp.arange(keys_all.shape[0], dtype=jnp.int32)
    allowed = (key_pos[None, :] <= query_pos[:, None]) & (seg_keys[None, :] == seg_query[:, None])
    return jnp.where(allowed[None], scores, MASK_FILL)


def attend_forward(query_seq, keys_seq, values_seq, segment_row, block, scale):
    length = query_seq.shape[0]

    def one_block(index):
        start = index * block
        query_blk = lax.dynamic_slice_in_dim(query_seq, start, block, 0)
        seg_query = lax.dynamic_slice_in_dim(segment_row, start, block, 0)
        scores = score_block(query_blk, keys_seq, seg_query, segment_row, start, scale)
        peak = jnp.max(scores, axis=-1, keepdims=True)
        expo = jnp.exp(scores - peak)
        total = jnp.sum(expo, axis=-1, keepdims=True)
        probs = expo / total
        mixed = jnp.einsum(
            "hqk,khd->qhd",
            probs.astype(jnp.bfloat16),
            values_seq,
            preferred_element_type=jnp.float32,
        )
        return (mixed.astype(jnp.bfloat16), peak[..., 0] + jnp.log(total[..., 0]))

    mixed, logsum = lax.map(one_block, jnp.arange(length // block, dtype=jnp.int32))
    return (mixed.reshape(length, -1), logsum)


def attend_backward(query_seq, keys_seq, values_seq, grad_seq, logsum, segment_row, block, scale):
    length = query_seq.shape[0]

    def one_block(carry, index):
        grad_keys, grad_values = carry
        start = index * block
        query_blk = lax.dynamic_slice_in_dim(query_seq, start, block, 0)
        grad_blk = lax.dynamic_slice_in_dim(grad_seq, start, block, 0)
        seg_query = lax.dynamic_slice_in_dim(segment_row, start, block, 0)
        scores = score_block(query_blk, keys_seq, seg_query, segment_row, start, scale)
        probs = jnp.exp(scores - logsum[index][..., None])
        grad_values = grad_values + jnp.einsum(
            "hqk,qhd->khd", probs.astype(jnp.bfloat16), grad_blk, preferred_element_type=jnp.float32
        )
        grad_probs = jnp.einsum(
            "qhd,khd->hqk", grad_blk, values_seq, preferred_element_type=jnp.float32
        )
        inner = jnp.sum(probs * grad_probs, axis=-1, keepdims=True)
        grad_scores = (probs * (grad_probs - inner)).astype(jnp.bfloat16)
        grad_query = (
            jnp.einsum("hqk,khd->qhd", grad_scores, keys_seq, preferred_element_type=jnp.float32)
            * scale
        )
        grad_keys = (
            grad_keys
            + jnp.einsum("hqk,qhd->khd", grad_scores, query_blk, preferred_element_type=jnp.float32)
            * scale
        )
        return ((grad_keys, grad_values), grad_query)

    zeros_kv = jnp.zeros(keys_seq.shape, jnp.float32)
    (grad_keys, grad_values), grad_query = lax.scan(
        one_block, (zeros_kv, zeros_kv), jnp.arange(length // block, dtype=jnp.int32)
    )
    return (
        grad_query.reshape(length, -1),
        grad_keys.reshape(length, -1),
        grad_values.reshape(length, -1),
    )


def shards(tokens, segments, w_qkv, w_out, w_gate_up, w_down, norm_attn, norm_mlp, cotangent):
    qkv_full, out_full, gu_full, down_full, gain_attn, gain_mlp = (
        lax.all_gather(w_qkv, ("fsdp", "ctx"), axis=1, tiled=True),
        lax.all_gather(w_out, ("fsdp", "ctx"), axis=1, tiled=True),
        lax.all_gather(w_gate_up, ("fsdp", "ctx"), axis=1, tiled=True),
        lax.all_gather(w_down, ("fsdp", "ctx"), axis=1, tiled=True),
        lax.all_gather(norm_attn, ("fsdp", "ctx"), axis=0, tiled=True),
        lax.all_gather(norm_mlp, ("fsdp", "ctx"), axis=0, tiled=True),
    )
    seqs, rows, width = tokens.shape
    length = segments.shape[1]
    heads_tp = qkv_full.shape[2] // HD
    heads_dev = heads_tp // lax.axis_size("ctx")
    block = min(512, length)
    scale = 1.0 / math.sqrt(HD)
    offset = lax.axis_index("ctx") * rows
    resid_in = tokens.reshape(seqs * rows, width).astype(jnp.float32)
    scale_one = rms_scale(resid_in)
    unit_one = resid_in * scale_one
    normed1 = (unit_one * gain_attn.astype(jnp.float32)).astype(jnp.bfloat16)
    projected = jnp.einsum("rd,cde->cre", normed1, qkv_full, preferred_element_type=jnp.float32)
    positions_all = jax.vmap(doc_positions)(segments)
    local_pos = lax.dynamic_slice_in_dim(positions_all, offset, rows, 1)
    cosine, sine = rope_tables(local_pos, HD)
    query_rows = (
        rotate(projected[0].reshape(seqs, rows, heads_tp, HD), cosine, sine)
        .astype(jnp.bfloat16)
        .reshape(seqs, rows, -1)
    )
    keys_rows = (
        rotate(projected[1].reshape(seqs, rows, heads_tp, HD), cosine, sine)
        .astype(jnp.bfloat16)
        .reshape(seqs, rows, -1)
    )
    values_rows = projected[2].astype(jnp.bfloat16).reshape(seqs, rows, -1)
    headed = lax.all_to_all(
        jnp.stack([query_rows, keys_rows, values_rows]),
        "ctx",
        split_axis=3,
        concat_axis=2,
        tiled=True,
    )
    seq_index = 0
    mixed_seq, logsum_seq = attend_forward(
        headed[0, seq_index].reshape(length, heads_dev, HD),
        headed[1, seq_index].reshape(length, heads_dev, HD),
        headed[2, seq_index].reshape(length, heads_dev, HD),
        segments[seq_index],
        block,
        scale,
    )
    mixed_list = [mixed_seq]
    logsum_list = [logsum_seq]
    attn_rows = lax.all_to_all(
        jnp.stack(mixed_list), "ctx", split_axis=1, concat_axis=2, tiled=True
    )
    attn_flat = attn_rows.reshape(seqs * rows, -1)
    attn_part = jnp.dot(attn_flat, out_full, preferred_element_type=jnp.float32)
    hidden1 = resid_in + lax.psum(attn_part, "tp")
    scale_two = rms_scale(hidden1)
    unit_two = hidden1 * scale_two
    normed2 = (unit_two * gain_mlp.astype(jnp.float32)).astype(jnp.bfloat16)
    gate_up = jnp.einsum("rd,cdf->crf", normed2, gu_full, preferred_element_type=jnp.float32)
    sigma = jax.nn.sigmoid(gate_up[0])
    silu_gate = gate_up[0] * sigma
    act = (silu_gate * gate_up[1]).astype(jnp.bfloat16)
    down_part = jnp.dot(act, down_full, preferred_element_type=jnp.float32)
    output = (
        (hidden1 + lax.psum(down_part.astype(jnp.bfloat16), "tp").astype(jnp.float32))
        .astype(jnp.bfloat16)
        .reshape(seqs, rows, width)
    )
    qkv_full, out_full, gu_full, down_full, gain_attn, gain_mlp = (
        lax.all_gather(w_qkv, ("fsdp", "ctx"), axis=1, tiled=True),
        lax.all_gather(w_out, ("fsdp", "ctx"), axis=1, tiled=True),
        lax.all_gather(w_gate_up, ("fsdp", "ctx"), axis=1, tiled=True),
        lax.all_gather(w_down, ("fsdp", "ctx"), axis=1, tiled=True),
        lax.all_gather(norm_attn, ("fsdp", "ctx"), axis=0, tiled=True),
        lax.all_gather(norm_mlp, ("fsdp", "ctx"), axis=0, tiled=True),
    )
    grad_in = cotangent.reshape(seqs * rows, width)
    grad_down_part = jnp.einsum("rf,rd->fd", act, grad_in, preferred_element_type=jnp.float32)
    grad_act = jnp.einsum("rd,fd->rf", grad_in, down_full, preferred_element_type=jnp.float32)
    grad_gate = grad_act * gate_up[1] * sigma * (1.0 + gate_up[0] * (1.0 - sigma))
    grad_up = grad_act * silu_gate
    grad_gu = jnp.stack([grad_gate, grad_up]).astype(jnp.bfloat16)
    grad_gu_part = jnp.einsum("rd,crf->cdf", normed2, grad_gu, preferred_element_type=jnp.float32)
    grad_normed2 = lax.psum(
        jnp.einsum("crf,cdf->rd", grad_gu, gu_full, preferred_element_type=jnp.float32), "tp"
    )
    grad_gain_mlp = jnp.sum(grad_normed2 * unit_two, axis=0)
    grad_unit_two = grad_normed2 * gain_mlp.astype(jnp.float32)
    grad_hidden1 = grad_in.astype(jnp.float32) + scale_two * (
        grad_unit_two - unit_two * jnp.mean(grad_unit_two * unit_two, axis=-1, keepdims=True)
    )
    grad_branch = grad_hidden1.astype(jnp.bfloat16)
    grad_out_part = jnp.einsum(
        "re,rd->ed", attn_flat, grad_branch, preferred_element_type=jnp.float32
    )
    grad_attn = jnp.einsum(
        "rd,ed->re", grad_branch, out_full, preferred_element_type=jnp.float32
    ).astype(jnp.bfloat16)
    grad_headed = lax.all_to_all(
        grad_attn.reshape(seqs, rows, -1), "ctx", split_axis=2, concat_axis=1, tiled=True
    )
    seq_index = 0
    grad_q_seq, grad_k_seq, grad_v_seq = attend_backward(
        headed[0, seq_index].reshape(length, heads_dev, HD),
        headed[1, seq_index].reshape(length, heads_dev, HD),
        headed[2, seq_index].reshape(length, heads_dev, HD),
        grad_headed[seq_index].reshape(length, heads_dev, HD),
        logsum_list[seq_index],
        segments[seq_index],
        block,
        scale,
    )
    grad_q_list = [grad_q_seq.astype(jnp.bfloat16)]
    grad_k_list = [grad_k_seq.astype(jnp.bfloat16)]
    grad_v_list = [grad_v_seq.astype(jnp.bfloat16)]
    grad_back = lax.all_to_all(
        jnp.stack([jnp.stack(grad_q_list), jnp.stack(grad_k_list), jnp.stack(grad_v_list)]),
        "ctx",
        split_axis=2,
        concat_axis=3,
        tiled=True,
    )
    grad_query_pre = unrotate(
        grad_back[0].reshape(seqs, rows, heads_tp, HD).astype(jnp.float32), cosine, sine
    )
    grad_keys_pre = unrotate(
        grad_back[1].reshape(seqs, rows, heads_tp, HD).astype(jnp.float32), cosine, sine
    )
    grad_proj = jnp.stack(
        [
            grad_query_pre.astype(jnp.bfloat16).reshape(seqs * rows, -1),
            grad_keys_pre.astype(jnp.bfloat16).reshape(seqs * rows, -1),
            grad_back[2].reshape(seqs * rows, -1),
        ]
    )
    grad_qkv_part = jnp.einsum(
        "rd,cre->cde", normed1, grad_proj, preferred_element_type=jnp.float32
    )
    grad_normed1 = lax.psum(
        jnp.einsum("cre,cde->rd", grad_proj, qkv_full, preferred_element_type=jnp.float32), "tp"
    )
    grad_gain_attn = jnp.sum(grad_normed1 * unit_one, axis=0)
    grad_unit_one = grad_normed1 * gain_attn.astype(jnp.float32)
    grad_tokens = grad_hidden1 + scale_one * (
        grad_unit_one - unit_one * jnp.mean(grad_unit_one * unit_one, axis=-1, keepdims=True)
    )
    grad_tokens = grad_tokens.astype(jnp.bfloat16).reshape(seqs, rows, width)
    shares = (
        lax.psum_scatter(grad_qkv_part, ("fsdp", "ctx"), scatter_dimension=1, tiled=True),
        lax.psum_scatter(grad_out_part, ("fsdp", "ctx"), scatter_dimension=1, tiled=True),
        lax.psum_scatter(grad_gu_part, ("fsdp", "ctx"), scatter_dimension=1, tiled=True),
        lax.psum_scatter(grad_down_part, ("fsdp", "ctx"), scatter_dimension=1, tiled=True),
        lax.psum_scatter(grad_gain_attn, ("fsdp", "ctx"), scatter_dimension=0, tiled=True),
        lax.psum_scatter(grad_gain_mlp, ("fsdp", "ctx"), scatter_dimension=0, tiled=True),
    )
    return (output, grad_tokens, shares[0], shares[1], shares[2], shares[3], shares[4], shares[5])


def solution(mesh):
    in_specs = (
        P("fsdp", "ctx", None),
        P("fsdp", None),
        P(None, ("fsdp", "ctx"), "tp"),
        P("tp", ("fsdp", "ctx")),
        P(None, ("fsdp", "ctx"), "tp"),
        P("tp", ("fsdp", "ctx")),
        P(("fsdp", "ctx")),
        P(("fsdp", "ctx")),
        P("fsdp", "ctx", None),
    )
    out_specs = (
        P("fsdp", "ctx", None),
        P("fsdp", "ctx", None),
        P(None, ("fsdp", "ctx"), "tp"),
        P("tp", ("fsdp", "ctx")),
        P(None, ("fsdp", "ctx"), "tp"),
        P("tp", ("fsdp", "ctx")),
        P(("fsdp", "ctx")),
        P(("fsdp", "ctx")),
    )
    return jax.shard_map(shards, mesh=mesh, in_specs=in_specs, out_specs=out_specs, check_vma=False)
```

profile of v0, /device:TPU:0, one launch (start us, length us, event | category | flops | bytes accessed | tf_op | source)
XLA Modules:
  0.0 3742.5 jit_solution(10813770452052715159)
XLA Ops:
  8.6 29.4 all-gather
  49.8 158.4 %all-gather.7.cloned.1.call-done = bf16[3,3072,768]{2,1,0:T(8,128)(2,1)} async-done(((bf16[3,384,768]{2,1,0:T(8,128)(2,1)}), bf16[3,3072,768]{2,1,0:T(8,128)(2,1)}) %all-gather.7.cloned.1.call-update) | async-done | bytes 14155792 | tf_op jit(solution)/shard_map/all_gather | solution.py:126
  208.2 10.7 convolution_bitcast_fusion.5
  228.9 4.0 fusion.74
  233.2 4.2 copy.207
  242.4 105.7 %all-to-all-done = bf16[3,1,512,768]{2,0,1,3:T(4,128)(2,1)S(1)} async-done(((bf16[3,1,512,768]{2,0,1,3:T(4,128)(2,1)}), bf16[3,1,512,768]{2,0,1,3:T(4,128)(2,1)S(1)}, u32[]{:S(2)}, u32[]{:S(2)}) %all-to-all-start) | async-done | bytes 2359328 | tf_op jit(solution)/shard_map/all_to_all | solution.py:159
  352.5 44.3 %while.27 = (s32[]{:T(128)}, bf16[4,512,2,96]{1,3,2,0:T(8,128)(2,1)}, f32[4,2,512]{2,1,0:T(2,128)}, s32[4]{0:T(128)S(1)}, s32[1,2048]{1,0:T(1,128)S(1)}, /*index...) while((s32[]{:T(128)}, ...), condition=%wide.region_6.7_spmd, body=%wide.region_3.6_spmd.sunk | while | flops 833715712 | bytes 31377620 | solution.py:79
  403.4 12.6 reduce.4
  418.4 17.0 all_to_all.60
  437.9 4.5 copy.214
  443.2 7.1 fusion.103
  451.6 36.1 all-gather.1
  487.7 80.0 %all-reduce.8.cloned.1.call-done = f32[512,3072]{1,0:T(8,128)} async-done(((f32[512,3072]{1,0:T(8,128)}), f32[512,3072]{1,0:T(8,128)}) %all-reduce.8.cloned.1.call-update) | async-done | bytes 6291472 | tf_op jit(solution)/shard_map/psum | solution.py:182
  567.8 7.2 multiply_reduce_fusion.3
  575.0 474.8 %all-gather.11.cloned.1.call-done = bf16[2,3072,2048]{2,1,0:T(8,128)(2,1)} async-done(((bf16[2,384,2048]{2,1,0:T(8,128)(2,1)}), bf16[2,3072,2048]{2,1,0:T(8,128)(2,1)}) %all-gather.11.cloned.1.call-update) | async-done | bytes 25165840 | tf_op jit(solution)/shard_map/all_gather | solution.py:128
  1049.8 21.9 convolution_bitcast_fusion.4
  1071.6 157.4 %all-gather.13.cloned.1.call-done = bf16[2048,3072]{1,0:T(8,128)(2,1)} async-done(((bf16[2048,384]{1,0:T(8,128)(2,1)}), bf16[2048,3072]{1,0:T(8,128)(2,1)}) %all-gather.13.cloned.1.call-update) | async-done | bytes 12582928 | tf_op jit(solution)/shard_map/all_gather | solution.py:129
  1229.0 16.1 fusion.70
  1245.1 19.6 convolution_bitcast_fusion.3
  1264.8 14.8 convolution_convert_fusion
  1279.7 103.0 %all-reduce.12.cloned.1.call-done = f32[512,3072]{1,0:T(8,128)} async-done(((f32[512,3072]{1,0:T(8,128)}), f32[512,3072]{1,0:T(8,128)}) %all-reduce.12.cloned.1.call-update) | async-done | bytes 6291472 | tf_op jit(solution)/shard_map/psum | solution.py:211
  1382.7 6.1 multiply_reduce_fusion.1
  1388.8 65.5 %all-reduce.10.cloned.1.call-done = bf16[512,3072]{1,0:T(8,128)(2,1)} async-done(((bf16[512,3072]{1,0:T(8,128)(2,1)}), bf16[512,3072]{1,0:T(8,128)(2,1)}) %all-reduce.10.cloned.1.call-update) | async-done | bytes 3145744 | tf_op jit(solution)/shard_map/psum | solution.py:192
  1454.3 9.5 multiply_add_fusion
  1466.5 5.9 fusion.82
  1475.8 6.3 reduce.5
  1484.5 4.8 all-to-all-start.2
  1489.3 19.9 all-to-all-done.2
  1518.8 130.5 %while.28 = (s32[]{:T(128)}, f32[2048,2,96]{0,2,1:T(8,128)S(1)}, f32[2048,2,96]{0,2,1:T(8,128)}, bf16[4,512,2,96]{1,3,2,0:T(8,128)(2,1)}, s32[4]{0:T(128)S(1)}, ...) while((s32[]{:T(128)}, f32[2048,2,96]{0,2,1:T(8,128)S(1)}, ...), condition=%wide.region_14.15_spmd.clone, body=%wide.region_12.14_spmd.clone.sunk | while | flops 2049932800 | bytes 144095792 | solution.py:114
  1520.2 5.5 fusion.156
  1529.4 6.9 multiply_reduce_fusion.5
  1536.3 4.0 multiply_convert_fusion.6
  1543.7 5.3 fusion.159
  1552.8 5.5 fusion.156
  1561.9 6.9 multiply_reduce_fusion.5
  1568.9 4.0 multiply_convert_fusion.6
  1576.3 5.3 fusion.159
  1585.4 5.5 fusion.156
  1594.5 6.9 multiply_reduce_fusion.5
  1601.5 4.0 multiply_convert_fusion.6
  1608.9 5.3 fusion.159
  1618.0 5.5 fusion.156
  1627.1 6.9 multiply_reduce_fusion.5
  1634.0 4.0 multiply_convert_fusion.6
  1641.5 5.3 fusion.159
  1655.7 4.8 copy.219
  1660.5 5.0 all-to-all-start.3
  1667.2 91.0 %all-to-all-done.3 = bf16[3,1,2048,192]{3,0,1,2:T(4,128)(2,1)} async-done(((bf16[3,1,2048,192]{3,0,1,2:T(4,128)(2,1)}), bf16[3,1,2048,192]{3,0,1,2:T(4,128)(2,1)}, u32[]{:S(2)}, u32[]{:S(2)}) %all-to-all-start.3) | async-done | bytes 2359328 | tf_op jit(solution)/shard_map/all_to_all | solution.py:243
  1758.2 6.9 copy.221
  1790.2 12.4 convolution_bitcast_fusion.2
  1804.5 15.0 convolution_bitcast_fusion.1
  1820.2 24.8 convolution_bitcast_fusion
  1845.1 9.2 fusion.75
  1854.4 17.2 fusion.63
  1873.5 47.3 %all-reduce.14.cloned.1.call-done = f32[512,3072]{1,0:T(8,128)} async-done(((f32[512,3072]{1,0:T(8,128)}), f32[512,3072]{1,0:T(8,128)}) %all-reduce.14.cloned.1.call-update) | async-done | bytes 6291472 | tf_op jit(solution)/shard_map/psum | solution.py:266
  1920.9 3.9 fusion.49
  1924.8 39.6 %all-reduce.2 = (f32[3072]{0:T(1024)S(1)}, f32[3072]{0:T(1024)S(1)}) all-reduce(f32[3072]{0:T(1024)S(1)} %get-tuple-element.222, f32[3072]{0:T(1024)S(1)} %copy-done.29), channel_id=6, replica_groups=mesh['fsdp'=2,'ctx'=4,'tp'=4] {'fsdp','ctx'}, use_global_device_ids=true, to_apply=%region_22.23.clone | all-reduce | flops 6144 | bytes 49152
  1965.8 7.1 fusion.61
  1972.8 401.3 %reduce-scatter.5.cloned.1.call-done = f32[3,384,768]{1,2,0:T(8,128)} async-done(((f32[3,3072,768]{1,2,0:T(8,128)}), f32[3,384,768]{1,2,0:T(8,128)}) %reduce-scatter.5.cloned.1.call-update) | async-done | bytes 3538960 | tf_op jit(solution)/shard_map/reduce_scatter | solution.py:276
  2374.1 5.2 copy.231
  2379.3 784.1 %reduce-scatter.9.cloned.1.call-done = f32[2,384,2048]{1,2,0:T(8,128)} async-done(((f32[2,3072,2048]{1,2,0:T(8,128)}), f32[2,384,2048]{1,2,0:T(8,128)}) %reduce-scatter.9.cloned.1.call-update) | async-done | bytes 6291472 | tf_op jit(solution)/shard_map/reduce_scatter | solution.py:278
  3163.4 6.6 copy.232
  3170.0 158.9 %reduce-scatter.7.cloned.1.call-done = f32[768,384]{1,0:T(8,128)} async-done(((f32[768,3072]{1,0:T(8,128)}), f32[768,384]{1,0:T(8,128)}) %reduce-scatter.7.cloned.1.call-update) | async-done | bytes 1179664 | tf_op jit(solution)/shard_map/reduce_scatter | solution.py:277
  3328.9 406.6 %reduce-scatter.11.cloned.1.call-done = f32[2048,384]{1,0:T(8,128)} async-done(((f32[2048,3072]{1,0:T(8,128)}), f32[2048,384]{1,0:T(8,128)}) %reduce-scatter.11.cloned.1.call-update) | async-done | bytes 3145744 | tf_op jit(solution)/shard_map/reduce_scatter | solution.py:279
  (305 shorter events, 177.4 us)
Async XLA Ops:
  7.2 201.1 %all-gather.7.cloned.1.call-start = ((), (), s32[]{:S(2)}) async-start(), calls=%async_computation.8 | async-start | bytes 15925248 | tf_op jit(solution)/shard_map/all_gather | solution.py:126
  38.0 170.2 %copy-start.27 = (f32[8,1,384]{2,1,0:T(1,128)}, f32[8,1,384]{2,1,0:T(1,128)S(1)}, u32[]{:S(2)}) copy-start(f32[8,1,384]{2,1,0:T(1,128)S(1)} %convert_element_type.264) | copy-start | bytes 36868
  40.2 8.9 copy-start.13
  41.6 7.5 copy-start.2
  49.8 169.1 %copy-start.32 = (f32[512]{0:T(512)}, f32[512]{0:T(512)S(1)}, u32[]{:S(2)}) copy-start(f32[512]{0:T(512)S(1)} %add_rsqrt_fusion.1) | copy-start | bytes 6148
  218.9 2.4 copy-start.7
  227.0 2.0 copy-start.11
  228.9 4.0 copy-start.12
  237.5 110.6 %all-to-all-start = ((bf16[3,1,512,768]{2,0,1,3:T(4,128)(2,1)}), bf16[3,1,512,768]{2,0,1,3:T(4,128)(2,1)S(1)}, u32[]{:S(2)}, u32[]{:S(2)}) async-start(bf16[3,1,512,768]{2,0,1,3:T(4,128)(2,1)} %copy.207), calls=%async_computation | async-start | bytes 6291456 | tf_op jit(solution)/shard_map/all_to_all | solution.py:159
  241.2 202.0 %all-gather.9.cloned.1.call-start = ((), (), s32[]{:S(2)}) async-start(), calls=%async_computation.9 | async-start | bytes 5308416 | tf_op jit(solution)/shard_map/all_gather | solution.py:127
  241.9 325.9 %all-reduce.8.cloned.1.call-start = ((), (), s32[]{:S(2)}) async-start(), calls=%async_computation.10 | async-start | bytes 12582912 | tf_op jit(solution)/shard_map/psum | solution.py:182
  349.4 3.0 copy-start.15
  396.7 21.6 copy-start.8
  443.2 7.2 copy-start.9
  450.4 599.4 %all-gather.11.cloned.1.call-start = ((), (), s32[]{:S(2)}) async-start(), calls=%async_computation.11 | async-start | bytes 28311552 | tf_op jit(solution)/shard_map/all_gather | solution.py:128
  450.9 778.1 %all-gather.13.cloned.1.call-start = ((), (), s32[]{:S(2)}) async-start(), calls=%async_computation.12 | async-start | bytes 14155776 | tf_op jit(solution)/shard_map/all_gather | solution.py:129
  451.5 931.1 %all-reduce.12.cloned.1.call-start = ((), (), s32[]{:S(2)}) async-start(), calls=%async_computation.14 | async-start | bytes 12582912 | tf_op jit(solution)/shard_map/psum | solution.py:211
  487.7 966.6 %copy-start.25 = (f32[8,1,384]{2,1,0:T(1,128)}, f32[8,1,384]{2,1,0:T(1,128)S(1)}, u32[]{:S(2)}) copy-start(f32[8,1,384]{2,1,0:T(1,128)S(1)} %convert_element_type.265) | copy-start | bytes 36868
  575.0 879.3 %copy-start.30 = (f32[512]{0:T(512)}, f32[512]{0:T(512)S(1)}, u32[]{:S(2)}) copy-start(f32[512]{0:T(512)S(1)} %add_rsqrt_fusion) | copy-start | bytes 6148
  1264.7 189.5 %all-reduce.10.cloned.1.call-start = ((), (), s32[]{:S(2)}) async-start(), calls=%async_computation.13 | async-start | bytes 6291456 | tf_op jit(solution)/shard_map/psum | solution.py:192
  1463.8 2.6 copy-start.1
  1484.5 24.7 all-to-all-start.2
  1489.3 29.6 copy-start.16
  1518.8 6.8 copy-start.4
  1529.3 6.9 slice-start
  1529.3 6.9 slice-start.1
  1540.2 3.4 copy-start.17
  1543.7 5.4 copy-start
  1543.7 5.4 copy-start.22
  1549.0 2.4 copy-start.5
  1551.4 6.8 copy-start.4
  1561.9 6.9 slice-start
  1561.9 6.9 slice-start.1
  1572.8 3.4 copy-start.17
  1576.3 5.4 copy-start
  1576.3 5.4 copy-start.22
  1581.6 2.4 copy-start.5
  1584.0 6.8 copy-start.4
  1594.5 6.9 slice-start
  1594.5 6.9 slice-start.1
  1605.4 3.4 copy-start.17
  1608.9 5.4 copy-start
  1608.9 5.4 copy-start.22
  1614.2 2.4 copy-start.5
  1616.6 6.8 copy-start.4
  1627.1 6.9 slice-start
  1627.1 6.9 slice-start.1
  1638.0 3.4 copy-start.17
  1641.4 5.4 copy-start
  1641.4 5.4 copy-start.22
  1646.8 2.4 copy-start.5
  1649.4 3.5 copy-start.24
  1660.5 5.0 copy-start.6
  1660.5 97.8 %all-to-all-start.3 = ((bf16[3,1,2048,192]{3,0,1,2:T(4,128)(2,1)}), bf16[3,1,2048,192]{3,0,1,2:T(4,128)(2,1)}, u32[]{:S(2)}, u32[]{:S(2)}) async-start(bf16[3,1,2048,192]{3,0,1,2:T(4,128)(2,1)} %copy.219), calls=%async_computation.3 | async-start | bytes 8388608 | tf_op jit(solution)/shard_map/all_to_all | solution.py:243
  1665.5 255.4 %all-reduce.14.cloned.1.call-start = ((), (), s32[]{:S(2)}) async-start(), calls=%async_computation.15 | async-start | bytes 12582912 | tf_op jit(solution)/shard_map/psum | solution.py:266
  1765.2 5.3 copy-start.14
  1779.8 5.9 copy-start.10
  1785.7 4.5 copy-start.21
  1802.6 1.9 copy-start.33
  1802.7 571.5 %reduce-scatter.5.cloned.1.call-start = ((), (), s32[]{:S(2)}) async-start(), calls=%async_computation.16 | async-start | bytes 31850496 | tf_op jit(solution)/shard_map/reduce_scatter | solution.py:276
  1819.5 1343.9 %reduce-scatter.9.cloned.1.call-start = ((), (), s32[]{:S(2)}) async-start(), calls=%async_computation.18 | async-start | bytes 56623104 | tf_op jit(solution)/shard_map/reduce_scatter | solution.py:278
  1845.1 1483.8 %reduce-scatter.7.cloned.1.call-start = ((), (), s32[]{:S(2)}) async-start(), calls=%async_computation.17 | async-start | bytes 10616832 | tf_op jit(solution)/shard_map/reduce_scatter | solution.py:277
  1854.3 1881.1 %reduce-scatter.11.cloned.1.call-start = ((), (), s32[]{:S(2)}) async-start(), calls=%async_computation.19 | async-start | bytes 28311552 | tf_op jit(solution)/shard_map/reduce_scatter | solution.py:279
  1873.5 51.3 %copy-start.29 = (f32[3072]{0:T(1024)S(1)}, f32[3072]{0:T(1024)}, u32[]{:S(2)}) copy-start(f32[3072]{0:T(1024)} %get-tuple-element.220) | copy-start | bytes 36868
  (16 other events, 18.8 us)
Sparse Core Ops, SparseCore 0:
  10.1 198.0 all-gather.6
  244.0 127.3 all-gather.8
  450.5 117.2 all-reduce.7
  569.2 480.5 all-gather.10
  1051.6 177.3 all-gather.12
  1264.9 117.7 all-reduce.11
  1385.6 68.6 all-reduce.9
  1802.8 118.0 all-reduce.13
  1924.8 449.3 reduce-scatter.4
  2377.9 785.5 reduce-scatter.8
  3167.6 161.2 reduce-scatter.6
  3333.2 402.2 reduce-scatter.10
where the time goes:
time: 3750 us; the launch traced here: 3740 us
  waiting for transfers between devices  3060 us (82%)
  matrix products  287 us (8%)
  blocking collectives  122 us (3%)
  local copies, waits for them, and re-layouts  119 us (3%)
  other arithmetic  114 us (3%)
    reduce_scatter x1, waiting for transfers between devices, shards(): lax.psum_scatter(grad_gu_part, ('fsdp', 'ctx'), scatter_dimension=1, tile...  784 us
    all_gather x1, waiting for transfers between devices, shards(): lax.all_gather(w_gate_up, ('fsdp', 'ctx'), axis=1, tiled=True)  475 us
    reduce_scatter x1, waiting for transfers between devices, shards(): lax.psum_scatter(grad_down_part, ('fsdp', 'ctx'), scatter_dimension=1, ti...  407 us
    reduce_scatter x1, waiting for transfers between devices, shards(): lax.psum_scatter(grad_qkv_part, ('fsdp', 'ctx'), scatter_dimension=1, til...  401 us
    reduce_scatter x1, waiting for transfers between devices, shards(): lax.psum_scatter(grad_out_part, ('fsdp', 'ctx'), scatter_dimension=1, til...  159 us
    all_gather x1, waiting for transfers between devices, shards(): lax.all_gather(w_qkv, ('fsdp', 'ctx'), axis=1, tiled=True)  158 us
    all_gather x1, waiting for transfers between devices, shards(): lax.all_gather(w_down, ('fsdp', 'ctx'), axis=1, tiled=True)  157 us
    all_to_all x1, waiting for transfers between devices, shards(): lax.all_to_all(jnp.stack([query_rows, keys_rows, values_rows]), 'ctx', sp...  106 us
  transfers between devices with their start and end apart: 15, of which 14 were waited for; matrix products, arithmetic and copies ran while one was open for 6% of the time, Pallas kernels for 0%

commit v1 on v0

v1 whole, which is shorter than its diff:
```python
import functools
import math

import jax
import jax.numpy as jnp
from jax import lax
from jax.experimental import pallas as pl
from jax.experimental.pallas import tpu as pltpu
from jax.sharding import PartitionSpec as P

HD = 96
HALF = HD // 2
LANES = 128
EPSILON = 1e-05
MASK_FILL = -1e30
ROPE_BASE = 10000.0
GROUP = ("ctx", "tp")
BLK = 256
MESH = pl.DeviceIdType.MESH
SUBS = 2
VLIM = 64 * 1024 * 1024 - 65536


def near_order(c, j, size):
    low = c < size // 2
    base = jnp.where(low, c, size - 1 - c)
    zig = jnp.where(j % 2 == 1, base - (j + 1) // 2, base + j // 2)
    place = jnp.where(j <= 2 * base, zig, j)
    return jnp.where(low, place, size - 1 - place)


def places():
    c, t = lax.axis_index("ctx"), lax.axis_index("tp")
    return c, t // 2, t % 2


def greet(c, y, k, size):
    barrier = pltpu.get_barrier_semaphore()

    @pl.when(c < size - 1)
    def _():
        pl.semaphore_signal(barrier, inc=1, device_id={"ctx": c + 1}, device_id_type=MESH)

    @pl.when(c > 0)
    def _():
        pl.semaphore_signal(barrier, inc=1, device_id={"ctx": c - 1}, device_id_type=MESH)

    pl.semaphore_signal(barrier, inc=1, device_id={"tp": (1 - y) * 2 + k}, device_id_type=MESH)
    pl.semaphore_signal(barrier, inc=1, device_id={"tp": y * 2 + 1 - k}, device_id_type=MESH)
    pl.semaphore_wait(barrier, jnp.where((c > 0) & (c < size - 1), 4, 3))


def gather_kernel(size, part, n_in, n_out, compute, *refs):
    x_ref = refs[0]
    hbm_ins = refs[1 : 1 + n_in]
    full_ref = refs[1 + n_in]
    outs = refs[2 + n_in : 2 + n_in + n_out]
    ins = refs[2 + n_in + n_out : 2 + 2 * n_in + n_out]
    buf, recv, zs, ys, ks, local, load, in_sems = refs[2 + 2 * n_in + n_out :]
    c, y, k = places()
    sub = part // SUBS

    def slot(cc, yy, kk, s):
        return buf.at[cc * 2 + yy, pl.ds(pl.multiple_of(kk * part + s * sub, sub), sub)]

    def copy(cc, yy, kk, s, sem, dev):
        return pltpu.make_async_remote_copy(
            src_ref=slot(cc, yy, kk, s),
            dst_ref=slot(cc, yy, kk, s),
            send_sem=sem,
            recv_sem=recv.at[cc * 2 + yy, kk, s],
            device_id=dev,
            device_id_type=MESH,
        )

    up, down = {"ctx": c + 1}, {"ctx": c - 1}
    ydev, kdev = {"tp": (1 - y) * 2 + k}, {"tp": y * 2 + 1 - k}

    def z_up(cc, s):
        return copy(cc, y, k, s, zs.at[0, cc, s], up)

    def z_down(cc, s):
        return copy(cc, y, k, s, zs.at[1, cc, s], down)

    def y_send(cc, s):
        return copy(cc, y, k, s, ys.at[cc, s], ydev)

    def k_send(cc, yy, s):
        return copy(cc, yy, k, s, ks.at[cc * 2 + yy, s], kdev)

    def pair_out(cc, yy):
        pair = cc * 2 + yy
        return pltpu.make_async_copy(
            buf.at[pair],
            full_ref.at[pl.ds(pl.multiple_of(pair * 2 * part, 2 * part), 2 * part)],
            local.at[pair],
        )

    def got(cc, yy, kk, s):
        copy(cc, yy, kk, s, ys.at[0, 0], ydev).wait_recv()

    mine = buf.at[c * 2 + y, pl.ds(pl.multiple_of(k * part, part), part)]
    first = pltpu.make_async_copy(x_ref, mine, load)
    first.start()
    for i in range(n_in):
        pltpu.make_async_copy(hbm_ins[i], ins[i], in_sems.at[i]).start()
    greet(c, y, k, size)
    first.wait()

    def z_stage(cc, s):
        @pl.when((cc <= c) & (c < size - 1))
        def _():
            z_up(cc, s).start()

        @pl.when((cc >= c) & (c > 0))
        def _():
            z_down(cc, s).start()

        y_send(cc, s).start()
        k_send(cc, y, s).start()

    for s in range(SUBS):
        z_stage(c, s)
    for i in range(n_in):
        pltpu.make_async_copy(hbm_ins[i], ins[i], in_sems.at[i]).wait()

    def finish(cc, yy):
        for s in range(SUBS):
            got(cc, yy, 1 - k, s)
        pair_out(cc, yy).start()
        compute(cc * 2 + yy, buf, ins, outs)

    def step(r, carry):
        for s in range(SUBS):
            for sign in (-1, 1):
                nxt = c + sign * (r + 1)

                @pl.when((nxt >= 0) & (nxt < size))
                def _():
                    got(nxt, y, k, s)
                    z_stage(nxt, s)

            for sign in (-1, 1):
                cc = c + sign * r

                @pl.when((cc >= 0) & (cc < size) & ((r > 0) | (sign > 0)))
                def _():
                    if s == SUBS - 1:
                        finish(cc, y)
                    got(cc, 1 - y, k, s)
                    k_send(cc, 1 - y, s).start()
                    if s == SUBS - 1:
                        finish(cc, 1 - y)

        return carry

    lax.fori_loop(0, size, step, 0)

    def drain(cc, carry):
        for s in range(SUBS):
            @pl.when((cc <= c) & (c < size - 1))
            def _():
                z_up(cc, s).wait_send()

            @pl.when((cc >= c) & (c > 0))
            def _():
                z_down(cc, s).wait_send()

            y_send(cc, s).wait_send()
            for yy in range(2):
                k_send(cc, yy, s).wait_send()
        for yy in range(2):
            pair_out(cc, yy).wait()
        return carry

    lax.fori_loop(0, size, drain, 0)


def gather_call(x, ins, out_shapes, compute, name, cid, size):
    part, width = x.shape
    any_spec = pl.BlockSpec(memory_space=pl.ANY)
    vmem = pl.BlockSpec(memory_space=pltpu.VMEM)
    full = jax.ShapeDtypeStruct((size * 4 * part, width), x.dtype)
    return pl.pallas_call(
        functools.partial(gather_kernel, size, part, len(ins), len(out_shapes), compute),
        out_shape=(full, *out_shapes),
        in_specs=[any_spec] * (1 + len(ins)),
        out_specs=(any_spec, *([vmem] * len(out_shapes))),
        scratch_shapes=[
            *(pltpu.VMEM(one.shape, one.dtype) for one in ins),
            pltpu.VMEM((size * 2, 2 * part, width), x.dtype),
            pltpu.SemaphoreType.DMA((size * 2, 2, SUBS)),
            pltpu.SemaphoreType.DMA((2, size, SUBS)),
            pltpu.SemaphoreType.DMA((size, SUBS)),
            pltpu.SemaphoreType.DMA((size * 2, SUBS)),
            pltpu.SemaphoreType.DMA((size * 2,)),
            pltpu.SemaphoreType.DMA,
            pltpu.SemaphoreType.DMA((max(len(ins), 1),)),
        ],
        compiler_params=pltpu.CompilerParams(
            collective_id=cid, has_side_effects=True, vmem_limit_bytes=VLIM
        ),
        name=name,
    )(x, *ins)


def reduce_kernel(size, part, n_in, n_out, final, *refs):
    a_ref, w_ref = refs[:2]
    ins = refs[2 : 2 + n_in]
    outs = refs[2 + n_in : 2 + n_in + n_out]
    (
        own,
        ksend,
        krecv,
        ysend,
        yrecv,
        qown,
        zsend,
        zrecv,
        total,
        k_sems,
        y_sems,
        z_sems,
    ) = refs[2 + n_in + n_out :]
    c, y, k = places()
    chunk = 16
    tile = 512
    width = total.shape[1]

    sub = part // SUBS

    def remote(src, dst, sems, dev):
        return pltpu.make_async_remote_copy(
            src_ref=src,
            dst_ref=dst,
            send_sem=sems.at[0],
            recv_sem=sems.at[1],
            device_id=dev,
            device_id_type=MESH,
        )

    ydev, kdev = {"tp": (1 - y) * 2 + k}, {"tp": y * 2 + 1 - k}

    def k_copy(cc, yy):
        pair = cc * 2 + yy
        return remote(ksend.at[pair], krecv.at[pair], k_sems.at[pair], kdev)

    def y_copy(cc, s):
        r = pl.ds(s * sub, sub)
        return remote(ysend.at[cc, r], yrecv.at[cc, r], y_sems.at[cc, s], ydev)

    def z_up(cc, s):
        r = pl.ds(s * sub, sub)
        return remote(zsend.at[cc, r], zrecv.at[0, cc, r], z_sems.at[0, cc, s], {"ctx": c + 1})

    def z_down(cc, s):
        r = pl.ds(s * sub, sub)
        return remote(zsend.at[cc, r], zrecv.at[1, cc, r], z_sems.at[1, cc, s], {"ctx": c - 1})

    greet(c, y, k, size)

    def rows(i):
        return pl.ds(pl.multiple_of(i * chunk, chunk), chunk)

    def sweep(body, s=None):
        steps = part // chunk
        lo, hi = (0, steps) if s is None else (s * steps // SUBS, (s + 1) * steps // SUBS)

        def one(i, carry):
            body(rows(i))
            return carry

        lax.fori_loop(lo, hi, one, 0)

    def produce(cc, yy, keep):
        pair = cc * 2 + yy
        mine = pl.ds(pl.multiple_of(pair * 2 * part + k * part, part), part)
        other = pl.ds(pl.multiple_of(pair * 2 * part + (1 - k) * part, part), part)

        def one(i, carry):
            lanes = pl.ds(pl.multiple_of(i * tile, tile), tile)
            w = w_ref[:, lanes]
            ksend[pair, :, lanes] = jnp.dot(
                a_ref[other, :], w, preferred_element_type=jnp.float32
            ).astype(jnp.bfloat16)
            own[keep, :, lanes] = jnp.dot(a_ref[mine, :], w, preferred_element_type=jnp.float32)
            return carry

        lax.fori_loop(0, width // tile, one, 0)
        k_copy(cc, yy).start()

    def first(j, carry):
        cc = near_order(c, size - 1 - j, size)
        produce(cc, 1 - y, 0)
        produce(cc, y, 1)
        k_copy(cc, 1 - y).wait_recv()

        def add_y(r):
            got = krecv[cc * 2 + 1 - y, r, :].astype(jnp.float32)
            ysend[cc, r, :] = (own[0, r, :] + got).astype(jnp.bfloat16)

        for s in range(SUBS):
            sweep(add_y, s)
            y_copy(cc, s).start()
        k_copy(cc, y).wait_recv()

        def add_k(r):
            qown[cc, r, :] = own[1, r, :] + krecv[cc * 2 + y, r, :].astype(jnp.float32)

        sweep(add_k)
        return carry

    lax.fori_loop(0, size, first, 0)

    def pass_on(cc, s, into, edge, send):
        @pl.when(jnp.logical_not(edge))
        def _():
            send(cc, s).wait_recv()

            def add(r):
                part_sum = qown[cc, r, :] + yrecv[cc, r, :].astype(jnp.float32)
                zsend[cc, r, :] = (part_sum + zrecv[into, cc, r, :].astype(jnp.float32)).astype(
                    jnp.bfloat16
                )

            sweep(add, s)

        @pl.when(edge)
        def _():
            def add(r):
                part_sum = qown[cc, r, :] + yrecv[cc, r, :].astype(jnp.float32)
                zsend[cc, r, :] = part_sum.astype(jnp.bfloat16)

            sweep(add, s)

        send(cc, s).start()

    def second(j, carry):
        cc = near_order(c, size - 1 - j, size)
        for s in range(SUBS):
            y_copy(cc, s).wait_recv()

            @pl.when(cc > c)
            def _():
                pass_on(cc, s, 0, c == 0, z_up)

            @pl.when(cc < c)
            def _():
                pass_on(cc, s, 1, c == size - 1, z_down)

        return carry

    lax.fori_loop(0, size, second, 0)

    def add_own(r):
        total[r, :] = qown[c, r, :] + yrecv[c, r, :].astype(jnp.float32)

    sweep(add_own)

    @pl.when(c > 0)
    def _():
        for s in range(SUBS):
            z_up(c, s).wait_recv()

        def add(r):
            total[r, :] += zrecv[0, c, r, :].astype(jnp.float32)

        sweep(add)

    @pl.when(c < size - 1)
    def _():
        for s in range(SUBS):
            z_down(c, s).wait_recv()

        def add(r):
            total[r, :] += zrecv[1, c, r, :].astype(jnp.float32)

        sweep(add)

    final(total, sweep, ins, outs)

    def drain(cc, carry):
        for yy in range(2):
            k_copy(cc, yy).wait_send()
        for s in range(SUBS):
            y_copy(cc, s).wait_send()

            @pl.when(cc > c)
            def _():
                z_up(cc, s).wait_send()

            @pl.when(cc < c)
            def _():
                z_down(cc, s).wait_send()

        return carry

    lax.fori_loop(0, size, drain, 0)


def reduce_call(a, w, ins, out_shapes, final, name, cid, size):
    width = w.shape[1]
    part = a.shape[0] // (size * 4)
    vmem = pl.BlockSpec(memory_space=pltpu.VMEM)
    low, full = jnp.bfloat16, jnp.float32
    return pl.pallas_call(
        functools.partial(reduce_kernel, size, part, len(ins), len(out_shapes), final),
        out_shape=tuple(out_shapes),
        in_specs=[vmem] * (2 + len(ins)),
        out_specs=tuple([vmem] * len(out_shapes)),
        scratch_shapes=[
            pltpu.VMEM((2, part, width), full),
            pltpu.VMEM((size * 2, part, width), low),
            pltpu.VMEM((size * 2, part, width), low),
            pltpu.VMEM((size, part, width), low),
            pltpu.VMEM((size, part, width), low),
            pltpu.VMEM((size, part, width), full),
            pltpu.VMEM((size, part, width), low),
            pltpu.VMEM((2, size, part, width), low),
            pltpu.VMEM((part, width), full),
            pltpu.SemaphoreType.DMA((size * 2, 2)),
            pltpu.SemaphoreType.DMA((size, SUBS, 2)),
            pltpu.SemaphoreType.DMA((2, size, SUBS, 2)),
        ],
        compiler_params=pltpu.CompilerParams(
            collective_id=cid, has_side_effects=True, vmem_limit_bytes=VLIM
        ),
        name=name,
    )(a, w, *ins)


def doc_positions(segment_row):
    places_in = jnp.arange(segment_row.shape[0], dtype=jnp.int32)
    starts = jnp.concatenate([jnp.ones((1,), dtype=jnp.bool_), segment_row[1:] != segment_row[:-1]])
    first = lax.cummax(jnp.where(starts, places_in, jnp.zeros_like(places_in)), axis=0)
    return places_in - first


def rope_tables(positions):
    freqs = ROPE_BASE ** (-(jnp.arange(HALF, dtype=jnp.float32) * 2.0 / HD))
    angles = positions.astype(jnp.float32)[:, None] * freqs
    gap = jnp.zeros((positions.shape[0], LANES // 2 - HALF), jnp.float32)
    cosine, sine = jnp.cos(angles), jnp.sin(angles)
    return (
        jnp.concatenate([cosine, gap, cosine, gap], axis=1),
        jnp.concatenate([-sine, gap, sine, gap], axis=1),
    )


def spread(array, axis):
    shape = array.shape
    halves = array.reshape(*shape[:axis], shape[axis] // HALF, HALF, *shape[axis + 1 :])
    pads = [(0, 0)] * halves.ndim
    pads[axis + 1] = (0, LANES // 2 - HALF)
    wide = jnp.pad(halves, pads)
    return wide.reshape(*shape[:axis], -1, *shape[axis + 1 :])


def unspread(array, axis):
    shape = array.shape
    half = LANES // 2
    halves = array.reshape(*shape[:axis], shape[axis] // half, half, *shape[axis + 1 :])
    kept = lax.slice_in_dim(halves, 0, HALF, axis=axis + 1)
    return kept.reshape(*shape[:axis], -1, *shape[axis + 1 :])


def nt(left, right):
    return lax.dot_general(left, right, (((1,), (1,)), ((), ())), preferred_element_type=jnp.float32)


def nn(left, right):
    return jnp.dot(left, right, preferred_element_type=jnp.float32)


def tn(left, right):
    return lax.dot_general(left, right, (((0,), (0,)), ((), ())), preferred_element_type=jnp.float32)


def qkv_kernel(heads, x_ref, w_ref, cos_ref, sin_ref, out_ref):
    proj = nt(x_ref[...], w_ref[...])
    for i in range(3 * heads):
        cut = slice(i * LANES, (i + 1) * LANES)
        one = proj[:, cut]
        if i < 2 * heads:
            one = one * cos_ref[...] + pltpu.roll(one, LANES // 2, 1) * sin_ref[...]
        out_ref[:, cut] = one.astype(jnp.bfloat16)


def qkv_call(x, w, cosine, sine, heads):
    rows, width = x.shape
    return pl.pallas_call(
        functools.partial(qkv_kernel, heads),
        out_shape=jax.ShapeDtypeStruct((rows, w.shape[0]), jnp.bfloat16),
        grid=(rows // BLK,),
        in_specs=[
            pl.BlockSpec((BLK, width), lambda i: (i, 0)),
            pl.BlockSpec(w.shape, lambda i: (0, 0)),
            pl.BlockSpec((BLK, LANES), lambda i: (i, 0)),
            pl.BlockSpec((BLK, LANES), lambda i: (i, 0)),
        ],
        out_specs=pl.BlockSpec((BLK, w.shape[0]), lambda i: (i, 0)),
        compiler_params=pltpu.CompilerParams(vmem_limit_bytes=VLIM),
        name="qkv",
    )(x, w, cosine, sine)


def block(ref, i, head):
    return ref[pl.ds(pl.multiple_of(i * BLK, BLK), BLK), head * LANES : (head + 1) * LANES]


def masked_scores(keys, query, seg_col, seg_row, kb, qb, scale):
    scores = nt(keys, query) * scale
    key_pos = kb * BLK + lax.broadcasted_iota(jnp.int32, scores.shape, 0)
    query_pos = qb * BLK + lax.broadcasted_iota(jnp.int32, scores.shape, 1)
    return jnp.where((key_pos <= query_pos) & (seg_col == seg_row), scores, MASK_FILL)


def attend_kernel(heads, scale, low_ref, qkv_ref, col_ref, row_ref, out_ref, lse_ref):
    blocks = qkv_ref.shape[0] // BLK

    def one(i, carry):
        cut = pl.ds(pl.multiple_of(i * BLK, BLK), BLK)
        seg_row = row_ref[:, cut]
        for h in range(heads):
            query = block(qkv_ref, i, h)

            def inner(kb, state):
                peak, total, acc = state
                keys = block(qkv_ref, kb, heads + h)
                seg_col = col_ref[pl.ds(pl.multiple_of(kb * BLK, BLK), BLK), :]
                scores = masked_scores(keys, query, seg_col, seg_row, kb, i, scale)
                new = jnp.maximum(peak, jnp.max(scores, axis=0, keepdims=True))
                fade = jnp.exp(peak - new)
                expo = jnp.exp(scores - new)
                total = total * fade + jnp.sum(expo, axis=0, keepdims=True)
                mixed = tn(block(qkv_ref, kb, 2 * heads + h), expo.astype(jnp.bfloat16))
                return new, total, acc * fade + mixed

            peak, total, acc = lax.fori_loop(
                low_ref[i],
                i + 1,
                inner,
                (
                    jnp.full((1, BLK), MASK_FILL, jnp.float32),
                    jnp.zeros((1, BLK), jnp.float32),
                    jnp.zeros((LANES, BLK), jnp.float32),
                ),
            )
            out_ref[cut, h * LANES : (h + 1) * LANES] = (acc / total).T.astype(jnp.bfloat16)
            lse_ref[h : h + 1, cut] = peak + jnp.log(total)
        return carry

    lax.fori_loop(0, blocks, one, 0)


def attend_call(qkv, seg, low, heads, scale):
    rows = qkv.shape[0]
    vmem = pl.BlockSpec(memory_space=pltpu.VMEM)
    return pl.pallas_call(
        functools.partial(attend_kernel, heads, scale),
        out_shape=(
            jax.ShapeDtypeStruct((rows, heads * LANES), jnp.bfloat16),
            jax.ShapeDtypeStruct((heads, rows), jnp.float32),
        ),
        in_specs=[pl.BlockSpec(memory_space=pltpu.SMEM), vmem, vmem, vmem],
        out_specs=(vmem, vmem),
        compiler_params=pltpu.CompilerParams(vmem_limit_bytes=VLIM),
        name="attend",
    )(low, qkv, seg[:, None], seg[None, :])


def attend_back_kernel(
    heads,
    scale,
    high_ref,
    qkv_ref,
    out_ref,
    grad_ref,
    lse_ref,
    col_ref,
    row_ref,
    cos_ref,
    sin_ref,
    res_ref,
    delta_ref,
    gq_ref,
):
    blocks = qkv_ref.shape[0] // BLK
    gq_ref[...] = jnp.zeros_like(gq_ref)

    def dots(i, carry):
        cut = pl.ds(pl.multiple_of(i * BLK, BLK), BLK)
        for h in range(heads):
            prod = block(out_ref, i, h).astype(jnp.float32) * block(grad_ref, i, h).astype(
                jnp.float32
            )
            delta_ref[h : h + 1, cut] = jnp.sum(prod.T, axis=0, keepdims=True)
        return carry

    lax.fori_loop(0, blocks, dots, 0)

    def turn_back(value, cut):
        low = value.astype(jnp.bfloat16).astype(jnp.float32)
        turned = low * cos_ref[cut, :] - pltpu.roll(low, LANES // 2, 1) * sin_ref[cut, :]
        return turned.astype(jnp.bfloat16)

    def one(kb, carry):
        cut = pl.ds(pl.multiple_of(kb * BLK, BLK), BLK)
        seg_col = col_ref[cut, :]
        for h in range(heads):
            keys = block(qkv_ref, kb, heads + h)
            values = block(qkv_ref, kb, 2 * heads + h)

            def inner(i, state):
                gk, gv = state
                at = pl.ds(pl.multiple_of(i * BLK, BLK), BLK)
                query = block(qkv_ref, i, h)
                grad = block(grad_ref, i, h)
                scores = masked_scores(keys, query, seg_col, row_ref[:, at], kb, i, scale)
                probs = jnp.exp(scores - lse_ref[h : h + 1, at])
                gv = gv + nn(probs.astype(jnp.bfloat16), grad)
                g_probs = nt(values, grad)
                g_scores = (probs * (g_probs - delta_ref[h : h + 1, at])).astype(jnp.bfloat16)
                gk = gk + nn(g_scores, query)
                lanes = slice(h * LANES, (h + 1) * LANES)
                gq_ref[at, lanes] += tn(g_scores, keys)
                return gk, gv

            zero = jnp.zeros((BLK, LANES), jnp.float32)
            gk, gv = lax.fori_loop(kb, high_ref[kb] + 1, inner, (zero, zero))
            at_k = slice((heads + h) * LANES, (heads + h + 1) * LANES)
            at_v = slice((2 * heads + h) * LANES, (2 * heads + h + 1) * LANES)
            res_ref[cut, at_k] = turn_back(gk * scale, cut)
            res_ref[cut, at_v] = gv.astype(jnp.bfloat16)
        return carry

    lax.fori_loop(0, blocks, one, 0)

    def close(i, carry):
        cut = pl.ds(pl.multiple_of(i * BLK, BLK), BLK)
        for h in range(heads):
            lanes = slice(h * LANES, (h + 1) * LANES)
            res_ref[cut, lanes] = turn_back(gq_ref[cut, lanes] * scale, cut)
        return carry

    lax.fori_loop(0, blocks, close, 0)


def attend_back_call(qkv, out, grad, lse, seg, high, cosine, sine, heads, scale):
    rows = qkv.shape[0]
    vmem = pl.BlockSpec(memory_space=pltpu.VMEM)
    return pl.pallas_call(
        functools.partial(attend_back_kernel, heads, scale),
        out_shape=jax.ShapeDtypeStruct(qkv.shape, jnp.bfloat16),
        in_specs=[pl.BlockSpec(memory_space=pltpu.SMEM)] + [vmem] * 8,
        out_specs=vmem,
        scratch_shapes=[
            pltpu.VMEM((heads, rows), jnp.float32),
            pltpu.VMEM((rows, heads * LANES), jnp.float32),
        ],
        compiler_params=pltpu.CompilerParams(vmem_limit_bytes=VLIM),
        name="attend_back",
    )(high, qkv, out, grad, lse, seg[:, None], seg[None, :], cosine, sine)


def cross(weight):
    size, groups = lax.axis_size("ctx"), lax.axis_size("fsdp")
    c, f = lax.axis_index("ctx"), lax.axis_index("fsdp")
    n = weight.shape[1] // size
    pieces = []
    for s in range(size):
        piece = lax.dynamic_slice_in_dim(weight, ((c + s) % size) * n, n, 1)
        if s:
            piece = lax.ppermute(piece, "ctx", [(i, (i + s) % size) for i in range(size)])
        pieces.append((piece, f * size + (c - s) % size))
    for g in range(1, groups):
        for s in range(size):
            piece = lax.ppermute(
                pieces[s][0], "fsdp", [(i, (i + g) % groups) for i in range(groups)]
            )
            pieces.append((piece, ((f - g) % groups) * size + (c - s) % size))
    return pieces


def join_kernel(count, cuts, groups, size, *refs):
    pieces, out, sems = refs[:count], refs[count], refs[count + 1]
    c, f = lax.axis_index("ctx"), lax.axis_index("fsdp")
    m, n, d = pieces[0].shape
    tall = out.shape[0] // m

    def copies(go):
        for i in range(count):
            g, s = i // size, i % size
            place = ((f + groups - g) % groups) * size + (c + size - s) % size
            lanes = pl.ds(pl.multiple_of(place * d, d), d)
            for j in range(m):
                for q, (src, dst, rows) in enumerate(cuts):
                    go(
                        pltpu.make_async_copy(
                            pieces[i].at[j, pl.ds(src, rows)],
                            out.at[pl.ds(j * tall + dst, rows), lanes],
                            sems.at[i, j * len(cuts) + q],
                        )
                    )

    copies(lambda one: one.start())
    for j in range(m):
        for k, (_, dst, rows) in enumerate(cuts):
            stop = cuts[k + 1][1] if k + 1 < len(cuts) else tall
            if dst + rows < stop:
                gap = stop - dst - rows
                out[pl.ds(j * tall + dst + rows, gap), :] = jnp.zeros(
                    (gap, out.shape[1]), out.dtype
                )
    copies(lambda one: one.wait())


def join(pieces, spaced, name):
    m, n, d = pieces[0][0].shape
    width = len(pieces) * d
    if d % LANES:
        buf = jnp.zeros((len(pieces), m, n, d), pieces[0][0].dtype)
        for piece, place in pieces:
            buf = lax.dynamic_update_slice(buf, piece[None], (place, 0, 0, 0))
        flat = buf.transpose(1, 2, 0, 3).reshape(m, n, width)
        flat = spread(flat, 1) if spaced else flat
        return flat.reshape(-1, width)
    cuts = [(0, 0, n)]
    if spaced:
        cuts = [(i * HALF, i * LANES // 2, HALF) for i in range(n // HALF)]
    tall = n * LANES // HD if spaced else n
    return pl.pallas_call(
        functools.partial(
            join_kernel,
            len(pieces),
            cuts,
            lax.axis_size("fsdp"),
            lax.axis_size("ctx"),
        ),
        out_shape=jax.ShapeDtypeStruct((m * tall, width), pieces[0][0].dtype),
        in_specs=[pl.BlockSpec(memory_space=pl.ANY)] * len(pieces),
        out_specs=pl.BlockSpec(memory_space=pltpu.VMEM),
        scratch_shapes=[pltpu.SemaphoreType.DMA((len(pieces), m * len(cuts)))],
        compiler_params=pltpu.CompilerParams(vmem_limit_bytes=VLIM),
        name=name,
    )(*[piece for piece, _ in pieces])


def hand_out(grad):
    size, groups = lax.axis_size("ctx"), lax.axis_size("fsdp")
    c, f = lax.axis_index("ctx"), lax.axis_index("fsdp")
    rows = grad.shape[0] // groups
    d = rows // size
    total = lax.dynamic_slice_in_dim(grad, f * rows, rows, 0)
    for g in range(1, groups):
        sent = lax.dynamic_slice_in_dim(grad, ((f + g) % groups) * rows, rows, 0)
        got = lax.ppermute(
            sent.astype(jnp.bfloat16), "fsdp", [(i, (i + g) % groups) for i in range(groups)]
        )
        total = total.astype(jnp.float32) + got.astype(jnp.float32)
    total = total.astype(jnp.bfloat16)
    out = jnp.zeros((size, d, grad.shape[1]), jnp.bfloat16)
    for s in range(size):
        piece = lax.dynamic_slice_in_dim(total, ((c + s) % size) * d, d, 0)
        if s:
            piece = lax.ppermute(piece, "ctx", [(i, (i + s) % size) for i in range(size)])
        out = lax.dynamic_update_slice(out, piece[None], ((c - s) % size, 0, 0))
    return out.astype(jnp.float32)


def wide_gather(part):
    full = lax.all_gather(part, GROUP, axis=0, tiled=True)
    return full


def mlp_block(half, pair, buf, ins, outs):
    w, g_act = ins
    act, g_gate, g_up = outs
    rows = buf.shape[1]
    tile = 256
    at = pl.ds(pl.multiple_of(pair * rows, rows), rows)

    def one(i, carry):
        lanes = pl.ds(pl.multiple_of(i * tile, tile), tile)
        gate = nt(buf[pair], w[lanes, :])
        up = nt(buf[pair], w[pl.ds(pl.multiple_of(half + i * tile, tile), tile), :])
        grad = g_act[at, lanes]
        sigma = 1.0 / (1.0 + jnp.exp(-gate))
        silu = gate * sigma
        act[at, lanes] = (silu * up).astype(jnp.bfloat16)
        g_up[at, lanes] = (grad * silu).astype(jnp.bfloat16)
        g_gate[at, lanes] = (grad * up * sigma * (1.0 + gate * (1.0 - sigma))).astype(jnp.bfloat16)
        return carry

    lax.fori_loop(0, half // tile, one, 0)


def attn_block(pair, buf, ins, outs):
    rows = buf.shape[1]
    at = pl.ds(pl.multiple_of(pair * rows, rows), rows)
    outs[0][at, :] = nt(buf[pair], ins[0][...]).astype(jnp.bfloat16)


def no_block(pair, buf, ins, outs):
    pass


def after_out(total, sweep, ins, outs):
    tokens, gain = ins
    hidden, normed = outs

    def one(r):
        value = tokens[r, :].astype(jnp.float32) + total[r, :]
        scale = lax.rsqrt(jnp.mean(value * value, axis=1, keepdims=True) + EPSILON)
        hidden[r, :] = value
        normed[r, :] = (value * scale * gain[...]).astype(jnp.bfloat16)

    sweep(one)


def norm_back(grad, value, gain, top):
    scale = lax.rsqrt(jnp.mean(value * value, axis=1, keepdims=True) + EPSILON)
    unit = value * scale
    g_unit = grad * gain
    inner = jnp.mean(g_unit * unit, axis=1, keepdims=True)
    return top + scale * (g_unit - unit * inner), grad * unit


def after_mlp(total, sweep, ins, outs):
    hidden, cot, gain = ins
    g_hidden, g_branch, g_gain = outs
    g_gain[...] = jnp.zeros_like(g_gain)

    def one(r):
        grad, part = norm_back(
            total[r, :], hidden[r, :], gain[...], cot[r, :].astype(jnp.float32)
        )
        g_hidden[r, :] = grad
        g_branch[r, :] = grad.astype(jnp.bfloat16)
        g_gain[...] += part

    sweep(one)


def after_qkv(total, sweep, ins, outs):
    tokens, g_hidden, gain = ins
    g_tokens, g_gain = outs
    g_gain[...] = jnp.zeros_like(g_gain)

    def one(r):
        grad, part = norm_back(
            total[r, :], tokens[r, :].astype(jnp.float32), gain[...], g_hidden[r, :]
        )
        g_tokens[r, :] = grad.astype(jnp.bfloat16)
        g_gain[...] += part

    sweep(one)


def shards(tokens, segments, w_qkv, w_out, w_gate_up, w_down, norm_attn, norm_mlp, cotangent):
    seqs, rows, width = tokens.shape
    size, tp_size = lax.axis_size("ctx"), lax.axis_size("tp")
    length = segments.shape[1]
    assert seqs == 1 and tp_size == 4
    part = rows // tp_size
    begin = lax.axis_index("tp") * part
    scale = 1.0 / math.sqrt(HD)
    low, full = jnp.bfloat16, jnp.float32
    heads = w_qkv.shape[2] // HD // size
    seg = segments[0]

    tokens_own = lax.dynamic_slice_in_dim(tokens[0], begin, part, 0)
    cot_own = lax.dynamic_slice_in_dim(cotangent[0], begin, part, 0)

    pieces_q = cross(w_qkv.transpose(0, 2, 1))
    gains = lax.all_gather(
        jnp.stack([norm_attn, norm_mlp]), ("fsdp", "ctx"), axis=1, tiled=True
    ).astype(full)
    gain_attn, gain_mlp = gains[0:1], gains[1:2]
    resid = tokens_own.astype(full)
    scale_one = lax.rsqrt(jnp.mean(resid * resid, axis=1, keepdims=True) + EPSILON)
    normed1_own = (resid * scale_one * gain_attn).astype(low)

    w_out, w_gate_up, w_down, cot_gate, _ = lax.optimization_barrier(
        (w_out, w_gate_up, w_down, cot_own, [p for p, _ in pieces_q[:size]])
    )
    wq = join(pieces_q, True, "join_qkv")
    wo = join(cross(w_out[None]), True, "join_out")
    wd = join(cross(w_down[None]), False, "join_down")
    wg = join(cross(w_gate_up.transpose(0, 2, 1)), False, "join_gate_up")
    half = wg.shape[0] // 2
    cot_full = wide_gather(cot_gate)

    positions = doc_positions(seg)
    cosine, sine = rope_tables(positions)
    starts = (jnp.arange(length, dtype=jnp.int32) - positions)[::BLK] // BLK
    marks = jnp.arange(length // BLK, dtype=jnp.int32)
    ends = jnp.sum((starts[None, :] <= marks[:, None]).astype(jnp.int32), axis=1) - 1

    normed1 = gather_call(normed1_own, [], [], no_block, "gather_normed1", 1, size)[0]
    qkv = qkv_call(normed1, wq, cosine, sine, heads)
    attn, lse = attend_call(qkv, seg, starts, heads, scale)

    row_shape = jax.ShapeDtypeStruct((part, width), full)
    row_low = jax.ShapeDtypeStruct((part, width), low)
    gain_shape = jax.ShapeDtypeStruct((16, width), full)
    hidden1, normed2_own = reduce_call(
        attn, wo, [tokens_own, gain_mlp], [row_shape, row_low], after_out, "reduce_out", 2, size
    )
    g_act = nt(cot_full, wd)
    half_shape = jax.ShapeDtypeStruct((length, half), low)
    normed2, act, g_gate, g_up = gather_call(
        normed2_own,
        [wg, g_act],
        [half_shape] * 3,
        functools.partial(mlp_block, half),
        "gather_mlp",
        3,
        size,
    )
    g_gu = jnp.concatenate([g_gate, g_up], axis=1)
    part_down, part_gu = tn(cot_full, act).astype(low), tn(normed2, g_gu).astype(low)
    g_gu, part_down, part_gu = lax.optimization_barrier((g_gu, part_down, part_gu))
    g_hidden1, g_branch_own, g_gain_mlp = reduce_call(
        g_gu,
        wg,
        [hidden1, cot_own, gain_mlp],
        [row_shape, row_low, gain_shape],
        after_mlp,
        "reduce_mlp",
        4,
        size,
    )
    down = lax.psum_scatter(nn(act, wd).astype(low), GROUP, scatter_dimension=0, tiled=True)
    output = (hidden1 + down.astype(full)).astype(low)
    output = lax.all_gather(output, "tp", axis=0, tiled=True)[None]

    g_branch, g_attn = gather_call(
        g_branch_own,
        [wo],
        [jax.ShapeDtypeStruct((length, heads * LANES), low)],
        attn_block,
        "gather_branch",
        5,
        size,
    )
    out_down = hand_out(part_down)
    out_gu = hand_out(part_gu)
    part_out = unspread(tn(g_branch, attn), 1).astype(low)
    g_attn, part_out = lax.optimization_barrier((g_attn, part_out))
    g_proj = attend_back_call(qkv, attn, g_attn, lse, seg, ends, cosine, sine, heads, scale)
    out_out = hand_out(part_out)
    part_qkv = unspread(tn(normed1, g_proj), 1).astype(low)
    g_proj, part_qkv = lax.optimization_barrier((g_proj, part_qkv))
    out_qkv = hand_out(part_qkv)
    g_tokens, g_gain_attn = reduce_call(
        g_proj,
        wq,
        [tokens_own, g_hidden1, gain_attn],
        [row_low, gain_shape],
        after_qkv,
        "reduce_qkv",
        6,
        size,
    )
    g_tokens = lax.all_gather(g_tokens, "tp", axis=0, tiled=True)[None]

    d = w_qkv.shape[1]
    grad_qkv = out_qkv.reshape(size, d, 3, -1).transpose(2, 1, 0, 3).reshape(3, d, -1)
    grad_gu = out_gu.reshape(size, d, 2, -1).transpose(2, 1, 0, 3).reshape(2, d, -1)
    grad_out = out_out.transpose(0, 2, 1).reshape(-1, d)
    grad_down = out_down.transpose(0, 2, 1).reshape(-1, d)

    gain_sums = lax.psum(
        jnp.stack([jnp.sum(g_gain_attn, axis=0), jnp.sum(g_gain_mlp, axis=0)]),
        ("fsdp", "ctx", "tp"),
    )
    mine = lax.axis_index("fsdp") * size + lax.axis_index("ctx")
    gain_grads = lax.dynamic_slice_in_dim(gain_sums, mine * d, d, 1)
    return (
        output,
        g_tokens,
        grad_qkv,
        grad_out,
        grad_gu,
        grad_down,
        gain_grads[0],
        gain_grads[1],
    )


def solution(mesh):
    in_specs = (
        P("fsdp", "ctx", None),
        P("fsdp", None),
        P(None, ("fsdp", "ctx"), "tp"),
        P("tp", ("fsdp", "ctx")),
        P(None, ("fsdp", "ctx"), "tp"),
        P("tp", ("fsdp", "ctx")),
        P(("fsdp", "ctx")),
        P(("fsdp", "ctx")),
        P("fsdp", "ctx", None),
    )
    out_specs = (
        P("fsdp", "ctx", None),
        P("fsdp", "ctx", None),
        P(None, ("fsdp", "ctx"), "tp"),
        P("tp", ("fsdp", "ctx")),
        P(None, ("fsdp", "ctx"), "tp"),
        P("tp", ("fsdp", "ctx")),
        P(("fsdp", "ctx")),
        P(("fsdp", "ctx")),
    )
    return jax.shard_map(shards, mesh=mesh, in_specs=in_specs, out_specs=out_specs, check_vma=False)
```

time: 3750 us -> 1380 us (0.37)
  waiting for transfers between devices: 3060 us -> 175 us
  Pallas kernels: 0 us -> 669 us
  matrix products: 287 us -> 74.6 us
  starting transfers between devices: 14.7 us -> 131 us
  other arithmetic: 114 us -> 30.5 us
  blocking collectives: 122 us -> 174 us
    reduce_scatter x4 -> x1, waiting for transfers between devices: 1750 us -> 0.01 us  [shards(): lax.psum_scatter(nn(act, wd).astype(low), GROUP, scatter_dimension=0, til...]
    all_gather x4 -> x3, waiting for transfers between devices: 791 us -> 0.02 us  [the longest x1 0.02 us: wide_gather(): full = lax.all_gather(part, GROUP, axis=0, tiled=True)]
    pallas_call x0 -> x13, Pallas kernels: none -> 669 us  [the longest x3 303 us: reduce_call(): pl.pallas_call(functools.partial(reduce_kernel, size, part, len(ins), len...]
    psum x4 -> x0, waiting for transfers between devices: 296 us -> none  [the longest x1 103 us: shards(): lax.psum(jnp.einsum('crf,cdf->rd', grad_gu, gu_full, preferred_element_ty...]
    all_to_all x3 -> x0, waiting for transfers between devices: 217 us -> none  [the longest x1 106 us: shards(): lax.all_to_all(jnp.stack([query_rows, keys_rows, values_rows]), 'ctx', sp...]
    dot_general x40 -> x6, matrix products: 287 us -> 74.6 us  [the longest x4 50.8 us: tn(): lax.dot_general(left, right, (((0,), (0,)), ((), ())), preferred_element_...]
    ppermute x0 -> x44, waiting for transfers between devices: none -> 175 us  [the longest x12 59.5 us: hand_out(): lax.ppermute(piece, 'ctx', [(i, (i + s) % size) for i in range(size)])]
    psum x0 -> x1, blocking collectives: none -> 140 us  [shards(): lax.psum(jnp.stack([jnp.sum(g_gain_attn, axis=0), jnp.sum(g_gain_mlp, axi...]
  transfers between devices with their start and end apart: 15 -> 48, of which waited for: 14 -> 16; matrix products, arithmetic and copies ran while one was open for 6% -> 11% of each run, Pallas kernels for 0% -> 43%
where the time goes in v1:
time: 1380 us; the launch traced here: 1360 us
  Pallas kernels  669 us (48%)
  waiting for transfers between devices  175 us (13%)
  blocking collectives  174 us (13%)
  starting transfers between devices  131 us (9%)
  local copies, waits for them, and re-layouts  87.6 us (6%)
  matrix products  74.6 us (5%)
  other arithmetic  30.5 us (2%)
  between operations  14.8 us (1%)
    pallas_call x3, Pallas kernels, reduce_call(): pl.pallas_call(functools.partial(reduce_kernel, size, part, len(ins), len...  303 us
    pallas_call x3, Pallas kernels, gather_call(): pl.pallas_call(functools.partial(gather_kernel, size, part, len(ins), len...  272 us
    psum x1, blocking collectives, shards(): lax.psum(jnp.stack([jnp.sum(g_gain_attn, axis=0), jnp.sum(g_gain_mlp, axi...  140 us
    ppermute x12, starting transfers between devices, cross(): lax.ppermute(piece, 'ctx', [(i, (i + s) % size) for i in range(size)])  64.1 us
    ppermute x12, waiting for transfers between devices, hand_out(): lax.ppermute(piece, 'ctx', [(i, (i + s) % size) for i in range(size)])  59.5 us
    dot_general x4, matrix products, tn(): lax.dot_general(left, right, (((0,), (0,)), ((), ())), preferred_element_...  50.8 us
    ppermute x16, waiting for transfers between devices, cross(): lax.ppermute(pieces[s][0], 'fsdp', [(i, (i + g) % groups) for i in range(...  44.8 us
    ppermute x12, starting transfers between devices, hand_out(): lax.ppermute(piece, 'ctx', [(i, (i + s) % size) for i in range(size)])  42.8 us
  transfers between devices with their start and end apart: 48, of which 16 were waited for; matrix products, arithmetic and copies ran while one was open for 11% of the time, Pallas kernels for 43%

profile of v1, /device:TPU:0, one launch (start us, length us, event | category | flops | bytes accessed | tf_op | source)
XLA Modules:
  0.0 1355.7 jit_solution(12659601921627662371)
XLA Ops:
  7.3 3.2 constant_dynamic-slice_fusion.17
  11.5 3.0 collective-permute-start
  15.6 2.6 collective-permute-start.1
  20.8 2.2 dynamic-slice_bitcast_fusion.5.refs_3_
  23.0 5.1 collective-permute-done.refs_1_
  28.1 18.1 %collective-permute-done.1.refs_2_ = bf16[3,192,384]{2,1,0:T(8,128)(2,1)} collective-permute-done((bf16[3,192,384]{2,1,0:T(8,128)(2,1)}, bf16[3,192,384]{2,1,0:T(8,128)(2,1)}, u32[]{:S(2)}, u32[]{:S(2)}) %collective-permute-start.1) | collective-permute-done | bytes 442400 | tf_op jit(solution)/shard_map/ppermute | solution.py:674
  47.9 33.9 %all_gather.12 = bf16[2,3072]{1,0:T(2,128)(2,1)S(1)} all-gather(bf16[2,384]{1,0:T(2,128)(2,1)S(1)} %pad_maximum_fusion.5), channel_id=1, replica_groups=mesh['fsdp'=2,'ctx'=4,'tp'=4] {'fsdp','ctx'}, dimensions={1}, use_global_device_ids=true | all-gather | bytes 13824 | tf_op jit(solution)/shard_map/all_gather | solution.py:876
  91.2 3.0 collective-permute-done.7.refs_1_
  96.6 5.0 collective-permute-start.21
  101.7 3.5 collective-permute-done.8.refs_2_
  105.1 2.8 collective-permute-start.23
  110.2 3.4 copy.69
  113.7 6.4 collective-permute-done.12.refs_6_
  125.5 16.6 %collective-permute-start.14 = (bf16[2,512,384]{2,1,0:T(8,128)(2,1)}, bf16[2,512,384]{2,1,0:T(8,128)(2,1)}, u32[]{:S(2)}, u32[]{:S(2)}) collective-permute-start(bf16[2,512,384]{2,1,0:T(8,128)(2,1)} %get-tuple-element.94), channel_id=1, source_target_pairs={{0,4},{4,8},{8,12},{12,0},{1,5},{5,9},{9,13},{13,1},{2,6},{6,10},{... | collective-permute-start | bytes 2359304 | tf_op jit(solution)/shard_map/ppermute | solution.py:674
  142.1 5.3 collective-permute-start.15
  147.4 23.0 %collective-permute-start.16 = (bf16[2,512,384]{2,1,0:T(8,128)(2,1)}, bf16[2,512,384]{2,1,0:T(8,128)(2,1)}, u32[]{:S(2)}, u32[]{:S(2)}) collective-permute-start(bf16[2,512,384]{2,1,0:T(8,128)(2,1)} %get-tuple-element.92), channel_id=1, source_target_pairs={{0,12},{4,0},{8,4},{12,8},{1,13},{5,1},{9,5},{13,9},{2,14},{6,2},{... | collective-permute-start | bytes 2359304 | tf_op jit(solution)/shard_map/ppermute | solution.py:674
  174.8 9.0 collective-permute-done.4.refs_5_
  185.1 8.2 collective-permute-done.5.refs_6_
  195.2 116.7 %gather_normed1.1.x_ref = bf16[2048,3072]{1,0:T(8,128)(2,1)} custom-call(bf16[128,3072]{1,0:T(8,128)(2,1)} %fusion.2.refs_0_), custom_call_target="tpu_custom_call" | custom-call | tf_op jit(solution)/shard_map/gather_normed1/pallas_call | solution.py:184
  320.3 3.7 fusion.5
  324.1 19.3 %collective-permute-done.26.refs_6_ = bf16[1,512,384]{2,1,0:T(8,128)(2,1)S(1)} collective-permute-done((bf16[1,512,384]{2,1,0:T(8,128)(2,1)}, bf16[1,512,384]{2,1,0:T(8,128)(2,1)S(1)}, u32[]{:S(2)}, u32[]{:S(2)}) %collective-permute-start.26) | collective-permute-done | bytes 393248 | tf_op jit(solution)/shard_map/ppermute | solution.py:678
  345.3 2.5 pad_maximum_fusion
  347.7 2.6 join_out.1.refs_1_
  350.4 5.0 join_qkv.1.w_ref.refs_1_
  355.4 16.1 %qkv.1.qkv_ref = bf16[2048,768]{1,0:T(8,128)(2,1)} custom-call(bf16[2048,3072]{1,0:T(8,128)(2,1)} %gather_normed1.1.x_ref, bf16[768,3072]{1,0:T(8,128)(2,1)} %join_qkv.1.w_ref.refs_1_, f32[2048,128]{1,0:T(8,128)} %get-tuple-element.111.cos_ref, f32[2048,128]{1,0:T(8,128)} %get-tuple-element.110.sin_ref), custom_call_target="tpu_custom_call" | custom-call | tf_op jit(solution)/shard_map/qkv/pallas_call | solution.py:491
  371.4 23.4 %attend.1 = (bf16[2048,256]{1,0:T(8,128)(2,1)}, f32[2,2048]{1,0:T(2,128)}) custom-call(s32[8]{0:T(128)} %and_select_fusion.low_ref, bf16[2048,768]{1,0:T(8,128)(2,1)} %qkv.1.qkv_ref, s32[2048,1]{1,0:T(8,128)} %copy.68.col_ref, s32[1,2048]{1,0:T(1,128)} %row_ref.3), custom_call_target="tpu_custom_call" | custom-call | tf_op jit(solution)/shard_map/attend/pallas_call | solution.py:559
  394.9 81.3 %reduce_out.1 = (f32[128,3072]{1,0:T(8,128)}, bf16[128,3072]{1,0:T(8,128)(2,1)}) custom-call(bf16[2048,256]{1,0:T(8,128)(2,1)} %get-tuple-element.34.refs_0_.out_ref, bf16[256,3072]{1,0:T(8,128)(2,1)} %join_out.1.refs_1_, bf16[128,3072]{1,0:T(8,128)(2,1)} %get-tuple-element.87.refs_2_, f32[1,3072]{1,0:T(1,128)} %get-tuple-element.119.refs_3_.refs_4_), custom_call_target="tpu_custom_call" | custom-call | tf_op jit(solution)/shard_map/reduce_out/pallas_call | solution.py:406
  476.2 3.6 join_down.1
  479.8 5.6 join_gate_up.1.refs_1_
  485.5 12.1 fusion.9.refs_2_
  497.5 80.1 %gather_mlp.1 = (bf16[2048,3072]{1,0:T(8,128)(2,1)}, bf16[2048,512]{1,0:T(8,128)(2,1)}, bf16[2048,512]{1,0:T(8,128)(2,1)}, bf16[2048,512]{1,0:T(8,128)(2,1)}) custom-call(bf16[128,3072]{1,0:T(8,128)(2,1)} %get-tuple-element.37.refs_0_, bf16[1024,3072]{1,0:T(8,128)(2,1)} %join_gate_up.1.refs_1_, f32[2048,512]{1,0:T(8,128)} %fusion.9.refs_2_), custom_call_target="tpu_custom_call" | custom-call | tf_op jit(solution)/shard_map/gather_mlp/pallas_call | solution.py:184
  577.7 11.8 convolution_convert_fusion
  594.2 12.6 convolution_convert_fusion.3
  606.9 15.7 %convolution_convert_fusion.1 = bf16[3072,1024]{1,0:T(8,128)(2,1)} fusion(bf16[2048,3072]{1,0:T(8,128)(2,1)S(1)} %bitcast.132, bf16[2048,1024]{1,0:T(8,128)(2,1)S(1)} %constant_dynamic-update-slice_fusion.5.refs_0_), kind=kOutput, calls=%fused_computation.3 | convolution fusion | flops 12888047616 | bytes 23068672 | tf_op jit(solution)/shard_map/dot_general | solution.py:476
  622.6 131.1 %reduce_mlp.1 = (f32[128,3072]{1,0:T(8,128)}, bf16[128,3072]{1,0:T(8,128)(2,1)}, f32[16,3072]{1,0:T(8,128)}) custom-call(bf16[2048,1024]{1,0:T(8,128)(2,1)} %copy-done.2, bf16[1024,3072]{1,0:T(8,128)(2,1)} %join_gate_up.1.refs_1_, f32[128,3072]{1,0:T(8,128)} %get-tuple-element.36.refs_2_, bf16[128,3072]{1,0:T(8,128)(2,1)} %dynamic-slice_bitcast_fusion.5.refs_3_, ...), custom_call_target="tpu_custom_call" | custom-call | tf_op jit(solution)/shard_map/reduce_mlp/pallas_call | solution.py:406
  753.7 75.6 %gather_branch.1 = (bf16[2048,3072]{1,0:T(8,128)(2,1)}, bf16[2048,256]{1,0:T(8,128)(2,1)}) custom-call(bf16[128,3072]{1,0:T(8,128)(2,1)} %get-tuple-element.46.refs_0_, bf16[256,3072]{1,0:T(8,128)(2,1)} %join_out.1.refs_1_), custom_call_target="tpu_custom_call" | custom-call | tf_op jit(solution)/shard_map/gather_branch/pallas_call | solution.py:184
  829.3 8.3 convolution_convert_fusion.4
  838.7 37.0 %attend_back.1.refs_0_ = bf16[2048,768]{1,0:T(8,128)(2,1)} custom-call(s32[8]{0:T(128)} %broadcast_add_fusion.high_ref, bf16[2048,768]{1,0:T(8,128)(2,1)} %qkv.1.qkv_ref, bf16[2048,256]{1,0:T(8,128)(2,1)} %get-tuple-element.34.refs_0_.out_ref, bf16[2048,256]{1,0:T(8,128)(2,1)} %get-tuple-element.49.grad_ref, f32[2,2048]{1,0:T(2,128)} %get-tuple-element.50.lse_ref, ...), custom_call_target="tpu_custom_call" | custom-call | tf_op jit(solution)/shard_map/attend_back/pallas_call | solution.py:652
  875.7 14.2 %convolution_convert_fusion.2 = bf16[3072,768]{0,1:T(8,128)(2,1)S(1)} fusion(bf16[2048,3072]{1,0:T(8,128)(2,1)} %gather_normed1.1.x_ref, bf16[2048,768]{1,0:T(8,128)(2,1)} %attend_back.1.refs_0_), kind=kOutput, calls=%fused_computation.4 | convolution fusion | flops 9666035712 | bytes 20447232 | tf_op jit(solution)/shard_map/dot_general | solution.py:476
  892.1 90.6 %reduce_qkv.1 = (bf16[128,3072]{1,0:T(8,128)(2,1)}, f32[16,3072]{1,0:T(8,128)}) custom-call(bf16[2048,768]{1,0:T(8,128)(2,1)} %attend_back.1.refs_0_, bf16[768,3072]{1,0:T(8,128)(2,1)} %join_qkv.1.w_ref.refs_1_, bf16[128,3072]{1,0:T(8,128)(2,1)} %get-tuple-element.87.refs_2_, f32[128,3072]{1,0:T(8,128)} %get-tuple-element.52.refs_3_, f32[1,3072]{1,0:T(1,128)} %copy-done.23), custom_call_target="tpu_custom_call" | custom-call | tf_op jit(solution)/shard_map/reduce_qkv/pallas_call | solution.py:406
  985.6 2.7 constant_dynamic-slice_fusion.3
  990.4 4.0 constant_dynamic-slice_fusion.7
  997.7 40.6 %collective-permute-done.32 = bf16[1536,192]{0,1:T(8,128)(2,1)S(1)} collective-permute-done((bf16[1536,192]{0,1:T(8,128)(2,1)S(1)}, bf16[1536,192]{0,1:T(8,128)(2,1)S(1)}, u32[]{:S(2)}, u32[]{:S(2)}) %collective-permute-start.32) | collective-permute-done | bytes 589856 | tf_op jit(solution)/shard_map/ppermute | solution.py:757
  1040.7 139.7 %psum.7 = f32[2,3072]{1,0:T(2,128)} all-reduce(f32[2,3072]{1,0:T(2,128)} %pad_maximum_fusion.4), channel_id=1, replica_groups=mesh['fsdp'=2,'ctx'=4,'tp'=4] {'fsdp','ctx','tp'}, use_global_device_ids=true, to_apply=%region_7.8 | all-reduce | flops 6144 | bytes 49152 | tf_op jit(solution)/shard_map/psum | solution.py:974
  1182.9 2.3 collective-permute-start.35
  1186.2 4.6 collective-permute-done.34
  1192.6 2.7 add_convert_fusion.3
  1195.3 2.3 add_convert_fusion.2
  1198.4 2.9 collective-permute-start.41
  1214.5 15.0 %collective-permute-done.42 = bf16[384,512]{1,0:T(8,128)(2,1)S(1)} collective-permute-done((bf16[384,512]{1,0:T(8,128)(2,1)S(1)}, bf16[384,512]{1,0:T(8,128)(2,1)S(1)}, u32[]{:S(2)}, u32[]{:S(2)}) %collective-permute-start.42) | collective-permute-done | bytes 393248 | tf_op jit(solution)/shard_map/ppermute | solution.py:766
  1229.5 9.5 collective-permute-start.31
  1247.6 4.4 add_convert_fusion
  1253.7 18.2 %collective-permute-start.37 = (bf16[384,1024]{1,0:T(8,128)(2,1)}, bf16[384,1024]{1,0:T(8,128)(2,1)}, u32[]{:S(2)}, u32[]{:S(2)}) collective-permute-start(bf16[384,1024]{1,0:T(8,128)(2,1)} %get-tuple-element.90), channel_id=1, source_target_pairs={{0,4},{4,8},{8,12},{12,0},{1,5},{5,9},{9,13},{13,1},{2,6},{6,10},{... | collective-permute-start | bytes 2359304 | tf_op jit(solution)/shard_map/ppermute | solution.py:766
  1273.8 2.9 collective-permute-start.39
  1276.8 22.8 %collective-permute-done.30 = bf16[384,576]{0,1:T(8,128)(2,1)} collective-permute-done((bf16[384,576]{0,1:T(8,128)(2,1)}, bf16[384,576]{0,1:T(8,128)(2,1)}, u32[]{:S(2)}, u32[]{:S(2)}) %collective-permute-start.30) | collective-permute-done | bytes 442400 | tf_op jit(solution)/shard_map/ppermute | solution.py:766
  1302.3 3.2 copy.82
  1305.5 2.3 copy.75
  1309.1 2.3 copy.76
  1311.4 14.5 %collective-permute-done.38 = bf16[384,1024]{1,0:T(8,128)(2,1)} collective-permute-done((bf16[384,1024]{1,0:T(8,128)(2,1)}, bf16[384,1024]{1,0:T(8,128)(2,1)}, u32[]{:S(2)}, u32[]{:S(2)}) %collective-permute-start.38) | collective-permute-done | bytes 786464 | tf_op jit(solution)/shard_map/ppermute | solution.py:766
  1325.9 2.3 copy.77
  1328.2 2.3 copy.78
  1333.7 3.0 copy.79
  1336.8 6.6 copy.83
  1343.3 3.9 copy.107
  (214 shorter events, 103.0 us)
Async XLA Ops:
  7.2 478.3 %all-gather.4.cloned.1.call-start = ((), (), s32[]{:S(2)}) async-start(), calls=%async_computation.1 | async-start | bytes 13369344 | tf_op jit(solution)/shard_map/all_gather | solution.py:772
  10.5 37.3 %copy-start.26 = (bf16[384]{0:T(512)(128)(2,1)S(1)}, bf16[384]{0:T(512)(128)(2,1)}, u32[]{:S(2)}) copy-start(bf16[384]{0:T(512)(128)(2,1)} %param.15) | copy-start | bytes 2308
  10.5 37.3 %copy-start.27 = (bf16[384]{0:T(512)(128)(2,1)S(1)}, bf16[384]{0:T(512)(128)(2,1)}, u32[]{:S(2)}) copy-start(bf16[384]{0:T(512)(128)(2,1)} %param.16) | copy-start | bytes 2308
  10.5 71.2 %copy-start.13 = (bf16[768,384]{1,0:T(8,128)(2,1)S(1)}, bf16[768,384]{1,0:T(8,128)(2,1)}, u32[]{:S(2)}) copy-start(bf16[768,384]{1,0:T(8,128)(2,1)} %param.12) | copy-start | bytes 1769476
  11.5 16.5 %collective-permute-start = (bf16[3,192,384]{2,1,0:T(8,128)(2,1)}, bf16[3,192,384]{2,1,0:T(8,128)(2,1)}, u32[]{:S(2)}, u32[]{:S(2)}) collective-permute-start(bf16[3,192,384]{2,1,0:T(8,128)(2,1)} %bitcast.125), channel_id=1, source_target_pairs={{0,4},{4,8},{8,12},{12,0},{1,5},{5,9},{9,13},{13,1},{2,6},{6,10},{... | collective-permute-start | bytes 1327112 | tf_op jit(solution)/shard_map/ppermute | solution.py:674
  15.6 30.6 %collective-permute-start.1 = (bf16[3,192,384]{2,1,0:T(8,128)(2,1)}, bf16[3,192,384]{2,1,0:T(8,128)(2,1)}, u32[]{:S(2)}, u32[]{:S(2)}) collective-permute-start(bf16[3,192,384]{2,1,0:T(8,128)(2,1)} %bitcast.6), channel_id=1, source_target_pairs={{0,8},{4,12},{8,0},{12,4},{1,9},{5,13},{9,1},{13,5},{2,10},{6,14},... | collective-permute-start | bytes 1327112 | tf_op jit(solution)/shard_map/ppermute | solution.py:674
  19.2 76.4 %copy-start.11 = (bf16[2048,384]{1,0:T(8,128)(2,1)S(1)}, bf16[2048,384]{1,0:T(8,128)(2,1)}, u32[]{:S(2)}) copy-start(bf16[2048,384]{1,0:T(8,128)(2,1)} %param.14) | copy-start | bytes 4718596
  19.2 27.0 %collective-permute-start.2 = (bf16[3,192,384]{2,1,0:T(8,128)(2,1)}, bf16[3,192,384]{2,1,0:T(8,128)(2,1)}, u32[]{:S(2)}, u32[]{:S(2)}) collective-permute-start(bf16[3,192,384]{2,1,0:T(8,128)(2,1)} %bitcast.126), channel_id=1, source_target_pairs={{0,12},{4,0},{8,4},{12,8},{1,13},{5,1},{9,5},{13,9},{2,14},{6,2},{... | collective-permute-start | bytes 1327112 | tf_op jit(solution)/shard_map/ppermute | solution.py:674
  20.8 75.8 %copy-start.10 = (bf16[3,384,192]{1,2,0:T(8,128)(2,1)}, bf16[3,384,192]{1,2,0:T(8,128)(2,1)S(1)}, u32[]{:S(2)}) copy-start(bf16[3,384,192]{1,2,0:T(8,128)(2,1)S(1)} %copy.84) | copy-start | bytes 1327108
  46.2 1146.4 %reduce-scatter.2.cloned.1.call-start = ((), (), s32[]{:S(2)}) async-start(), calls=%async_computation.2 | async-start | bytes 13369344 | tf_op jit(solution)/shard_map/reduce_scatter | solution.py:934
  46.3 50.4 %collective-permute-start.3 = (bf16[3,192,384]{2,1,0:T(8,128)(2,1)S(1)}, bf16[3,192,384]{2,1,0:T(8,128)(2,1)S(1)}, u32[]{:S(2)}, u32[]{:S(2)}) collective-permute-start(bf16[3,192,384]{2,1,0:T(8,128)(2,1)S(1)} %bitcast.121), channel_id=1, source_target_pairs={{0,16},{16,0},{1,17},{17,1},{2,18},{18,2},{3,19},{19,3},{4,20},{20... | collective-permute-start | bytes 1327112 | tf_op jit(solution)/shard_map/ppermute | solution.py:678
  82.5 27.4 %copy-start.14 = (bf16[1,192,384]{2,1,0:T(8,128)(2,1)}, bf16[1,192,384]{2,1,0:T(8,128)(2,1)S(1)}, u32[]{:S(2)}) copy-start(bf16[1,192,384]{2,1,0:T(8,128)(2,1)S(1)} %get-tuple-element.118.refs_0_) | copy-start | bytes 442372
  82.5 11.7 collective-permute-start.7
  85.2 87.3 %copy-start.23 = (f32[1,3072]{1,0:T(1,128)}, f32[1,3072]{1,0:T(1,128)S(1)}, u32[]{:S(2)}) copy-start(f32[1,3072]{1,0:T(1,128)S(1)} %get-tuple-element.120.refs_4_) | copy-start | bytes 36868
  87.4 17.7 %collective-permute-start.8 = (bf16[1,192,384]{2,1,0:T(8,128)(2,1)}, bf16[1,192,384]{2,1,0:T(8,128)(2,1)}, u32[]{:S(2)}, u32[]{:S(2)}) collective-permute-start(bf16[1,192,384]{2,1,0:T(8,128)(2,1)} %get-tuple-element.116), channel_id=1, source_target_pairs={{0,8},{4,12},{8,0},{12,4},{1,9},{5,13},{9,1},{13,5},{2,10},{6,14},... | collective-permute-start | bytes 442376 | tf_op jit(solution)/shard_map/ppermute | solution.py:674
  89.3 15.8 %collective-permute-start.9 = (bf16[1,192,384]{2,1,0:T(8,128)(2,1)}, bf16[1,192,384]{2,1,0:T(8,128)(2,1)S(1)}, u32[]{:S(2)}, u32[]{:S(2)}) collective-permute-start(bf16[1,192,384]{2,1,0:T(8,128)(2,1)} %get-tuple-element.115), channel_id=1, source_target_pairs={{0,12},{4,0},{8,4},{12,8},{1,13},{5,1},{9,5},{13,9},{2,14},{6,2},{... | collective-permute-start | bytes 442376 | tf_op jit(solution)/shard_map/ppermute | solution.py:674
  89.8 18.1 %collective-permute-start.10 = (bf16[1,192,384]{2,1,0:T(8,128)(2,1)S(1)}, bf16[1,192,384]{2,1,0:T(8,128)(2,1)S(1)}, u32[]{:S(2)}, u32[]{:S(2)}) collective-permute-start(bf16[1,192,384]{2,1,0:T(8,128)(2,1)S(1)} %get-tuple-element.118.refs_0_), channel_id=1, source_target_pairs={{0,16},{16,0},{1,17},{17,1},{2,18},{18,2},{3,19},{19,3},{4,20},{20... | collective-permute-start | bytes 442376 | tf_op jit(solution)/shard_map/ppermute | solution.py:678
  94.2 15.8 %copy-start.18 = (bf16[1,192,384]{2,1,0:T(8,128)(2,1)}, bf16[1,192,384]{2,1,0:T(8,128)(2,1)S(1)}, u32[]{:S(2)}) copy-start(bf16[1,192,384]{2,1,0:T(8,128)(2,1)S(1)} %collective-permute-done.7.refs_1_) | copy-start | bytes 442372
  94.2 15.4 %collective-permute-start.11 = (bf16[1,192,384]{2,1,0:T(8,128)(2,1)S(1)}, bf16[1,192,384]{2,1,0:T(8,128)(2,1)S(1)}, u32[]{:S(2)}, u32[]{:S(2)}) collective-permute-start(bf16[1,192,384]{2,1,0:T(8,128)(2,1)S(1)} %collective-permute-done.7.refs_1_), channel_id=1, source_target_pairs={{0,16},{16,0},{1,17},{17,1},{2,18},{18,2},{3,19},{19,3},{4,20},{20... | collective-permute-start | bytes 442376 | tf_op jit(solution)/shard_map/ppermute | solution.py:678
  96.6 17.0 %copy-start.12 = (bf16[1,512,384]{2,1,0:T(8,128)(2,1)}, bf16[1,512,384]{2,1,0:T(8,128)(2,1)S(1)}, u32[]{:S(2)}) copy-start(bf16[1,512,384]{2,1,0:T(8,128)(2,1)S(1)} %get-tuple-element.109.refs_0_) | copy-start | bytes 1179652
  96.6 13.3 copy-start.15
  96.6 45.4 %collective-permute-start.21 = (bf16[1,512,384]{2,1,0:T(8,128)(2,1)}, bf16[1,512,384]{2,1,0:T(8,128)(2,1)}, u32[]{:S(2)}, u32[]{:S(2)}) collective-permute-start(bf16[1,512,384]{2,1,0:T(8,128)(2,1)} %get-tuple-element.108), channel_id=1, source_target_pairs={{0,4},{4,8},{8,12},{12,0},{1,5},{5,9},{9,13},{13,1},{2,6},{6,10},{... | collective-permute-start | bytes 1179656 | tf_op jit(solution)/shard_map/ppermute | solution.py:674
  105.1 42.3 %collective-permute-start.22 = (bf16[1,512,384]{2,1,0:T(8,128)(2,1)}, bf16[1,512,384]{2,1,0:T(8,128)(2,1)}, u32[]{:S(2)}, u32[]{:S(2)}) collective-permute-start(bf16[1,512,384]{2,1,0:T(8,128)(2,1)} %get-tuple-element.107), channel_id=1, source_target_pairs={{0,8},{4,12},{8,0},{12,4},{1,9},{5,13},{9,1},{13,5},{2,10},{6,14},... | collective-permute-start | bytes 1179656 | tf_op jit(solution)/shard_map/ppermute | solution.py:674
  105.1 65.3 %collective-permute-start.23 = (bf16[1,512,384]{2,1,0:T(8,128)(2,1)}, bf16[1,512,384]{2,1,0:T(8,128)(2,1)}, u32[]{:S(2)}, u32[]{:S(2)}) collective-permute-start(bf16[1,512,384]{2,1,0:T(8,128)(2,1)} %get-tuple-element.106), channel_id=1, source_target_pairs={{0,12},{4,0},{8,4},{12,8},{1,13},{5,1},{9,5},{13,9},{2,14},{6,2},{... | collective-permute-start | bytes 1179656 | tf_op jit(solution)/shard_map/ppermute | solution.py:674
  107.9 63.9 %collective-permute-start.24 = (bf16[1,512,384]{2,1,0:T(8,128)(2,1)S(1)}, bf16[1,512,384]{2,1,0:T(8,128)(2,1)}, u32[]{:S(2)}, u32[]{:S(2)}) collective-permute-start(bf16[1,512,384]{2,1,0:T(8,128)(2,1)S(1)} %get-tuple-element.109.refs_0_), channel_id=1, source_target_pairs={{0,16},{16,0},{1,17},{17,1},{2,18},{18,2},{3,19},{19,3},{4,20},{20... | collective-permute-start | bytes 1179656 | tf_op jit(solution)/shard_map/ppermute | solution.py:678
  109.6 10.6 collective-permute-start.12
  113.7 58.8 %copy-start.1 = (bf16[128,3072]{1,0:T(8,128)(2,1)S(1)}, bf16[128,3072]{1,0:T(8,128)(2,1)}, u32[]{:S(2)}) copy-start(bf16[128,3072]{1,0:T(8,128)(2,1)} %get-tuple-element.87.refs_2_) | copy-start | bytes 2359300
  113.7 59.9 %copy-start.17 = (s32[1,2048]{1,0:T(1,128)S(1)}, s32[1,2048]{1,0:T(1,128)}, u32[]{:S(2)}) copy-start(s32[1,2048]{1,0:T(1,128)} %row_ref.3) | copy-start | bytes 24580
  120.1 5.4 collective-permute-start.13
  125.5 48.2 %copy-start.22 = (bf16[1,192,384]{2,1,0:T(8,128)(2,1)}, bf16[1,192,384]{2,1,0:T(8,128)(2,1)S(1)}, u32[]{:S(2)}) copy-start(bf16[1,192,384]{2,1,0:T(8,128)(2,1)S(1)} %collective-permute-done.13.refs_7_) | copy-start | bytes 442372
  125.5 191.5 %collective-permute-start.14 = (bf16[2,512,384]{2,1,0:T(8,128)(2,1)}, bf16[2,512,384]{2,1,0:T(8,128)(2,1)}, u32[]{:S(2)}, u32[]{:S(2)}) collective-permute-start(bf16[2,512,384]{2,1,0:T(8,128)(2,1)} %get-tuple-element.94), channel_id=1, source_target_pairs={{0,4},{4,8},{8,12},{12,0},{1,5},{5,9},{9,13},{13,1},{2,6},{6,10},{... | collective-permute-start | bytes 2359304 | tf_op jit(solution)/shard_map/ppermute | solution.py:674
  142.1 176.2 %collective-permute-start.15 = (bf16[2,512,384]{2,1,0:T(8,128)(2,1)}, bf16[2,512,384]{2,1,0:T(8,128)(2,1)}, u32[]{:S(2)}, u32[]{:S(2)}) collective-permute-start(bf16[2,512,384]{2,1,0:T(8,128)(2,1)} %get-tuple-element.93), channel_id=1, source_target_pairs={{0,8},{4,12},{8,0},{12,4},{1,9},{5,13},{9,1},{13,5},{2,10},{6,14},... | collective-permute-start | bytes 2359304 | tf_op jit(solution)/shard_map/ppermute | solution.py:674
  147.4 171.6 %collective-permute-start.16 = (bf16[2,512,384]{2,1,0:T(8,128)(2,1)}, bf16[2,512,384]{2,1,0:T(8,128)(2,1)}, u32[]{:S(2)}, u32[]{:S(2)}) collective-permute-start(bf16[2,512,384]{2,1,0:T(8,128)(2,1)} %get-tuple-element.92), channel_id=1, source_target_pairs={{0,12},{4,0},{8,4},{12,8},{1,13},{5,1},{9,5},{13,9},{2,14},{6,2},{... | collective-permute-start | bytes 2359304 | tf_op jit(solution)/shard_map/ppermute | solution.py:674
  170.4 13.4 collective-permute-start.4
  171.8 21.5 %collective-permute-start.5 = (bf16[3,192,384]{2,1,0:T(8,128)(2,1)}, bf16[3,192,384]{2,1,0:T(8,128)(2,1)}, u32[]{:S(2)}, u32[]{:S(2)}) collective-permute-start(bf16[3,192,384]{2,1,0:T(8,128)(2,1)} %collective-permute-done.1.refs_2_), channel_id=1, source_target_pairs={{0,16},{16,0},{1,17},{17,1},{2,18},{18,2},{3,19},{19,3},{4,20},{20... | collective-permute-start | bytes 1327112 | tf_op jit(solution)/shard_map/ppermute | solution.py:678
  183.8 131.1 %collective-permute-start.6 = (bf16[3,192,384]{2,1,0:T(8,128)(2,1)}, bf16[3,192,384]{2,1,0:T(8,128)(2,1)}, u32[]{:S(2)}, u32[]{:S(2)}) collective-permute-start(bf16[3,192,384]{2,1,0:T(8,128)(2,1)} %collective-permute-done.2.refs_3_), channel_id=1, source_target_pairs={{0,16},{16,0},{1,17},{17,1},{2,18},{18,2},{3,19},{19,3},{4,20},{20... | collective-permute-start | bytes 1327112 | tf_op jit(solution)/shard_map/ppermute | solution.py:678
  193.3 123.0 %collective-permute-start.25 = (bf16[1,512,384]{2,1,0:T(8,128)(2,1)}, bf16[1,512,384]{2,1,0:T(8,128)(2,1)}, u32[]{:S(2)}, u32[]{:S(2)}) collective-permute-start(bf16[1,512,384]{2,1,0:T(8,128)(2,1)} %collective-permute-done.21.refs_1_), channel_id=1, source_target_pairs={{0,16},{16,0},{1,17},{17,1},{2,18},{18,2},{3,19},{19,3},{4,20},{20... | collective-permute-start | bytes 1179656 | tf_op jit(solution)/shard_map/ppermute | solution.py:678
  314.9 164.9 %collective-permute-start.17 = (bf16[2,512,384]{2,1,0:T(8,128)(2,1)}, bf16[2,512,384]{2,1,0:T(8,128)(2,1)}, u32[]{:S(2)}, u32[]{:S(2)}) collective-permute-start(bf16[2,512,384]{2,1,0:T(8,128)(2,1)} %get-tuple-element.95.refs_0_), channel_id=1, source_target_pairs={{0,16},{16,0},{1,17},{17,1},{2,18},{18,2},{3,19},{19,3},{4,20},{20... | collective-permute-start | bytes 2359304 | tf_op jit(solution)/shard_map/ppermute | solution.py:678
  316.3 27.1 %collective-permute-start.26 = (bf16[1,512,384]{2,1,0:T(8,128)(2,1)}, bf16[1,512,384]{2,1,0:T(8,128)(2,1)S(1)}, u32[]{:S(2)}, u32[]{:S(2)}) collective-permute-start(bf16[1,512,384]{2,1,0:T(8,128)(2,1)} %collective-permute-done.22.refs_2_), channel_id=1, source_target_pairs={{0,16},{16,0},{1,17},{17,1},{2,18},{18,2},{3,19},{19,3},{4,20},{20... | collective-permute-start | bytes 1179656 | tf_op jit(solution)/shard_map/ppermute | solution.py:678
  317.0 162.8 %collective-permute-start.18 = (bf16[2,512,384]{2,1,0:T(8,128)(2,1)}, bf16[2,512,384]{2,1,0:T(8,128)(2,1)}, u32[]{:S(2)}, u32[]{:S(2)}) collective-permute-start(bf16[2,512,384]{2,1,0:T(8,128)(2,1)} %collective-permute-done.14.refs_1_), channel_id=1, source_target_pairs={{0,16},{16,0},{1,17},{17,1},{2,18},{18,2},{3,19},{19,3},{4,20},{20... | collective-permute-start | bytes 2359304 | tf_op jit(solution)/shard_map/ppermute | solution.py:678
  318.3 161.5 %collective-permute-start.19 = (bf16[2,512,384]{2,1,0:T(8,128)(2,1)}, bf16[2,512,384]{2,1,0:T(8,128)(2,1)}, u32[]{:S(2)}, u32[]{:S(2)}) collective-permute-start(bf16[2,512,384]{2,1,0:T(8,128)(2,1)} %collective-permute-done.15.refs_2_), channel_id=1, source_target_pairs={{0,16},{16,0},{1,17},{17,1},{2,18},{18,2},{3,19},{19,3},{4,20},{20... | collective-permute-start | bytes 2359304 | tf_op jit(solution)/shard_map/ppermute | solution.py:678
  319.0 160.8 %collective-permute-start.20 = (bf16[2,512,384]{2,1,0:T(8,128)(2,1)}, bf16[2,512,384]{2,1,0:T(8,128)(2,1)}, u32[]{:S(2)}, u32[]{:S(2)}) collective-permute-start(bf16[2,512,384]{2,1,0:T(8,128)(2,1)} %collective-permute-done.16.refs_3_), channel_id=1, source_target_pairs={{0,16},{16,0},{1,17},{17,1},{2,18},{18,2},{3,19},{19,3},{4,20},{20... | collective-permute-start | bytes 2359304 | tf_op jit(solution)/shard_map/ppermute | solution.py:678
  343.3 132.8 %collective-permute-start.27 = (bf16[1,512,384]{2,1,0:T(8,128)(2,1)}, bf16[1,512,384]{2,1,0:T(8,128)(2,1)}, u32[]{:S(2)}, u32[]{:S(2)}) collective-permute-start(bf16[1,512,384]{2,1,0:T(8,128)(2,1)} %collective-permute-done.23.refs_3_), channel_id=1, source_target_pairs={{0,16},{16,0},{1,17},{17,1},{2,18},{18,2},{3,19},{19,3},{4,20},{20... | collective-permute-start | bytes 1179656 | tf_op jit(solution)/shard_map/ppermute | solution.py:678
  589.5 753.9 %all-gather.8.cloned.1.call-start = ((), (), s32[]{:S(2)}) async-start(), calls=%async_computation.4 | async-start | bytes 3932160 | tf_op jit(solution)/shard_map/all_gather | solution.py:966
  592.6 14.2 %slice-start = ((s8[12582912]{0:T(1024)(128)(4,1)}), s8[4194304]{0:T(1024)(128)(4,1)S(1)}, s32[]{:S(2)}) async-start(s8[12582912]{0:T(1024)(128)(4,1)} %bitcast.131), calls=%async_computation.5 | async-start | bytes 8388608
  982.8 360.5 %all-gather.6.cloned.1.call-start = ((), (), s32[]{:S(2)}) async-start(), calls=%async_computation.3 | async-start | bytes 3932160 | tf_op jit(solution)/shard_map/all_gather | solution.py:936
  988.2 207.0 %collective-permute-start.40 = (bf16[1536,512]{1,0:T(8,128)(2,1)}, bf16[1536,512]{1,0:T(8,128)(2,1)}, u32[]{:S(2)}, u32[]{:S(2)}) collective-permute-start(bf16[1536,512]{1,0:T(8,128)(2,1)} %constant_dynamic-slice_fusion.3), channel_id=1, source_target_pairs={{0,16},{16,0},{1,17},{17,1},{2,18},{18,2},{3,19},{19,3},{4,20},{20... | collective-permute-start | bytes 4718600 | tf_op jit(solution)/shard_map/ppermute | solution.py:757
  988.3 50.1 %collective-permute-start.32 = (bf16[1536,192]{0,1:T(8,128)(2,1)S(1)}, bf16[1536,192]{0,1:T(8,128)(2,1)S(1)}, u32[]{:S(2)}, u32[]{:S(2)}) collective-permute-start(bf16[1536,192]{0,1:T(8,128)(2,1)S(1)} %constant_dynamic-slice_fusion.11), channel_id=1, source_target_pairs={{0,16},{16,0},{1,17},{17,1},{2,18},{18,2},{3,19},{19,3},{4,20},{20... | collective-permute-start | bytes 1769480 | tf_op jit(solution)/shard_map/ppermute | solution.py:757
  994.3 44.0 %copy-start.4 = (bf16[3072,4,48]{0,2,1:T(8,128)(2,1)S(1)}, bf16[3072,4,48]{0,2,1:T(8,128)(2,1)}, u32[]{:S(2)}) copy-start(bf16[3072,4,48]{0,2,1:T(8,128)(2,1)} %slice.53) | copy-start | bytes 3538948
  994.3 45.8 %copy-start.25 = (f32[3072]{0:T(1024)S(1)}, f32[3072]{0:T(1024)}, u32[]{:S(2)}) copy-start(f32[3072]{0:T(1024)} %reduce_sum.39) | copy-start | bytes 36868
  994.3 253.3 %collective-permute-start.36 = (bf16[1536,1024]{1,0:T(8,128)(2,1)}, bf16[1536,1024]{1,0:T(8,128)(2,1)}, u32[]{:S(2)}, u32[]{:S(2)}) collective-permute-start(bf16[1536,1024]{1,0:T(8,128)(2,1)} %constant_dynamic-slice_fusion.7), channel_id=1, source_target_pairs={{0,16},{16,0},{1,17},{17,1},{2,18},{18,2},{3,19},{19,3},{4,20},{20... | collective-permute-start | bytes 9437192 | tf_op jit(solution)/shard_map/ppermute | solution.py:757
  995.7 210.0 %collective-permute-start.28 = (bf16[1536,576]{0,1:T(8,128)(2,1)}, bf16[1536,576]{0,1:T(8,128)(2,1)}, u32[]{:S(2)}, u32[]{:S(2)}) collective-permute-start(bf16[1536,576]{0,1:T(8,128)(2,1)} %constant_dynamic-slice_fusion.16), channel_id=1, source_target_pairs={{0,16},{16,0},{1,17},{17,1},{2,18},{18,2},{3,19},{19,3},{4,20},{20... | collective-permute-start | bytes 5308424 | tf_op jit(solution)/shard_map/ppermute | solution.py:757
  1040.1 142.8 %collective-permute-start.33 = (bf16[384,192]{0,1:T(8,128)(2,1)}, bf16[384,192]{0,1:T(8,128)(2,1)}, u32[]{:S(2)}, u32[]{:S(2)}) collective-permute-start(bf16[384,192]{0,1:T(8,128)(2,1)} %get-tuple-element.114), channel_id=1, source_target_pairs={{0,4},{4,8},{8,12},{12,0},{1,5},{5,9},{9,13},{13,1},{2,6},{6,10},{... | collective-permute-start | bytes 442376 | tf_op jit(solution)/shard_map/ppermute | solution.py:766
  1181.9 8.9 collective-permute-start.34
  1182.9 8.5 collective-permute-start.35
  1198.4 14.2 %collective-permute-start.41 = (bf16[384,512]{1,0:T(8,128)(2,1)S(1)}, bf16[384,512]{1,0:T(8,128)(2,1)S(1)}, u32[]{:S(2)}, u32[]{:S(2)}) collective-permute-start(bf16[384,512]{1,0:T(8,128)(2,1)S(1)} %get-tuple-element.105), channel_id=1, source_target_pairs={{0,4},{4,8},{8,12},{12,0},{1,5},{5,9},{9,13},{13,1},{2,6},{6,10},{... | collective-permute-start | bytes 1179656 | tf_op jit(solution)/shard_map/ppermute | solution.py:766
  1201.3 28.2 %collective-permute-start.42 = (bf16[384,512]{1,0:T(8,128)(2,1)S(1)}, bf16[384,512]{1,0:T(8,128)(2,1)S(1)}, u32[]{:S(2)}, u32[]{:S(2)}) collective-permute-start(bf16[384,512]{1,0:T(8,128)(2,1)S(1)} %get-tuple-element.104), channel_id=1, source_target_pairs={{0,8},{4,12},{8,0},{12,4},{1,9},{5,13},{9,1},{13,5},{2,10},{6,14},... | collective-permute-start | bytes 1179656 | tf_op jit(solution)/shard_map/ppermute | solution.py:766
  1203.1 38.5 %collective-permute-start.43 = (bf16[384,512]{1,0:T(8,128)(2,1)}, bf16[384,512]{1,0:T(8,128)(2,1)}, u32[]{:S(2)}, u32[]{:S(2)}) collective-permute-start(bf16[384,512]{1,0:T(8,128)(2,1)} %get-tuple-element.103), channel_id=1, source_target_pairs={{0,12},{4,0},{8,4},{12,8},{1,13},{5,1},{9,5},{13,9},{2,14},{6,2},{... | collective-permute-start | bytes 1179656 | tf_op jit(solution)/shard_map/ppermute | solution.py:766
  1208.9 37.7 %collective-permute-start.29 = (bf16[384,576]{0,1:T(8,128)(2,1)}, bf16[384,576]{0,1:T(8,128)(2,1)}, u32[]{:S(2)}, u32[]{:S(2)}) collective-permute-start(bf16[384,576]{0,1:T(8,128)(2,1)} %get-tuple-element.98), channel_id=1, source_target_pairs={{0,4},{4,8},{8,12},{12,0},{1,5},{5,9},{9,13},{13,1},{2,6},{6,10},{... | collective-permute-start | bytes 1327112 | tf_op jit(solution)/shard_map/ppermute | solution.py:766
  1212.7 86.9 %collective-permute-start.30 = (bf16[384,576]{0,1:T(8,128)(2,1)}, bf16[384,576]{0,1:T(8,128)(2,1)}, u32[]{:S(2)}, u32[]{:S(2)}) collective-permute-start(bf16[384,576]{0,1:T(8,128)(2,1)} %get-tuple-element.97), channel_id=1, source_target_pairs={{0,8},{4,12},{8,0},{12,4},{1,9},{5,13},{9,1},{13,5},{2,10},{6,14},... | collective-permute-start | bytes 1327112 | tf_op jit(solution)/shard_map/ppermute | solution.py:766
  1229.5 71.1 %collective-permute-start.31 = (bf16[384,576]{0,1:T(8,128)(2,1)}, bf16[384,576]{0,1:T(8,128)(2,1)}, u32[]{:S(2)}, u32[]{:S(2)}) collective-permute-start(bf16[384,576]{0,1:T(8,128)(2,1)} %get-tuple-element.96), channel_id=1, source_target_pairs={{0,12},{4,0},{8,4},{12,8},{1,13},{5,1},{9,5},{13,9},{2,14},{6,2},{... | collective-permute-start | bytes 1327112 | tf_op jit(solution)/shard_map/ppermute | solution.py:766
  1253.7 55.4 %collective-permute-start.37 = (bf16[384,1024]{1,0:T(8,128)(2,1)}, bf16[384,1024]{1,0:T(8,128)(2,1)}, u32[]{:S(2)}, u32[]{:S(2)}) collective-permute-start(bf16[384,1024]{1,0:T(8,128)(2,1)} %get-tuple-element.90), channel_id=1, source_target_pairs={{0,4},{4,8},{8,12},{12,0},{1,5},{5,9},{9,13},{13,1},{2,6},{6,10},{... | collective-permute-start | bytes 2359304 | tf_op jit(solution)/shard_map/ppermute | solution.py:766
  1271.9 53.9 %collective-permute-start.38 = (bf16[384,1024]{1,0:T(8,128)(2,1)}, bf16[384,1024]{1,0:T(8,128)(2,1)}, u32[]{:S(2)}, u32[]{:S(2)}) collective-permute-start(bf16[384,1024]{1,0:T(8,128)(2,1)} %get-tuple-element.89), channel_id=1, source_target_pairs={{0,8},{4,12},{8,0},{12,4},{1,9},{5,13},{9,1},{13,5},{2,10},{6,14},... | collective-permute-start | bytes 2359304 | tf_op jit(solution)/shard_map/ppermute | solution.py:766
  1273.8 54.3 %collective-permute-start.39 = (bf16[384,1024]{1,0:T(8,128)(2,1)}, bf16[384,1024]{1,0:T(8,128)(2,1)}, u32[]{:S(2)}, u32[]{:S(2)}) collective-permute-start(bf16[384,1024]{1,0:T(8,128)(2,1)} %get-tuple-element.88), channel_id=1, source_target_pairs={{0,12},{4,0},{8,4},{12,8},{1,13},{5,1},{9,5},{13,9},{2,14},{6,2},{... | collective-permute-start | bytes 2359304 | tf_op jit(solution)/shard_map/ppermute | solution.py:766
  (17 other events, 73.5 us)
Sparse Core Ops, SparseCore 0:
  46.3 192.3 all-gather.3
  589.6 173.2 reduce-scatter.1
  982.9 31.6 all-gather.7
  1195.4 30.1 all-gather.5

commit v2 on v1

--- a/solution.py
+++ b/solution.py
@@ -7,6 +7,7 @@
 from jax.experimental import pallas as pl
 from jax.experimental.pallas import tpu as pltpu
 from jax.sharding import PartitionSpec as P
+
 
 HD = 96
 HALF = HD // 2
@@ -16,9 +17,14 @@
 ROPE_BASE = 10000.0
 GROUP = ("ctx", "tp")
 BLK = 256
+GAIN_ROWS = 16
 MESH = pl.DeviceIdType.MESH
 SUBS = 2
 VLIM = 64 * 1024 * 1024 - 65536
+
+
+def cost(us):
+    return pl.CostEstimate(flops=0, bytes_accessed=us * 3_000_000, transcendentals=0)
 
 
 def near_order(c, j, size):
@@ -50,13 +56,169 @@
     pl.semaphore_wait(barrier, jnp.where((c > 0) & (c < size - 1), 4, 3))
 
 
-def gather_kernel(size, part, n_in, n_out, compute, *refs):
+def greet_all(c, y, k, size, groups):
+    barrier = pltpu.get_barrier_semaphore()
+    f = lax.axis_index("fsdp")
+
+    def hello(dev):
+        pl.semaphore_signal(barrier, inc=1, device_id=dev, device_id_type=MESH)
+
+    for s in range(1, size):
+        hello({"ctx": (c + s) % size})
+    for g in range(1, groups):
+        hello({"fsdp": (f + g) % groups})
+    hello({"tp": (1 - y) * 2 + k})
+    hello({"tp": y * 2 + 1 - k})
+    pl.semaphore_wait(barrier, size + groups)
+
+
+class Moves:
+    def __init__(self, size, groups, sent, pieces, z_sems, x_sems):
+        self.size, self.groups, self.sent, self.pieces = size, groups, sent, pieces
+        self.z_sems, self.x_sems = z_sems, x_sems
+        self.c, self.f = lax.axis_index("ctx"), lax.axis_index("fsdp")
+
+    def z(self, w, s):
+        to = (self.c + s) % self.size
+        return pltpu.make_async_remote_copy(
+            src_ref=self.sent[w].at[to],
+            dst_ref=self.pieces[w].at[self.f * self.size + self.c],
+            send_sem=self.z_sems.at[w, s - 1, 0],
+            recv_sem=self.z_sems.at[w, s - 1, 1],
+            device_id={"ctx": to},
+            device_id_type=MESH,
+        )
+
+    def x(self, w, g, s):
+        slot = self.pieces[w].at[self.f * self.size + (self.c + self.size - s) % self.size]
+        return pltpu.make_async_remote_copy(
+            src_ref=slot if s else self.sent[w].at[self.c],
+            dst_ref=slot,
+            send_sem=self.x_sems.at[w, g - 1, s, 0],
+            recv_sem=self.x_sems.at[w, g - 1, s, 1],
+            device_id={"fsdp": (self.f + g) % self.groups},
+            device_id_type=MESH,
+        )
+
+    def start_z(self, w, s):
+        self.z(w, s).start()
+
+    def start_x(self, w, s):
+        if s:
+            self.z(w, s).wait_recv()
+        for g in range(1, self.groups):
+            self.x(w, g, s).start()
+
+    def finish(self):
+        for w in range(len(self.sent)):
+            for s in range(self.size):
+                if s:
+                    self.z(w, s).wait_send()
+                for g in range(1, self.groups):
+                    self.x(w, g, s).wait()
+
+
+class HandOut:
+    def __init__(self, size, groups, part, out, got, mine, ready, x_sems, z_sems, l_sems):
+        self.size, self.groups, self.part, self.out = size, groups, part, out
+        self.got, self.mine, self.ready = got, mine, ready
+        self.x_sems, self.z_sems, self.l_sems = x_sems, z_sems, l_sems
+        self.c, self.f = lax.axis_index("ctx"), lax.axis_index("fsdp")
+        self.d = mine.shape[1]
+
+    def rows(self, f, c):
+        return self.part.at[pl.ds(pl.multiple_of((f * self.size + c) * self.d, self.d), self.d)]
+
+    def x(self, g, cc):
+        to = (self.f + g) % self.groups
+        return pltpu.make_async_remote_copy(
+            src_ref=self.rows(to, cc),
+            dst_ref=self.got.at[g - 1, cc],
+            send_sem=self.x_sems.at[g - 1, cc, 0],
+            recv_sem=self.x_sems.at[g - 1, cc, 1],
+            device_id={"fsdp": to},
+            device_id_type=MESH,
+        )
+
+    def load(self, cc):
+        return pltpu.make_async_copy(self.rows(self.f, cc), self.mine.at[cc], self.l_sems.at[cc])
+
+    def z(self, cc, source):
+        return pltpu.make_async_remote_copy(
+            src_ref=self.ready.at[cc],
+            dst_ref=self.out.at[self.c],
+            send_sem=self.z_sems.at[cc, 0],
+            recv_sem=self.z_sems.at[source, 1],
+            device_id={"ctx": cc},
+            device_id_type=MESH,
+        )
+
+    def keep(self):
+        return pltpu.make_async_copy(
+            self.ready.at[self.c], self.out.at[self.c], self.l_sems.at[self.size]
+        )
+
+    def each(self, body):
+        def one(i, carry):
+            body(i)
+            return carry
+
+        lax.fori_loop(0, self.size, one, 0)
+
+    def start(self, cc):
+        for g in range(1, self.groups):
+            self.x(g, cc).start()
+        self.load(cc).start()
+
+    def step(self, cc):
+        self.load(cc).wait()
+        for g in range(1, self.groups):
+            self.x(g, cc).wait_recv()
+
+        def add(i, carry):
+            r = pl.ds(pl.multiple_of(i * 16, 16), 16)
+            value = self.mine[cc, r, :].astype(jnp.float32)
+            for g in range(1, self.groups):
+                value = value + self.got[g - 1, cc, r, :].astype(jnp.float32)
+            self.ready[cc, r, :] = value.astype(jnp.bfloat16)
+            return carry
+
+        lax.fori_loop(0, self.d // 16, add, 0)
+
+        @pl.when(cc != self.c)
+        def _():
+            self.z(cc, self.c).start()
+
+        @pl.when(cc == self.c)
+        def _():
+            self.keep().start()
+
+    def finish(self):
+        def one(cc):
+            for g in range(1, self.groups):
+                self.x(g, cc).wait_send()
+
+            @pl.when(cc != self.c)
+            def _():
+                self.z(cc, self.c).wait_send()
+                self.z(cc, cc).wait_recv()
+
+        self.each(one)
+        self.keep().wait()
+
+
+def gather_kernel(size, groups, plan, n_move, part, n_in, n_out, compute, *refs):
     x_ref = refs[0]
     hbm_ins = refs[1 : 1 + n_in]
-    full_ref = refs[1 + n_in]
-    outs = refs[2 + n_in : 2 + n_in + n_out]
-    ins = refs[2 + n_in + n_out : 2 + 2 * n_in + n_out]
-    buf, recv, zs, ys, ks, local, load, in_sems = refs[2 + 2 * n_in + n_out :]
+    sent = refs[1 + n_in : 1 + n_in + n_move]
+    refs = refs[1 + n_in + n_move :]
+    full_ref = refs[0]
+    outs = refs[1 : 1 + n_out]
+    moved = refs[1 + n_out : 1 + n_out + n_move]
+    refs = refs[1 + n_out + n_move :]
+    ins = refs[:n_in]
+    buf, recv, zs, ys, ks, local, load, in_sems, *move_sems = refs[n_in:]
+    moves = Moves(size, groups, sent, moved, *move_sems) if n_move else None
     c, y, k = places()
     sub = part // SUBS
 
@@ -104,7 +266,10 @@
     first.start()
     for i in range(n_in):
         pltpu.make_async_copy(hbm_ins[i], ins[i], in_sems.at[i]).start()
-    greet(c, y, k, size)
+    if moves:
+        greet_all(c, y, k, size, groups)
+    else:
+        greet(c, y, k, size)
     first.wait()
 
     def z_stage(cc, s):
@@ -121,6 +286,12 @@
 
     for s in range(SUBS):
         z_stage(c, s)
+
+    def move_on(step):
+        for kind, w, s in plan.get(step, ()):
+            (moves.start_z if kind == "z" else moves.start_x)(w, s)
+
+    move_on(-1)
     for i in range(n_in):
         pltpu.make_async_copy(hbm_ins[i], ins[i], in_sems.at[i]).wait()
 
@@ -152,6 +323,13 @@
                     if s == SUBS - 1:
                         finish(cc, 1 - y)
 
+        for at in sorted(plan):
+            if at >= 0:
+
+                @pl.when(r == at)
+                def _():
+                    move_on(at)
+
         return carry
 
     lax.fori_loop(0, size, step, 0)
@@ -174,18 +352,39 @@
         return carry
 
     lax.fori_loop(0, size, drain, 0)
-
-
-def gather_call(x, ins, out_shapes, compute, name, cid, size):
+    if moves:
+        moves.finish()
+
+
+def gather_call(x, ins, out_shapes, compute, cid, size, sent=(), plan=None):
     part, width = x.shape
+    groups = lax.axis_size("fsdp")
+    dma = pltpu.SemaphoreType.DMA
     any_spec = pl.BlockSpec(memory_space=pl.ANY)
     vmem = pl.BlockSpec(memory_space=pltpu.VMEM)
     full = jax.ShapeDtypeStruct((size * 4 * part, width), x.dtype)
     return pl.pallas_call(
-        functools.partial(gather_kernel, size, part, len(ins), len(out_shapes), compute),
-        out_shape=(full, *out_shapes),
-        in_specs=[any_spec] * (1 + len(ins)),
-        out_specs=(any_spec, *([vmem] * len(out_shapes))),
+        functools.partial(
+            gather_kernel,
+            size,
+            groups,
+            plan or {},
+            len(sent),
+            part,
+            len(ins),
+            len(out_shapes),
+            compute,
+        ),
+        out_shape=(
+            full,
+            *out_shapes,
+            *(
+                jax.ShapeDtypeStruct((groups * size, *one.shape[1:]), one.dtype)
+                for one in sent
+            ),
+        ),
+        in_specs=[any_spec] * (1 + len(ins) + len(sent)),
+        out_specs=(any_spec, *([vmem] * len(out_shapes)), *([any_spec] * len(sent))),
         scratch_shapes=[
             *(pltpu.VMEM(one.shape, one.dtype) for one in ins),
             pltpu.VMEM((size * 2, 2 * part, width), x.dtype),
@@ -196,18 +395,27 @@
             pltpu.SemaphoreType.DMA((size * 2,)),
             pltpu.SemaphoreType.DMA,
             pltpu.SemaphoreType.DMA((max(len(ins), 1),)),
+            *(
+                [dma((len(sent), size - 1, 2)), dma((len(sent), max(groups - 1, 1), size, 2))]
+                if sent
+                else []
+            ),
         ],
         compiler_params=pltpu.CompilerParams(
             collective_id=cid, has_side_effects=True, vmem_limit_bytes=VLIM
         ),
-        name=name,
-    )(x, *ins)
-
-
-def reduce_kernel(size, part, n_in, n_out, final, *refs):
+        cost_estimate=cost(75),
+    )(x, *ins, *sent)
+
+
+def reduce_kernel(size, groups, last, plan, n_move, part, n_in, n_out, final, *refs):
     a_ref, w_ref = refs[:2]
     ins = refs[2 : 2 + n_in]
+    sent = refs[2 + n_in : 2 + n_in + n_move]
+    refs = refs[n_move:]
     outs = refs[2 + n_in : 2 + n_in + n_out]
+    moved = refs[2 + n_in + n_out : 2 + n_in + n_out + n_move]
+    refs = refs[n_move:]
     (
         own,
         ksend,
@@ -218,11 +426,16 @@
         zsend,
         zrecv,
         total,
+        prod,
         k_sems,
         y_sems,
         z_sems,
+        *extra,
     ) = refs[2 + n_in + n_out :]
+    moves = Moves(size, groups, sent, moved, *extra) if n_move else None
+    hand = HandOut(size, groups, ins[-1], outs[2], *extra[9:]) if last else None
     c, y, k = places()
+    depth = a_ref.shape[1]
     chunk = 16
     tile = 512
     width = total.shape[1]
@@ -257,7 +470,16 @@
         r = pl.ds(s * sub, sub)
         return remote(zsend.at[cc, r], zrecv.at[1, cc, r], z_sems.at[1, cc, s], {"ctx": c - 1})
 
-    greet(c, y, k, size)
+    if last or moves:
+        greet_all(c, y, k, size, groups)
+    else:
+        greet(c, y, k, size)
+
+    def move_on(step):
+        for kind, w, s in plan.get(step, ()):
+            (moves.start_z if kind == "z" else moves.start_x)(w, s)
+
+    move_on(-1)
 
     def rows(i):
         return pl.ds(pl.multiple_of(i * chunk, chunk), chunk)
@@ -274,25 +496,27 @@
 
     def produce(cc, yy, keep):
         pair = cc * 2 + yy
-        mine = pl.ds(pl.multiple_of(pair * 2 * part + k * part, part), part)
-        other = pl.ds(pl.multiple_of(pair * 2 * part + (1 - k) * part, part), part)
+        both = pl.ds(pl.multiple_of(pair * 2 * part, 2 * part), 2 * part)
+        mine = pl.ds(pl.multiple_of(k * part, part), part)
+        other = pl.ds(pl.multiple_of((1 - k) * part, part), part)
 
         def one(i, carry):
             lanes = pl.ds(pl.multiple_of(i * tile, tile), tile)
-            w = w_ref[:, lanes]
-            ksend[pair, :, lanes] = jnp.dot(
-                a_ref[other, :], w, preferred_element_type=jnp.float32
-            ).astype(jnp.bfloat16)
-            own[keep, :, lanes] = jnp.dot(a_ref[mine, :], w, preferred_element_type=jnp.float32)
+            prod[...] = jnp.dot(
+                a_ref[both, :], w_ref[0:depth, lanes], preferred_element_type=jnp.float32
+            )
+            ksend[pair, :, lanes] = prod[other, :].astype(jnp.bfloat16)
+            own[keep, :, lanes] = prod[mine, :]
             return carry
 
         lax.fori_loop(0, width // tile, one, 0)
         k_copy(cc, yy).start()
 
-    def first(j, carry):
+    def first(j):
         cc = near_order(c, size - 1 - j, size)
+        if last:
+            hand.start(cc)
         produce(cc, 1 - y, 0)
-        produce(cc, y, 1)
         k_copy(cc, 1 - y).wait_recv()
 
         def add_y(r):
@@ -302,15 +526,13 @@
         for s in range(SUBS):
             sweep(add_y, s)
             y_copy(cc, s).start()
+        produce(cc, y, 1)
         k_copy(cc, y).wait_recv()
 
         def add_k(r):
             qown[cc, r, :] = own[1, r, :] + krecv[cc * 2 + y, r, :].astype(jnp.float32)
 
         sweep(add_k)
-        return carry
-
-    lax.fori_loop(0, size, first, 0)
 
     def pass_on(cc, s, into, edge, send):
         @pl.when(jnp.logical_not(edge))
@@ -335,49 +557,82 @@
 
         send(cc, s).start()
 
-    def second(j, carry):
+    def second(j):
         cc = near_order(c, size - 1 - j, size)
         for s in range(SUBS):
-            y_copy(cc, s).wait_recv()
 
             @pl.when(cc > c)
             def _():
+                y_copy(cc, s).wait_recv()
                 pass_on(cc, s, 0, c == 0, z_up)
 
             @pl.when(cc < c)
             def _():
+                y_copy(cc, s).wait_recv()
                 pass_on(cc, s, 1, c == size - 1, z_down)
 
+        if last:
+            hand.step(cc)
+
+        for at in sorted(plan):
+            if at >= 0:
+
+                @pl.when(j == at)
+                def _():
+                    move_on(at)
+
+    lag = jnp.where((c == 0) | (c == size - 1), 1, 2)
+
+    def both(i, carry):
+        @pl.when(i < size)
+        def _():
+            first(i)
+
+        @pl.when((i >= lag) & (i - lag < size))
+        def _():
+            second(i - lag)
+
         return carry
 
-    lax.fori_loop(0, size, second, 0)
-
-    def add_own(r):
-        total[r, :] = qown[c, r, :] + yrecv[c, r, :].astype(jnp.float32)
-
-    sweep(add_own)
-
-    @pl.when(c > 0)
-    def _():
-        for s in range(SUBS):
+    lax.fori_loop(0, size + 2, both, 0)
+
+    def sum_up(r):
+        own_sum = qown[c, r, :] + yrecv[c, r, :].astype(jnp.float32)
+
+        @pl.when(c == 0)
+        def _():
+            total[r, :] = own_sum + zrecv[1, c, r, :].astype(jnp.float32)
+
+        @pl.when(c == size - 1)
+        def _():
+            total[r, :] = own_sum + zrecv[0, c, r, :].astype(jnp.float32)
+
+        @pl.when((c > 0) & (c < size - 1))
+        def _():
+            below = own_sum + zrecv[0, c, r, :].astype(jnp.float32)
+            total[r, :] = below + zrecv[1, c, r, :].astype(jnp.float32)
+
+    begin, one_chunk, end = final(total, ins, outs, extra)
+    begin()
+    for s in range(SUBS):
+        y_copy(c, s).wait_recv()
+
+        @pl.when(c > 0)
+        def _():
             z_up(c, s).wait_recv()
 
-        def add(r):
-            total[r, :] += zrecv[0, c, r, :].astype(jnp.float32)
-
-        sweep(add)
-
-    @pl.when(c < size - 1)
-    def _():
-        for s in range(SUBS):
+        @pl.when(c < size - 1)
+        def _():
             z_down(c, s).wait_recv()
 
-        def add(r):
-            total[r, :] += zrecv[1, c, r, :].astype(jnp.float32)
-
-        sweep(add)
-
-    final(total, sweep, ins, outs)
+        def close(r):
+            sum_up(r)
+            one_chunk(r)
+
+        sweep(close, s)
+    end()
+    if last:
+        spread_out(size, groups, c, y, k, ydev, kdev, outs, extra)
 
     def drain(cc, carry):
         for yy in range(2):
@@ -396,18 +651,133 @@
         return carry
 
     lax.fori_loop(0, size, drain, 0)
-
-
-def reduce_call(a, w, ins, out_shapes, final, name, cid, size):
+    if moves:
+        moves.finish()
+    if last:
+        hand.finish()
+
+
+def spread_out(size, groups, c, y, k, ydev, kdev, outs, extra):
+    rows_all, sums, got, row_sems, k_sem, y_sem, f_sems, z_sems, out_sem = extra[:9]
+    f = lax.axis_index("fsdp")
+
+    def copy(src, dst, sems, dev):
+        return pltpu.make_async_remote_copy(
+            src_ref=src,
+            dst_ref=dst,
+            send_sem=sems.at[0],
+            recv_sem=sems.at[1],
+            device_id=dev,
+            device_id_type=MESH,
+        )
+
+    def row_copy(yy, kk, n, dev):
+        slot = rows_all.at[yy * 2 + kk]
+        return copy(slot, slot, row_sems.at[n], dev)
+
+    to_y, to_k, on_k = row_copy(y, k, 0, ydev), row_copy(y, k, 1, kdev), row_copy(1 - y, k, 2, kdev)
+    to_y.start()
+    to_k.start()
+
+    def add(n, first, count):
+        value = sums[n]
+        for i in range(first, first + count):
+            value = value + got[i]
+        sums[n + 1] = value
+
+    swap_k = copy(sums.at[0], got.at[0], k_sem, kdev)
+    swap_k.start()
+    swap_k.wait()
+    add(0, 0, 1)
+    swap_y = copy(sums.at[1], got.at[1], y_sem, ydev)
+    swap_y.start()
+    swap_y.wait()
+    add(1, 1, 1)
+    swaps = [
+        copy(sums.at[2], got.at[1 + g], f_sems.at[g - 1], {"fsdp": (f + g) % groups})
+        for g in range(1, groups)
+    ]
+    for one in swaps:
+        one.start()
+    for one in swaps:
+        one.wait()
+    add(2, 2, groups - 1)
+    swaps = [
+        copy(sums.at[3], got.at[groups + s], z_sems.at[s - 1], {"ctx": (c + s) % size})
+        for s in range(1, size)
+    ]
+    for one in swaps:
+        one.start()
+    row_copy(1 - y, k, 0, ydev).wait_recv()
+    on_k.start()
+    for one in swaps:
+        one.wait()
+    add(3, groups + 1, size - 1)
+    outs[1][...] = sums[4]
+    row_copy(y, 1 - k, 1, kdev).wait_recv()
+    row_copy(1 - y, 1 - k, 2, kdev).wait_recv()
+    to_y.wait_send()
+    to_k.wait_send()
+    on_k.wait_send()
+    out = pltpu.make_async_copy(rows_all, outs[0], out_sem)
+    out.start()
+    out.wait()
+
+
+def reduce_call(a, w, ins, out_shapes, final, cid, size, last=False, sent=(), plan=None):
     width = w.shape[1]
     part = a.shape[0] // (size * 4)
     vmem = pl.BlockSpec(memory_space=pltpu.VMEM)
     low, full = jnp.bfloat16, jnp.float32
+    groups = lax.axis_size("fsdp")
+    any_spec = pl.BlockSpec(memory_space=pl.ANY)
+    dma = pltpu.SemaphoreType.DMA
+    out_specs, extra = [vmem] * len(out_shapes), []
+    if sent:
+        extra = [dma((len(sent), size - 1, 2)), dma((len(sent), max(groups - 1, 1), size, 2))]
+    if last:
+        out_specs[0] = out_specs[2] = any_spec
+        extra = [
+            pltpu.VMEM((4, part, width), low),
+            pltpu.VMEM((5, 8, width), full),
+            pltpu.VMEM((groups + size, 8, width), full),
+            dma((3, 2)),
+            dma((2,)),
+            dma((2,)),
+            dma((max(groups - 1, 1), 2)),
+            dma((size - 1, 2)),
+            dma,
+            pltpu.VMEM((max(groups - 1, 1), *out_shapes[2].shape), low),
+            pltpu.VMEM(out_shapes[2].shape, low),
+            pltpu.VMEM(out_shapes[2].shape, low),
+            dma((max(groups - 1, 1), size, 2)),
+            dma((size, 2)),
+            dma((size + 1,)),
+        ]
     return pl.pallas_call(
-        functools.partial(reduce_kernel, size, part, len(ins), len(out_shapes), final),
-        out_shape=tuple(out_shapes),
-        in_specs=[vmem] * (2 + len(ins)),
-        out_specs=tuple([vmem] * len(out_shapes)),
+        functools.partial(
+            reduce_kernel,
+            size,
+            groups,
+            last,
+            plan or {},
+            len(sent),
+            part,
+            len(ins),
+            len(out_shapes),
+            final,
+        ),
+        out_shape=(
+            *out_shapes,
+            *(
+                jax.ShapeDtypeStruct((groups * size, *one.shape[1:]), one.dtype)
+                for one in sent
+            ),
+        ),
+        in_specs=[vmem] * (1 + len(ins))
+        + [any_spec if last else vmem]
+        + [any_spec] * len(sent),
+        out_specs=(*out_specs, *([any_spec] * len(sent))),
         scratch_shapes=[
             pltpu.VMEM((2, part, width), full),
             pltpu.VMEM((size * 2, part, width), low),
@@ -418,15 +788,17 @@
             pltpu.VMEM((size, part, width), low),
             pltpu.VMEM((2, size, part, width), low),
             pltpu.VMEM((part, width), full),
+            pltpu.VMEM((2 * part, 512), full),
             pltpu.SemaphoreType.DMA((size * 2, 2)),
             pltpu.SemaphoreType.DMA((size, SUBS, 2)),
             pltpu.SemaphoreType.DMA((2, size, SUBS, 2)),
+            *extra,
         ],
         compiler_params=pltpu.CompilerParams(
             collective_id=cid, has_side_effects=True, vmem_limit_bytes=VLIM
         ),
-        name=name,
-    )(a, w, *ins)
+        cost_estimate=cost(85),
+    )(a, w, *ins, *sent)
 
 
 def doc_positions(segment_row):
@@ -476,8 +848,13 @@
     return lax.dot_general(left, right, (((0,), (0,)), ((), ())), preferred_element_type=jnp.float32)
 
 
-def qkv_kernel(heads, x_ref, w_ref, cos_ref, sin_ref, out_ref):
-    proj = nt(x_ref[...], w_ref[...])
+def qkv_kernel(heads, x_ref, w_ref, gain_ref, cos_ref, sin_ref, out_ref, normed_ref):
+    for i in range(BLK // 16):
+        at = slice(i * 16, (i + 1) * 16)
+        x = x_ref[at, :].astype(jnp.float32)
+        scale = lax.rsqrt(jnp.mean(x * x, axis=1, keepdims=True) + EPSILON)
+        normed_ref[at, :] = (x * scale * gain_ref[...]).astype(jnp.bfloat16)
+    proj = nt(normed_ref[...], w_ref[...])
     for i in range(3 * heads):
         cut = slice(i * LANES, (i + 1) * LANES)
         one = proj[:, cut]
@@ -486,22 +863,31 @@
         out_ref[:, cut] = one.astype(jnp.bfloat16)
 
 
-def qkv_call(x, w, cosine, sine, heads):
+def qkv_call(x, w, gain, cosine, sine, heads):
     rows, width = x.shape
+    tall = 3 * heads * LANES
     return pl.pallas_call(
         functools.partial(qkv_kernel, heads),
-        out_shape=jax.ShapeDtypeStruct((rows, w.shape[0]), jnp.bfloat16),
+        out_shape=(
+            jax.ShapeDtypeStruct((rows, tall), jnp.bfloat16),
+            jax.ShapeDtypeStruct((rows, width), jnp.bfloat16),
+        ),
         grid=(rows // BLK,),
         in_specs=[
             pl.BlockSpec((BLK, width), lambda i: (i, 0)),
-            pl.BlockSpec(w.shape, lambda i: (0, 0)),
+            pl.BlockSpec((tall, width), lambda i: (0, 0)),
+            pl.BlockSpec((1, width), lambda i: (0, 0)),
             pl.BlockSpec((BLK, LANES), lambda i: (i, 0)),
             pl.BlockSpec((BLK, LANES), lambda i: (i, 0)),
         ],
-        out_specs=pl.BlockSpec((BLK, w.shape[0]), lambda i: (i, 0)),
+        out_specs=(
+            pl.BlockSpec((BLK, tall), lambda i: (i, 0)),
+            pl.BlockSpec((BLK, width), lambda i: (i, 0)),
+        ),
         compiler_params=pltpu.CompilerParams(vmem_limit_bytes=VLIM),
+        cost_estimate=cost(18),
         name="qkv",
-    )(x, w, cosine, sine)
+    )(x, w, gain, cosine, sine)
 
 
 def block(ref, i, head):
@@ -565,6 +951,7 @@
         in_specs=[pl.BlockSpec(memory_space=pltpu.SMEM), vmem, vmem, vmem],
         out_specs=(vmem, vmem),
         compiler_params=pltpu.CompilerParams(vmem_limit_bytes=VLIM),
+        cost_estimate=cost(20),
         name="attend",
     )(low, qkv, seg[:, None], seg[None, :])
 
@@ -659,94 +1046,97 @@
             pltpu.VMEM((rows, heads * LANES), jnp.float32),
         ],
         compiler_params=pltpu.CompilerParams(vmem_limit_bytes=VLIM),
+        cost_estimate=cost(32),
         name="attend_back",
     )(high, qkv, out, grad, lse, seg[:, None], seg[None, :], cosine, sine)
 
 
-def cross(weight):
-    size, groups = lax.axis_size("ctx"), lax.axis_size("fsdp")
+def join_kernel(cuts, groups, size, d, *refs):
+    *pieces, out, sems = refs
     c, f = lax.axis_index("ctx"), lax.axis_index("fsdp")
-    n = weight.shape[1] // size
-    pieces = []
-    for s in range(size):
-        piece = lax.dynamic_slice_in_dim(weight, ((c + s) % size) * n, n, 1)
-        if s:
-            piece = lax.ppermute(piece, "ctx", [(i, (i + s) % size) for i in range(size)])
-        pieces.append((piece, f * size + (c - s) % size))
-    for g in range(1, groups):
-        for s in range(size):
-            piece = lax.ppermute(
-                pieces[s][0], "fsdp", [(i, (i + g) % groups) for i in range(groups)]
-            )
-            pieces.append((piece, ((f - g) % groups) * size + (c - s) % size))
-    return pieces
-
-
-def join_kernel(count, cuts, groups, size, *refs):
-    pieces, out, sems = refs[:count], refs[count], refs[count + 1]
-    c, f = lax.axis_index("ctx"), lax.axis_index("fsdp")
-    m, n, d = pieces[0].shape
-    tall = out.shape[0] // m
 
     def copies(go):
-        for i in range(count):
+        for i in range(groups * size):
             g, s = i // size, i % size
             place = ((f + groups - g) % groups) * size + (c + size - s) % size
             lanes = pl.ds(pl.multiple_of(place * d, d), d)
-            for j in range(m):
-                for q, (src, dst, rows) in enumerate(cuts):
-                    go(
-                        pltpu.make_async_copy(
-                            pieces[i].at[j, pl.ds(src, rows)],
-                            out.at[pl.ds(j * tall + dst, rows), lanes],
-                            sems.at[i, j * len(cuts) + q],
-                        )
+            for q, (src, dst, rows) in enumerate(cuts):
+                if len(pieces) > 2:
+                    piece = pieces[i]
+                else:
+                    piece = pieces[1].at[place] if i else pieces[0].at[c]
+                go(
+                    pltpu.make_async_copy(
+                        piece.at[pl.ds(src, rows)], out.at[pl.ds(dst, rows), lanes], sems.at[i, q]
                     )
+                )
 
     copies(lambda one: one.start())
-    for j in range(m):
-        for k, (_, dst, rows) in enumerate(cuts):
-            stop = cuts[k + 1][1] if k + 1 < len(cuts) else tall
-            if dst + rows < stop:
-                gap = stop - dst - rows
-                out[pl.ds(j * tall + dst + rows, gap), :] = jnp.zeros(
-                    (gap, out.shape[1]), out.dtype
-                )
+    for q, (_, dst, rows) in enumerate(cuts):
+        stop = cuts[q + 1][1] if q + 1 < len(cuts) else out.shape[0]
+        if dst + rows < stop:
+            gap = stop - dst - rows
+            out[pl.ds(dst + rows, gap), :] = jnp.zeros((gap, out.shape[1]), out.dtype)
     copies(lambda one: one.wait())
 
 
-def join(pieces, spaced, name):
-    m, n, d = pieces[0][0].shape
-    width = len(pieces) * d
+def join(sent, pieces, spaced, tail=0):
+    size, groups = lax.axis_size("ctx"), lax.axis_size("fsdp")
+    c, f = lax.axis_index("ctx"), lax.axis_index("fsdp")
+    count, (n, d) = size * groups, sent.shape[1:]
+    n = n - tail
+    width = count * d
     if d % LANES:
-        buf = jnp.zeros((len(pieces), m, n, d), pieces[0][0].dtype)
-        for piece, place in pieces:
-            buf = lax.dynamic_update_slice(buf, piece[None], (place, 0, 0, 0))
-        flat = buf.transpose(1, 2, 0, 3).reshape(m, n, width)
-        flat = spread(flat, 1) if spaced else flat
-        return flat.reshape(-1, width)
+        own = lax.dynamic_slice_in_dim(sent, c, 1, 0)
+        if isinstance(pieces, list):
+            buf = jnp.zeros((count, n + tail, d), sent.dtype)
+            for i, one in enumerate(pieces):
+                g, s = i // size, i % size
+                place = ((f + groups - g) % groups) * size + (c + size - s) % size
+                buf = lax.dynamic_update_slice(buf, one[None], (place, 0, 0))
+        else:
+            buf = lax.dynamic_update_slice(pieces, own, (f * size + c, 0, 0))
+        flat = buf.transpose(1, 0, 2).reshape(n + tail, width)
+        return jnp.concatenate([spread(flat[:n], 0), flat[n:]]) if spaced else flat
     cuts = [(0, 0, n)]
     if spaced:
         cuts = [(i * HALF, i * LANES // 2, HALF) for i in range(n // HALF)]
     tall = n * LANES // HD if spaced else n
+    if tail:
+        cuts.append((n, tall, tail))
+        tall += tail
+    refs = pieces if isinstance(pieces, list) else [sent, pieces]
     return pl.pallas_call(
-        functools.partial(
-            join_kernel,
-            len(pieces),
-            cuts,
-            lax.axis_size("fsdp"),
-            lax.axis_size("ctx"),
-        ),
-        out_shape=jax.ShapeDtypeStruct((m * tall, width), pieces[0][0].dtype),
-        in_specs=[pl.BlockSpec(memory_space=pl.ANY)] * len(pieces),
+        functools.partial(join_kernel, cuts, groups, size, d),
+        out_shape=jax.ShapeDtypeStruct((tall, width), sent.dtype),
+        in_specs=[pl.BlockSpec(memory_space=pl.ANY)] * len(refs),
         out_specs=pl.BlockSpec(memory_space=pltpu.VMEM),
-        scratch_shapes=[pltpu.SemaphoreType.DMA((len(pieces), m * len(cuts)))],
+        scratch_shapes=[pltpu.SemaphoreType.DMA((count, len(cuts)))],
         compiler_params=pltpu.CompilerParams(vmem_limit_bytes=VLIM),
-        name=name,
-    )(*[piece for piece, _ in pieces])
-
-
-def hand_out(grad):
+        cost_estimate=cost(4),
+    )(*refs)
+
+
+def cross(sent):
+    size, groups = lax.axis_size("ctx"), lax.axis_size("fsdp")
+    c = lax.axis_index("ctx")
+    pieces = []
+    for s in range(size):
+        piece = lax.dynamic_index_in_dim(sent, (c + s) % size, 0, False)
+        if s:
+            piece = lax.ppermute(piece, "ctx", [(i, (i + s) % size) for i in range(size)])
+        pieces.append(piece)
+    for g in range(1, groups):
+        for s in range(size):
+            pieces.append(
+                lax.ppermute(
+                    pieces[s], "fsdp", [(i, (i + g) % groups) for i in range(groups)]
+                )
+            )
+    return pieces
+
+
+def hand_out(grad, beside=None):
     size, groups = lax.axis_size("ctx"), lax.axis_size("fsdp")
     c, f = lax.axis_index("ctx"), lax.axis_index("fsdp")
     rows = grad.shape[0] // groups
@@ -754,18 +1144,18 @@
     total = lax.dynamic_slice_in_dim(grad, f * rows, rows, 0)
     for g in range(1, groups):
         sent = lax.dynamic_slice_in_dim(grad, ((f + g) % groups) * rows, rows, 0)
-        got = lax.ppermute(
-            sent.astype(jnp.bfloat16), "fsdp", [(i, (i + g) % groups) for i in range(groups)]
-        )
+        got = lax.ppermute(sent, "fsdp", [(i, (i + g) % groups) for i in range(groups)])
         total = total.astype(jnp.float32) + got.astype(jnp.float32)
     total = total.astype(jnp.bfloat16)
+    if beside is not None:
+        total, beside = lax.optimization_barrier((total, beside))
     out = jnp.zeros((size, d, grad.shape[1]), jnp.bfloat16)
     for s in range(size):
         piece = lax.dynamic_slice_in_dim(total, ((c + s) % size) * d, d, 0)
         if s:
             piece = lax.ppermute(piece, "ctx", [(i, (i + s) % size) for i in range(size)])
         out = lax.dynamic_update_slice(out, piece[None], ((c - s) % size, 0, 0))
-    return out.astype(jnp.float32)
+    return out if beside is None else (out, beside)
 
 
 def wide_gather(part):
@@ -774,7 +1164,7 @@
 
 
 def mlp_block(half, pair, buf, ins, outs):
-    w, g_act = ins
+    w, wd, cot = ins
     act, g_gate, g_up = outs
     rows = buf.shape[1]
     tile = 256
@@ -784,7 +1174,7 @@
         lanes = pl.ds(pl.multiple_of(i * tile, tile), tile)
         gate = nt(buf[pair], w[lanes, :])
         up = nt(buf[pair], w[pl.ds(pl.multiple_of(half + i * tile, tile), tile), :])
-        grad = g_act[at, lanes]
+        grad = nt(cot[at, :], wd[lanes, :])
         sigma = 1.0 / (1.0 + jnp.exp(-gate))
         silu = gate * sigma
         act[at, lanes] = (silu * up).astype(jnp.bfloat16)
@@ -805,7 +1195,11 @@
     pass
 
 
-def after_out(total, sweep, ins, outs):
+def nothing():
+    pass
+
+
+def after_out(total, ins, outs, extra):
     tokens, gain = ins
     hidden, normed = outs
 
@@ -815,7 +1209,7 @@
         hidden[r, :] = value
         normed[r, :] = (value * scale * gain[...]).astype(jnp.bfloat16)
 
-    sweep(one)
+    return nothing, one, nothing
 
 
 def norm_back(grad, value, gain, top):
@@ -826,10 +1220,12 @@
     return top + scale * (g_unit - unit * inner), grad * unit
 
 
-def after_mlp(total, sweep, ins, outs):
+def after_mlp(total, ins, outs, extra):
     hidden, cot, gain = ins
     g_hidden, g_branch, g_gain = outs
-    g_gain[...] = jnp.zeros_like(g_gain)
+
+    def begin():
+        g_gain[...] = jnp.zeros_like(g_gain)
 
     def one(r):
         grad, part = norm_back(
@@ -839,22 +1235,49 @@
         g_branch[r, :] = grad.astype(jnp.bfloat16)
         g_gain[...] += part
 
-    sweep(one)
-
-
-def after_qkv(total, sweep, ins, outs):
-    tokens, g_hidden, gain = ins
-    g_tokens, g_gain = outs
-    g_gain[...] = jnp.zeros_like(g_gain)
+    return begin, one, nothing
+
+
+def after_qkv(total, ins, outs, extra):
+    tokens, g_hidden, gain, g_gain_mlp, _ = ins
+    rows_all, sums = extra[:2]
+    place = lax.axis_index("tp")
+
+    def begin():
+        sums[4] = jnp.zeros(sums.shape[1:], jnp.float32)
 
     def one(r):
         grad, part = norm_back(
             total[r, :], tokens[r, :].astype(jnp.float32), gain[...], g_hidden[r, :]
         )
-        g_tokens[r, :] = grad.astype(jnp.bfloat16)
-        g_gain[...] += part
-
-    sweep(one)
+        rows_all[place, r, :] = grad.astype(jnp.bfloat16)
+        sums[4] += part[0:8] + part[8:16]
+
+    def end():
+        sums[0] = jnp.concatenate(
+            [
+                jnp.sum(sums[4], axis=0, keepdims=True),
+                jnp.sum(g_gain_mlp[...], axis=0, keepdims=True),
+                jnp.zeros((6, total.shape[1]), jnp.float32),
+            ],
+            axis=0,
+        )
+
+    return begin, one, end
+
+
+PLAN = {
+    -1: [("z", 0, 1), ("z", 0, 2), ("z", 0, 3), ("x", 0, 0), ("x", 1, 0)],
+    0: [("z", 1, 1), ("z", 1, 2), ("z", 1, 3), ("x", 0, 1)],
+    1: [("x", 0, 2), ("x", 0, 3), ("x", 1, 1)],
+    2: [("x", 1, 2), ("x", 1, 3)],
+}
+PLAN_OUT = {
+    -1: [("z", 0, 1), ("z", 0, 2), ("z", 0, 3), ("x", 0, 0)],
+    1: [("x", 0, 1)],
+    2: [("x", 0, 2)],
+    3: [("x", 0, 3)],
+}
 
 
 def shards(tokens, segments, w_qkv, w_out, w_gate_up, w_down, norm_attn, norm_mlp, cotangent):
@@ -872,23 +1295,29 @@
     tokens_own = lax.dynamic_slice_in_dim(tokens[0], begin, part, 0)
     cot_own = lax.dynamic_slice_in_dim(cotangent[0], begin, part, 0)
 
-    pieces_q = cross(w_qkv.transpose(0, 2, 1))
-    gains = lax.all_gather(
-        jnp.stack([norm_attn, norm_mlp]), ("fsdp", "ctx"), axis=1, tiled=True
-    ).astype(full)
+    d = w_qkv.shape[1]
+    gain_rows = jnp.concatenate(
+        [norm_attn[None], norm_mlp[None], jnp.zeros((GAIN_ROWS - 2, d), low)], axis=0
+    )
+    sent_q = w_qkv.transpose(0, 2, 1).reshape(3, size, -1, d).transpose(1, 0, 2, 3)
+    sent_q = jnp.concatenate(
+        [sent_q.reshape(size, -1, d), jnp.broadcast_to(gain_rows, (size, GAIN_ROWS, d))], axis=1
+    )
+    sent_o = w_out.reshape(size, -1, d)
+    sent_g = w_gate_up.transpose(0, 2, 1).reshape(2, size, -1, d).transpose(1, 0, 2, 3)
+    sent_g = sent_g.reshape(size, -1, d)
+    sent_d = w_down.reshape(size, -1, d)
+    tokens_full, moved_q, moved_o = gather_call(
+        tokens_own, [], [], no_block, 1, size, [sent_q, sent_o], PLAN
+    )
+    wq = join(sent_q, moved_q, True, GAIN_ROWS)
+    wo = join(sent_o, moved_o, True)
+    wg = join(sent_g, cross(sent_g), False)
+    half = sent_d.shape[1]
+    tall = 3 * heads * LANES
+    gains = wq[tall : tall + 2].astype(full)
     gain_attn, gain_mlp = gains[0:1], gains[1:2]
-    resid = tokens_own.astype(full)
-    scale_one = lax.rsqrt(jnp.mean(resid * resid, axis=1, keepdims=True) + EPSILON)
-    normed1_own = (resid * scale_one * gain_attn).astype(low)
-
-    w_out, w_gate_up, w_down, cot_gate, _ = lax.optimization_barrier(
-        (w_out, w_gate_up, w_down, cot_own, [p for p, _ in pieces_q[:size]])
-    )
-    wq = join(pieces_q, True, "join_qkv")
-    wo = join(cross(w_out[None]), True, "join_out")
-    wd = join(cross(w_down[None]), False, "join_down")
-    wg = join(cross(w_gate_up.transpose(0, 2, 1)), False, "join_gate_up")
-    half = wg.shape[0] // 2
+    cot_gate, tokens_full = lax.optimization_barrier((cot_own, tokens_full))
     cot_full = wide_gather(cot_gate)
 
     positions = doc_positions(seg)
@@ -897,50 +1326,49 @@
     marks = jnp.arange(length // BLK, dtype=jnp.int32)
     ends = jnp.sum((starts[None, :] <= marks[:, None]).astype(jnp.int32), axis=1) - 1
 
-    normed1 = gather_call(normed1_own, [], [], no_block, "gather_normed1", 1, size)[0]
-    qkv = qkv_call(normed1, wq, cosine, sine, heads)
+    qkv, normed1 = qkv_call(tokens_full, wq, gain_attn, cosine, sine, heads)
     attn, lse = attend_call(qkv, seg, starts, heads, scale)
 
     row_shape = jax.ShapeDtypeStruct((part, width), full)
     row_low = jax.ShapeDtypeStruct((part, width), low)
     gain_shape = jax.ShapeDtypeStruct((16, width), full)
-    hidden1, normed2_own = reduce_call(
-        attn, wo, [tokens_own, gain_mlp], [row_shape, row_low], after_out, "reduce_out", 2, size
+    hidden1, normed2_own, moved_d = reduce_call(
+        attn,
+        wo,
+        [tokens_own, gain_mlp],
+        [row_shape, row_low],
+        after_out,
+        2,
+        size,
+        sent=[sent_d],
+        plan=PLAN_OUT,
     )
-    g_act = nt(cot_full, wd)
+    wd = join(sent_d, moved_d, False)
     half_shape = jax.ShapeDtypeStruct((length, half), low)
     normed2, act, g_gate, g_up = gather_call(
         normed2_own,
-        [wg, g_act],
+        [wg, wd, cot_full],
         [half_shape] * 3,
         functools.partial(mlp_block, half),
-        "gather_mlp",
         3,
         size,
     )
     g_gu = jnp.concatenate([g_gate, g_up], axis=1)
+    down_part = nn(act, wd).astype(low)
+    down = lax.psum_scatter(down_part, GROUP, scatter_dimension=0, tiled=True)
+    output = (hidden1 + down.astype(full)).astype(low)
+    output = lax.all_gather(output, "tp", axis=0, tiled=True)[None]
+
     part_down, part_gu = tn(cot_full, act).astype(low), tn(normed2, g_gu).astype(low)
     g_gu, part_down, part_gu = lax.optimization_barrier((g_gu, part_down, part_gu))
     g_hidden1, g_branch_own, g_gain_mlp = reduce_call(
-        g_gu,
-        wg,
-        [hidden1, cot_own, gain_mlp],
-        [row_shape, row_low, gain_shape],
-        after_mlp,
-        "reduce_mlp",
-        4,
-        size,
+        g_gu, wg, [hidden1, cot_own, gain_mlp], [row_shape, row_low, gain_shape], after_mlp, 4, size
     )
-    down = lax.psum_scatter(nn(act, wd).astype(low), GROUP, scatter_dimension=0, tiled=True)
-    output = (hidden1 + down.astype(full)).astype(low)
-    output = lax.all_gather(output, "tp", axis=0, tiled=True)[None]
-
     g_branch, g_attn = gather_call(
         g_branch_own,
         [wo],
         [jax.ShapeDtypeStruct((length, heads * LANES), low)],
         attn_block,
-        "gather_branch",
         5,
         size,
     )
@@ -952,29 +1380,31 @@
     out_out = hand_out(part_out)
     part_qkv = unspread(tn(normed1, g_proj), 1).astype(low)
     g_proj, part_qkv = lax.optimization_barrier((g_proj, part_qkv))
-    out_qkv = hand_out(part_qkv)
-    g_tokens, g_gain_attn = reduce_call(
+    g_tokens, gain_sums, out_qkv = reduce_call(
         g_proj,
         wq,
-        [tokens_own, g_hidden1, gain_attn],
-        [row_low, gain_shape],
+        [tokens_own, g_hidden1, gain_attn, g_gain_mlp, part_qkv],
+        [
+            jax.ShapeDtypeStruct((tp_size, part, width), low),
+            jax.ShapeDtypeStruct((8, width), full),
+            jax.ShapeDtypeStruct((size, d, part_qkv.shape[1]), low),
+        ],
         after_qkv,
-        "reduce_qkv",
         6,
         size,
+        True,
     )
-    g_tokens = lax.all_gather(g_tokens, "tp", axis=0, tiled=True)[None]
-
-    d = w_qkv.shape[1]
-    grad_qkv = out_qkv.reshape(size, d, 3, -1).transpose(2, 1, 0, 3).reshape(3, d, -1)
-    grad_gu = out_gu.reshape(size, d, 2, -1).transpose(2, 1, 0, 3).reshape(2, d, -1)
-    grad_out = out_out.transpose(0, 2, 1).reshape(-1, d)
-    grad_down = out_down.transpose(0, 2, 1).reshape(-1, d)
-
-    gain_sums = lax.psum(
-        jnp.stack([jnp.sum(g_gain_attn, axis=0), jnp.sum(g_gain_mlp, axis=0)]),
-        ("fsdp", "ctx", "tp"),
-    )
+    g_tokens = g_tokens.reshape(1, rows, width)
+
+    def natural(grad, count):
+        wide = grad.astype(full).reshape(size, d, count, -1).transpose(2, 1, 0, 3)
+        return wide.reshape(count, d, -1)
+
+    grad_gu = natural(out_gu, 2)
+    grad_out = out_out.astype(full).transpose(0, 2, 1).reshape(-1, d)
+    grad_down = out_down.astype(full).transpose(0, 2, 1).reshape(-1, d)
+    grad_qkv = natural(out_qkv, 3)
+
     mine = lax.axis_index("fsdp") * size + lax.axis_index("ctx")
     gain_grads = lax.dynamic_slice_in_dim(gain_sums, mine * d, d, 1)
     return (

time: 1380 us -> 1160 us (0.84)
  the two profiles are of different devices: /device:TPU:0 before, /device:TPU:15 now
where the time goes in v2:
time: 1160 us; the launch traced here: 1150 us
  Pallas kernels  738 us (64%)
  waiting for transfers between devices  206 us (18%)
  local copies, waits for them, and re-layouts  83.9 us (7%)
  matrix products  61.5 us (5%)
  other arithmetic  25.3 us (2%)
  starting transfers between devices  22.3 us (2%)
  between operations  14.8 us (1%)
    pallas_call x3, Pallas kernels, reduce_call(): pl.pallas_call(functools.partial(reduce_kernel, size, groups, last, plan...  365 us
    pallas_call x3, Pallas kernels, gather_call(): pl.pallas_call(functools.partial(gather_kernel, size, groups, plan or {},...  283 us
    ppermute x3, waiting for transfers between devices, cross(): lax.ppermute(piece, 'ctx', [(i, (i + s) % size) for i in range(size)])  109 us
    ppermute x9, waiting for transfers between devices, hand_out(): lax.ppermute(piece, 'ctx', [(i, (i + s) % size) for i in range(size)])  97.4 us
    dot_general x4, matrix products, tn(): lax.dot_general(left, right, (((0,), (0,)), ((), ())), preferred_element_...  49.8 us
    pallas_call x1, Pallas kernels, attend_back_call(): pl.pallas_call(functools.partial(attend_back_kernel, heads, scale), out_s...  33.1 us
    unnamed x48, local copies, waits for them, and re-layouts  24.3 us
  transfers between devices with their start and end apart: 22, of which 5 were waited for; matrix products, arithmetic and copies ran while one was open for 12% of the time, Pallas kernels for 46%

profile of v2, /device:TPU:15, one launch (start us, length us, event | category | flops | bytes accessed | tf_op | source)
XLA Modules:
  0.0 1151.5 jit_solution(15861942905397701246)
XLA Ops:
  7.2 2.8 copy.54
  10.2 2.1 dynamic-slice_bitcast_fusion.5.refs_0_.refs_2_
  12.3 2.1 dynamic-slice_bitcast_fusion.6.refs_3_
  14.6 1.4 pad_maximum_fusion.refs_1_.refs_0_
  16.0 117.2 %shard_map.152 = (bf16[2048,3072]{1,0:T(8,128)(2,1)}, bf16[8,592,384]{2,1,0:T(8,128)(2,1)}, bf16[8,192,384]{2,1,0:T(8,128)(2,1)}) custom-call(bf16[128,3072]{1,0:T(8,128)(2,1)} %dynamic-slice_bitcast_fusion.5.refs_0_.refs_2_, bf16[4,592,384]{2,1,0:T(8,128)(2,1)} %pad_maximum_fusion.refs_1_.refs_0_, bf16[4,192,384]{2,1,0:T(8,128)(2,1)} %bitcast.107), custom_call_target="tpu_custom_call" | custom-call | bytes 225000000 | tf_op jit(solution)/shard_map/pallas_call | solution.py:366
  133.3 6.2 reshape.127
  139.4 5.2 copy.57
  144.7 1.8 dynamic-slice_bitcast_fusion.1
  147.7 1.3 collective-permute-start.2
  149.0 1.3 collective-permute-start.3
  151.7 3.7 fusion.2
  155.5 2.5 pad_maximum_fusion.1
  157.9 5.2 shard_map.153.w_ref.refs_1_
  163.1 1.3 slice.45
  164.4 2.0 copy.56.col_ref
  166.4 2.7 shard_map.154.refs_1_
  169.9 38.4 %collective-permute-done.refs_1_ = bf16[1024,384]{1,0:T(8,128)(2,1)} collective-permute-done((bf16[1024,384]{1,0:T(8,128)(2,1)}, bf16[1024,384]{1,0:T(8,128)(2,1)}, u32[]{:S(2)}, u32[]{:S(2)}) %collective-permute-start) | collective-permute-done | bytes 786464 | tf_op jit(solution)/shard_map/ppermute | solution.py:1127
  208.3 70.3 %collective-permute-done.1.refs_2_ = bf16[1024,384]{1,0:T(8,128)(2,1)} collective-permute-done((bf16[1024,384]{1,0:T(8,128)(2,1)}, bf16[1024,384]{1,0:T(8,128)(2,1)}, u32[]{:S(2)}, u32[]{:S(2)}) %collective-permute-start.1) | collective-permute-done | bytes 786464 | tf_op jit(solution)/shard_map/ppermute | solution.py:1127
  278.8 1.3 collective-permute-start.6
  280.7 18.8 %qkv.1 = (bf16[2048,768]{1,0:T(8,128)(2,1)}, bf16[2048,3072]{1,0:T(8,128)(2,1)}) custom-call(bf16[2048,3072]{1,0:T(8,128)(2,1)} %get-tuple-element.40.x_ref, bf16[784,3072]{1,0:T(8,128)(2,1)} %shard_map.153.w_ref.refs_1_, f32[1,3072]{1,0:T(1,128)} %get-tuple-element.113.gain_ref.refs_4_, f32[2048,128]{1,0:T(8,128)} %get-tuple-element.108.cos_ref, ...), custom_call_target="tpu_custom_call" | custom-call | bytes 54000000 | tf_op jit(solution)/shard_map/qkv/pallas_call | solution.py:869
  300.7 20.8 %attend.1 = (bf16[2048,256]{1,0:T(8,128)(2,1)}, f32[2,2048]{1,0:T(2,128)}) custom-call(s32[8]{0:T(128)} %and_select_fusion.low_ref, bf16[2048,768]{1,0:T(8,128)(2,1)} %get-tuple-element.42.qkv_ref, s32[2048,1]{1,0:T(8,128)} %copy.56.col_ref, s32[1,2048]{1,0:T(1,128)} %row_ref.3), custom_call_target="tpu_custom_call" | custom-call | bytes 60000000 | tf_op jit(solution)/shard_map/attend/pallas_call | solution.py:945
  321.5 89.7 %shard_map.155 = (f32[128,3072]{1,0:T(8,128)}, bf16[128,3072]{1,0:T(8,128)(2,1)}, bf16[8,512,384]{2,1,0:T(8,128)(2,1)}) custom-call(bf16[2048,256]{1,0:T(8,128)(2,1)} %get-tuple-element.43.refs_0_.out_ref, bf16[256,3072]{1,0:T(8,128)(2,1)} %shard_map.154.refs_1_, bf16[128,3072]{1,0:T(8,128)(2,1)} %dynamic-slice_bitcast_fusion.5.refs_0_.refs_2_, ...), custom_call_target="tpu_custom_call" | custom-call | bytes 255000000 | tf_op jit(solution)/shard_map/pallas_call | solution.py:757
  411.2 3.6 shard_map.157.refs_2_
  414.9 5.6 shard_map.156.refs_1_
  420.5 85.0 %shard_map.158 = (bf16[2048,3072]{1,0:T(8,128)(2,1)}, bf16[2048,512]{1,0:T(8,128)(2,1)}, bf16[2048,512]{1,0:T(8,128)(2,1)}, bf16[2048,512]{1,0:T(8,128)(2,1)}) custom-call(bf16[128,3072]{1,0:T(8,128)(2,1)} %get-tuple-element.46.refs_0_, bf16[1024,3072]{1,0:T(8,128)(2,1)} %shard_map.156.refs_1_, bf16[512,3072]{1,0:T(8,128)(2,1)} %shard_map.157.refs_2_, ...), custom_call_target="tpu_custom_call" | custom-call | bytes 225000000 | tf_op jit(solution)/shard_map/pallas_call | solution.py:366
  505.5 11.7 %convolution_convert_fusion = bf16[2048,3072]{1,0:T(8,128)(2,1)} fusion(bf16[2048,512]{1,0:T(8,128)(2,1)} %get-tuple-element.49, bf16[512,3072]{1,0:T(8,128)(2,1)} %shard_map.157.refs_2_), kind=kOutput, calls=%fused_computation | convolution fusion | flops 6448742400 | bytes 17825792 | tf_op jit(solution)/shard_map/dot_general | solution.py:844
  518.5 1.9 constant_dynamic-update-slice_fusion.6
  522.0 12.6 %convolution_convert_fusion.3 = bf16[3072,512]{1,0:T(8,128)(2,1)} fusion(bf16[2048,3072]{1,0:T(8,128)(2,1)} %all-gather.3.cloned.1.call-done.refs_3_, bf16[2048,512]{1,0:T(8,128)(2,1)S(1)} %copy-done.15), kind=kOutput, calls=%fused_computation.5 | convolution fusion | flops 6444023808 | bytes 17825792 | tf_op jit(solution)/shard_map/dot_general | solution.py:848
  534.6 15.7 %convolution_convert_fusion.1 = bf16[3072,1024]{1,0:T(8,128)(2,1)} fusion(bf16[2048,3072]{1,0:T(8,128)(2,1)S(1)} %bitcast.113, bf16[2048,1024]{1,0:T(8,128)(2,1)S(1)} %constant_dynamic-update-slice_fusion.5.refs_0_), kind=kOutput, calls=%fused_computation.3 | convolution fusion | flops 12888047616 | bytes 23068672 | tf_op jit(solution)/shard_map/dot_general | solution.py:848
  550.4 113.5 %shard_map.159 = (f32[128,3072]{1,0:T(8,128)}, bf16[128,3072]{1,0:T(8,128)(2,1)}, f32[16,3072]{1,0:T(8,128)}) custom-call(bf16[2048,1024]{1,0:T(8,128)(2,1)} %copy-done.1, bf16[1024,3072]{1,0:T(8,128)(2,1)} %shard_map.156.refs_1_, f32[128,3072]{1,0:T(8,128)} %get-tuple-element.45.refs_2_, bf16[128,3072]{1,0:T(8,128)(2,1)} %dynamic-slice_bitcast_fusion.6.refs_3_, ...), custom_call_target="tpu_custom_call" | custom-call | bytes 255000000 | tf_op jit(solution)/shard_map/pallas_call | solution.py:757
  663.9 81.0 %shard_map.160 = (bf16[2048,3072]{1,0:T(8,128)(2,1)}, bf16[2048,256]{1,0:T(8,128)(2,1)}) custom-call(bf16[128,3072]{1,0:T(8,128)(2,1)} %get-tuple-element.54.refs_0_, bf16[256,3072]{1,0:T(8,128)(2,1)} %shard_map.154.refs_1_), custom_call_target="tpu_custom_call" | custom-call | bytes 225000000 | tf_op jit(solution)/shard_map/pallas_call | solution.py:366
  744.9 8.5 convolution_convert_fusion.4
  758.1 2.0 constant_dynamic-slice_fusion.8
  760.6 33.1 %attend_back.1.refs_0_ = bf16[2048,768]{1,0:T(8,128)(2,1)} custom-call(s32[8]{0:T(128)} %broadcast_add_fusion.high_ref, bf16[2048,768]{1,0:T(8,128)(2,1)} %get-tuple-element.42.qkv_ref, bf16[2048,256]{1,0:T(8,128)(2,1)} %get-tuple-element.43.refs_0_.out_ref, bf16[2048,256]{1,0:T(8,128)(2,1)} %get-tuple-element.57.grad_ref, ...), custom_call_target="tpu_custom_call" | custom-call | bytes 96000000 | tf_op jit(solution)/shard_map/attend_back/pallas_call | solution.py:1039
  793.7 1.5 add_convert_fusion.3
  796.8 5.6 collective-permute-start.8
  802.5 2.6 add_convert_fusion.2
  805.1 13.0 %convolution_convert_fusion.2 = bf16[3072,768]{0,1:T(8,128)(2,1)S(1)} fusion(bf16[2048,3072]{1,0:T(8,128)(2,1)} %get-tuple-element.59, bf16[2048,768]{1,0:T(8,128)(2,1)S(1)} %copy-done), kind=kOutput, calls=%fused_computation.4 | convolution fusion | flops 9666035712 | bytes 20447232 | tf_op jit(solution)/shard_map/dot_general | solution.py:848
  818.4 3.7 copy.59.refs_6_
  822.1 161.5 %shard_map.161 = (bf16[4,128,3072]{2,1,0:T(8,128)(2,1)}, f32[8,3072]{1,0:T(8,128)}, bf16[4,384,576]{2,1,0:T(8,128)(2,1)}) custom-call(bf16[2048,768]{1,0:T(8,128)(2,1)} %attend_back.1.refs_0_, bf16[784,3072]{1,0:T(8,128)(2,1)} %shard_map.153.w_ref.refs_1_, bf16[128,3072]{1,0:T(8,128)(2,1)} %dynamic-slice_bitcast_fusion.5.refs_0_.refs_2_, ...), custom_call_target="tpu_custom_call" | custom-call | bytes 255000000 | tf_op jit(solution)/shard_map/pallas_call | solution.py:757
  983.6 4.2 copy.60
  987.8 2.2 copy.61
  990.0 2.9 copy.69
  993.0 1.5 dynamic-slice_reduce_fusion
  994.5 1.3 collective-permute-start.9
  997.8 7.2 collective-permute-done.9
  1006.2 1.8 add_convert_fusion.1
  1008.2 3.1 collective-permute-start.17
  1011.3 4.4 add_convert_fusion
  1015.7 1.7 constant_dynamic-slice_fusion.5
  1017.6 3.3 collective-permute-start.13
  1022.6 10.3 collective-permute-done.17
  1033.7 79.9 %collective-permute-done.18 = bf16[384,512]{1,0:T(8,128)(2,1)} collective-permute-done((bf16[384,512]{1,0:T(8,128)(2,1)S(1)}, bf16[384,512]{1,0:T(8,128)(2,1)}, u32[]{:S(2)}, u32[]{:S(2)}) %collective-permute-start.18) | collective-permute-done | bytes 393248 | tf_op jit(solution)/shard_map/ppermute | solution.py:1156
  1113.7 1.3 copy.68
  1115.0 1.9 reshape.153
  1119.4 2.3 copy.63
  1121.7 2.3 copy.64
  1124.0 2.3 copy.65
  1126.2 1.4 constant_dynamic-update-slice_fusion.3
  1127.6 1.3 constant_dynamic-update-slice_fusion.2
  1129.5 3.1 copy.66
  1132.6 6.6 copy.70
  1139.2 3.9 copy.86
  1143.1 1.7 copy.87
  (124 shorter events, 24.9 us)
Async XLA Ops:
  7.2 413.3 %all-gather.3.cloned.1.call-start = ((), (), s32[]{:S(2)}) async-start(), calls=%async_computation.1 | async-start | bytes 13369344 | tf_op jit(solution)/shard_map/all_gather | solution.py:1162
  7.2 3.0 copy-start.12
  7.2 3.0 copy-start.13
  133.2 669.3 %reduce-scatter.2.cloned.1.call-start = ((), (), s32[]{:S(2)}) async-start(), calls=%async_computation.2 | async-start | bytes 13369344 | tf_op jit(solution)/shard_map/reduce_scatter | solution.py:1358
  144.7 5.6 copy-start.11
  146.4 61.9 %collective-permute-start = (bf16[1024,384]{1,0:T(8,128)(2,1)}, bf16[1024,384]{1,0:T(8,128)(2,1)}, u32[]{:S(2)}, u32[]{:S(2)}) collective-permute-start(bf16[1024,384]{1,0:T(8,128)(2,1)} %get-tuple-element.102), channel_id=1, source_target_pairs={{0,4},{4,8},{8,12},{12,0},{1,5},{5,9},{9,13},{13,1},{2,6},{6,10},{... | collective-permute-start | bytes 2359304 | tf_op jit(solution)/shard_map/ppermute | solution.py:1127
  147.6 131.0 %collective-permute-start.1 = (bf16[1024,384]{1,0:T(8,128)(2,1)}, bf16[1024,384]{1,0:T(8,128)(2,1)}, u32[]{:S(2)}, u32[]{:S(2)}) collective-permute-start(bf16[1024,384]{1,0:T(8,128)(2,1)} %get-tuple-element.101), channel_id=1, source_target_pairs={{0,8},{4,12},{8,0},{12,4},{1,9},{5,13},{9,1},{13,5},{2,10},{6,14},... | collective-permute-start | bytes 2359304 | tf_op jit(solution)/shard_map/ppermute | solution.py:1127
  147.7 131.1 %collective-permute-start.2 = (bf16[1024,384]{1,0:T(8,128)(2,1)}, bf16[1024,384]{1,0:T(8,128)(2,1)}, u32[]{:S(2)}, u32[]{:S(2)}) collective-permute-start(bf16[1024,384]{1,0:T(8,128)(2,1)} %get-tuple-element.100), channel_id=1, source_target_pairs={{0,12},{4,0},{8,4},{12,8},{1,13},{5,1},{9,5},{13,9},{2,14},{6,2},{... | collective-permute-start | bytes 2359304 | tf_op jit(solution)/shard_map/ppermute | solution.py:1127
  149.0 265.9 %collective-permute-start.3 = (bf16[1024,384]{1,0:T(8,128)(2,1)}, bf16[1024,384]{1,0:T(8,128)(2,1)}, u32[]{:S(2)}, u32[]{:S(2)}) collective-permute-start(bf16[1024,384]{1,0:T(8,128)(2,1)} %get-tuple-element.103.refs_0_), channel_id=1, source_target_pairs={{0,16},{16,0},{1,17},{17,1},{2,18},{18,2},{3,19},{19,3},{4,20},{20... | collective-permute-start | bytes 2359304 | tf_op jit(solution)/shard_map/ppermute | solution.py:1132
  208.3 206.5 %collective-permute-start.4 = (bf16[1024,384]{1,0:T(8,128)(2,1)}, bf16[1024,384]{1,0:T(8,128)(2,1)}, u32[]{:S(2)}, u32[]{:S(2)}) collective-permute-start(bf16[1024,384]{1,0:T(8,128)(2,1)} %collective-permute-done.refs_1_), channel_id=1, source_target_pairs={{0,16},{16,0},{1,17},{17,1},{2,18},{18,2},{3,19},{19,3},{4,20},{20... | collective-permute-start | bytes 2359304 | tf_op jit(solution)/shard_map/ppermute | solution.py:1132
  278.6 136.3 %collective-permute-start.5 = (bf16[1024,384]{1,0:T(8,128)(2,1)}, bf16[1024,384]{1,0:T(8,128)(2,1)}, u32[]{:S(2)}, u32[]{:S(2)}) collective-permute-start(bf16[1024,384]{1,0:T(8,128)(2,1)} %collective-permute-done.1.refs_2_), channel_id=1, source_target_pairs={{0,16},{16,0},{1,17},{17,1},{2,18},{18,2},{3,19},{19,3},{4,20},{20... | collective-permute-start | bytes 2359304 | tf_op jit(solution)/shard_map/ppermute | solution.py:1132
  278.8 136.1 %collective-permute-start.6 = (bf16[1024,384]{1,0:T(8,128)(2,1)}, bf16[1024,384]{1,0:T(8,128)(2,1)}, u32[]{:S(2)}, u32[]{:S(2)}) collective-permute-start(bf16[1024,384]{1,0:T(8,128)(2,1)} %collective-permute-done.2.refs_3_), channel_id=1, source_target_pairs={{0,16},{16,0},{1,17},{17,1},{2,18},{18,2},{3,19},{19,3},{4,20},{20... | collective-permute-start | bytes 2359304 | tf_op jit(solution)/shard_map/ppermute | solution.py:1132
  517.2 0.7 copy-start.14
  517.2 3.2 copy-start.10
  517.2 622.0 %all-gather.5.cloned.1.call-start = ((), (), s32[]{:S(2)}) async-start(), calls=%async_computation.3 | async-start | bytes 3932160 | tf_op jit(solution)/shard_map/all_gather | solution.py:1360
  520.4 1.6 copy-start.15
  520.4 14.2 %slice-start.2 = ((s8[12582912]{0:T(1024)(128)(4,1)}), s8[4194304]{0:T(1024)(128)(4,1)S(1)}, s32[]{:S(2)}) async-start(s8[12582912]{0:T(1024)(128)(4,1)} %bitcast.112), calls=%async_computation.6 | async-start | bytes 8388608
  522.0 12.7 %copy-start.1 = (bf16[2048,1024]{1,0:T(8,128)(2,1)}, bf16[2048,1024]{1,0:T(8,128)(2,1)S(1)}, u32[]{:S(2)}) copy-start(bf16[2048,1024]{1,0:T(8,128)(2,1)S(1)} %constant_dynamic-update-slice_fusion.5.refs_0_) | copy-start | bytes 12582916
  522.0 12.7 %slice-start.3 = ((s8[12582912]{0:T(1024)(128)(4,1)}), s8[4194304]{0:T(1024)(128)(4,1)S(1)}, s32[]{:S(2)}) async-start(s8[12582912]{0:T(1024)(128)(4,1)} %bitcast.112), calls=%async_computation.7 | async-start | bytes 8388608
  522.0 12.7 %slice-start.4 = ((s8[12582912]{0:T(1024)(128)(4,1)}), s8[4194304]{0:T(1024)(128)(4,1)S(1)}, s32[]{:S(2)}) async-start(s8[12582912]{0:T(1024)(128)(4,1)} %bitcast.112), calls=%async_computation.8 | async-start | bytes 8388608
  744.9 13.2 %slice-start = ((s8[6291456]{0:T(1024)(128)(4,1)}), s8[4194304]{0:T(1024)(128)(4,1)S(1)}, s32[]{:S(2)}) async-start(s8[6291456]{0:T(1024)(128)(4,1)} %bitcast.96), calls=%async_computation.4 | async-start | bytes 8388608
  744.9 13.2 %slice-start.1 = ((s8[6291456]{0:T(1024)(128)(4,1)}), s8[2097152]{0:T(1024)(128)(4,1)S(1)}, s32[]{:S(2)}) async-start(s8[6291456]{0:T(1024)(128)(4,1)} %bitcast.96), calls=%async_computation.5 | async-start | bytes 4194304
  753.4 2.5 copy-start.4
  753.5 1.0 copy-start.2
  755.3 38.3 %collective-permute-start.7 = (bf16[1536,192]{0,1:T(8,128)(2,1)}, bf16[1536,192]{0,1:T(8,128)(2,1)}, u32[]{:S(2)}, u32[]{:S(2)}) collective-permute-start(bf16[1536,192]{0,1:T(8,128)(2,1)} %constant_dynamic-slice_fusion.12), channel_id=1, source_target_pairs={{0,16},{16,0},{1,17},{17,1},{2,18},{18,2},{3,19},{19,3},{4,20},{20... | collective-permute-start | bytes 1769480 | tf_op jit(solution)/shard_map/ppermute | solution.py:1147
  757.2 249.0 %collective-permute-start.15 = (bf16[1536,512]{1,0:T(8,128)(2,1)}, bf16[1536,512]{1,0:T(8,128)(2,1)}, u32[]{:S(2)}, u32[]{:S(2)}) collective-permute-start(bf16[1536,512]{1,0:T(8,128)(2,1)} %constant_dynamic-slice_fusion.4), channel_id=1, source_target_pairs={{0,16},{16,0},{1,17},{17,1},{2,18},{18,2},{3,19},{19,3},{4,20},{20... | collective-permute-start | bytes 4718600 | tf_op jit(solution)/shard_map/ppermute | solution.py:1147
  760.0 251.2 %collective-permute-start.11 = (bf16[1536,1024]{1,0:T(8,128)(2,1)}, bf16[1536,1024]{1,0:T(8,128)(2,1)}, u32[]{:S(2)}, u32[]{:S(2)}) collective-permute-start(bf16[1536,1024]{1,0:T(8,128)(2,1)} %constant_dynamic-slice_fusion.8), channel_id=1, source_target_pairs={{0,16},{16,0},{1,17},{17,1},{2,18},{18,2},{3,19},{19,3},{4,20},{20... | collective-permute-start | bytes 9437192 | tf_op jit(solution)/shard_map/ppermute | solution.py:1147
  793.7 11.4 copy-start
  795.2 0.8 copy-start.9
  796.8 200.0 %collective-permute-start.8 = (bf16[384,192]{0,1:T(8,128)(2,1)}, bf16[384,192]{0,1:T(8,128)(2,1)}, u32[]{:S(2)}, u32[]{:S(2)}) collective-permute-start(bf16[384,192]{0,1:T(8,128)(2,1)} %get-tuple-element.111), channel_id=1, source_target_pairs={{0,4},{4,8},{8,12},{12,0},{1,5},{5,9},{9,13},{13,1},{2,6},{6,10},{... | collective-permute-start | bytes 442376 | tf_op jit(solution)/shard_map/ppermute | solution.py:1156
  993.0 13.2 %copy-start.5 = (bf16[3072,512]{1,0:T(8,128)(2,1)S(1)}, bf16[3072,512]{1,0:T(8,128)(2,1)}, u32[]{:S(2)}) copy-start(bf16[3072,512]{1,0:T(8,128)(2,1)} %convolution_convert_fusion.3) | copy-start | bytes 9437188
  994.5 10.5 collective-permute-start.9
  995.8 9.2 collective-permute-start.10
  1008.1 13.1 %collective-permute-start.16 = (bf16[384,512]{1,0:T(8,128)(2,1)S(1)}, bf16[384,512]{1,0:T(8,128)(2,1)S(1)}, u32[]{:S(2)}, u32[]{:S(2)}) collective-permute-start(bf16[384,512]{1,0:T(8,128)(2,1)S(1)} %get-tuple-element.106), channel_id=1, source_target_pairs={{0,4},{4,8},{8,12},{12,0},{1,5},{5,9},{9,13},{13,1},{2,6},{6,10},{... | collective-permute-start | bytes 1179656 | tf_op jit(solution)/shard_map/ppermute | solution.py:1156
  1008.2 24.6 %collective-permute-start.17 = (bf16[384,512]{1,0:T(8,128)(2,1)S(1)}, bf16[384,512]{1,0:T(8,128)(2,1)S(1)}, u32[]{:S(2)}, u32[]{:S(2)}) collective-permute-start(bf16[384,512]{1,0:T(8,128)(2,1)S(1)} %get-tuple-element.105), channel_id=1, source_target_pairs={{0,8},{4,12},{8,0},{12,4},{1,9},{5,13},{9,1},{13,5},{2,10},{6,14},... | collective-permute-start | bytes 1179656 | tf_op jit(solution)/shard_map/ppermute | solution.py:1156
  1017.4 102.0 %collective-permute-start.12 = (bf16[384,1024]{1,0:T(8,128)(2,1)}, bf16[384,1024]{1,0:T(8,128)(2,1)}, u32[]{:S(2)}, u32[]{:S(2)}) collective-permute-start(bf16[384,1024]{1,0:T(8,128)(2,1)} %get-tuple-element.98), channel_id=1, source_target_pairs={{0,4},{4,8},{8,12},{12,0},{1,5},{5,9},{9,13},{13,1},{2,6},{6,10},{... | collective-permute-start | bytes 2359304 | tf_op jit(solution)/shard_map/ppermute | solution.py:1156
  1017.6 104.1 %collective-permute-start.13 = (bf16[384,1024]{1,0:T(8,128)(2,1)}, bf16[384,1024]{1,0:T(8,128)(2,1)}, u32[]{:S(2)}, u32[]{:S(2)}) collective-permute-start(bf16[384,1024]{1,0:T(8,128)(2,1)} %get-tuple-element.97), channel_id=1, source_target_pairs={{0,8},{4,12},{8,0},{12,4},{1,9},{5,13},{9,1},{13,5},{2,10},{6,14},... | collective-permute-start | bytes 2359304 | tf_op jit(solution)/shard_map/ppermute | solution.py:1156
  1020.9 103.1 %collective-permute-start.14 = (bf16[384,1024]{1,0:T(8,128)(2,1)}, bf16[384,1024]{1,0:T(8,128)(2,1)}, u32[]{:S(2)}, u32[]{:S(2)}) collective-permute-start(bf16[384,1024]{1,0:T(8,128)(2,1)} %get-tuple-element.96), channel_id=1, source_target_pairs={{0,12},{4,0},{8,4},{12,8},{1,13},{5,1},{9,5},{13,9},{2,14},{6,2},{... | collective-permute-start | bytes 2359304 | tf_op jit(solution)/shard_map/ppermute | solution.py:1156
  1021.3 92.4 %collective-permute-start.18 = (bf16[384,512]{1,0:T(8,128)(2,1)S(1)}, bf16[384,512]{1,0:T(8,128)(2,1)}, u32[]{:S(2)}, u32[]{:S(2)}) collective-permute-start(bf16[384,512]{1,0:T(8,128)(2,1)S(1)} %get-tuple-element.104), channel_id=1, source_target_pairs={{0,12},{4,0},{8,4},{12,8},{1,13},{5,1},{9,5},{13,9},{2,14},{6,2},{... | collective-permute-start | bytes 1179656 | tf_op jit(solution)/shard_map/ppermute | solution.py:1156
  1113.7 3.2 copy-start.8
  1118.1 1.1 copy-start.7
  1126.2 2.7 copy-start.6
  1139.2 3.9 copy-start.3
Sparse Core Ops, SparseCore 0:
  133.3 154.4 all-gather.2
  517.3 187.7 reduce-scatter.1
  805.2 38.6 all-gather.4

commit v3 on v2

--- a/solution.py
+++ b/solution.py
@@ -20,6 +20,7 @@
 GAIN_ROWS = 16
 MESH = pl.DeviceIdType.MESH
 SUBS = 2
+PARTS = 4
 VLIM = 64 * 1024 * 1024 - 65536
 
 
@@ -440,7 +441,7 @@
     tile = 512
     width = total.shape[1]
 
-    sub = part // SUBS
+    sub = part // PARTS
 
     def remote(src, dst, sems, dev):
         return pltpu.make_async_remote_copy(
@@ -486,7 +487,7 @@
 
     def sweep(body, s=None):
         steps = part // chunk
-        lo, hi = (0, steps) if s is None else (s * steps // SUBS, (s + 1) * steps // SUBS)
+        lo, hi = (0, steps) if s is None else (s * steps // PARTS, (s + 1) * steps // PARTS)
 
         def one(i, carry):
             body(rows(i))
@@ -523,7 +524,7 @@
             got = krecv[cc * 2 + 1 - y, r, :].astype(jnp.float32)
             ysend[cc, r, :] = (own[0, r, :] + got).astype(jnp.bfloat16)
 
-        for s in range(SUBS):
+        for s in range(PARTS):
             sweep(add_y, s)
             y_copy(cc, s).start()
         produce(cc, y, 1)
@@ -559,7 +560,7 @@
 
     def second(j):
         cc = near_order(c, size - 1 - j, size)
-        for s in range(SUBS):
+        for s in range(PARTS):
 
             @pl.when(cc > c)
             def _():
@@ -614,7 +615,7 @@
 
     begin, one_chunk, end = final(total, ins, outs, extra)
     begin()
-    for s in range(SUBS):
+    for s in range(PARTS):
         y_copy(c, s).wait_recv()
 
         @pl.when(c > 0)
@@ -637,7 +638,7 @@
     def drain(cc, carry):
         for yy in range(2):
             k_copy(cc, yy).wait_send()
-        for s in range(SUBS):
+        for s in range(PARTS):
             y_copy(cc, s).wait_send()
 
             @pl.when(cc > c)
@@ -790,8 +791,8 @@
             pltpu.VMEM((part, width), full),
             pltpu.VMEM((2 * part, 512), full),
             pltpu.SemaphoreType.DMA((size * 2, 2)),
-            pltpu.SemaphoreType.DMA((size, SUBS, 2)),
-            pltpu.SemaphoreType.DMA((2, size, SUBS, 2)),
+            pltpu.SemaphoreType.DMA((size, PARTS, 2)),
+            pltpu.SemaphoreType.DMA((2, size, PARTS, 2)),
             *extra,
         ],
         compiler_params=pltpu.CompilerParams(
@@ -1136,7 +1137,7 @@
     return pieces
 
 
-def hand_out(grad, beside=None):
+def hand_out(grad):
     size, groups = lax.axis_size("ctx"), lax.axis_size("fsdp")
     c, f = lax.axis_index("ctx"), lax.axis_index("fsdp")
     rows = grad.shape[0] // groups
@@ -1147,15 +1148,48 @@
         got = lax.ppermute(sent, "fsdp", [(i, (i + g) % groups) for i in range(groups)])
         total = total.astype(jnp.float32) + got.astype(jnp.float32)
     total = total.astype(jnp.bfloat16)
-    if beside is not None:
-        total, beside = lax.optimization_barrier((total, beside))
-    out = jnp.zeros((size, d, grad.shape[1]), jnp.bfloat16)
+    pieces = []
     for s in range(size):
         piece = lax.dynamic_slice_in_dim(total, ((c + s) % size) * d, d, 0)
         if s:
             piece = lax.ppermute(piece, "ctx", [(i, (i + s) % size) for i in range(size)])
-        out = lax.dynamic_update_slice(out, piece[None], ((c - s) % size, 0, 0))
-    return out if beside is None else (out, beside)
+        pieces.append(piece)
+    return pieces
+
+
+def finish_kernel(size, *refs):
+    gu, down, out = refs[:size], refs[size : 2 * size], refs[2 * size : 3 * size]
+    rows, gu_ref, down_ref, out_ref, rows_ref = refs[3 * size :]
+    c = lax.axis_index("ctx")
+    half, narrow = down[0].shape[1], out[0].shape[1]
+    for s in range(size):
+        source = (c + size - s) % size
+        lanes = pl.ds(pl.multiple_of(source * half, half), half)
+        for j in range(2):
+            gu_ref[j, :, lanes] = gu[s][:, j * half : (j + 1) * half].astype(jnp.float32)
+        down_ref[lanes, :] = down[s][...].astype(jnp.float32).T
+        at = pl.ds(pl.multiple_of(source * narrow, narrow), narrow)
+        out_ref[at, :] = out[s][...].astype(jnp.float32).T
+    rows_ref[...] = rows[...]
+
+
+def finish_call(gu, down, out, rows, size):
+    d, full = gu[0].shape[0], jnp.float32
+    vmem = pl.BlockSpec(memory_space=pltpu.VMEM)
+    return pl.pallas_call(
+        functools.partial(finish_kernel, size),
+        out_shape=(
+            jax.ShapeDtypeStruct((2, d, size * down[0].shape[1]), full),
+            jax.ShapeDtypeStruct((size * down[0].shape[1], d), full),
+            jax.ShapeDtypeStruct((size * out[0].shape[1], d), full),
+            jax.ShapeDtypeStruct(rows.shape, rows.dtype),
+        ),
+        in_specs=[vmem] * (3 * size + 1),
+        out_specs=(vmem,) * 4,
+        compiler_params=pltpu.CompilerParams(vmem_limit_bytes=VLIM),
+        cost_estimate=cost(8),
+        name="finish",
+    )(*gu, *down, *out, rows)
 
 
 def wide_gather(part):
@@ -1299,13 +1333,12 @@
     gain_rows = jnp.concatenate(
         [norm_attn[None], norm_mlp[None], jnp.zeros((GAIN_ROWS - 2, d), low)], axis=0
     )
-    sent_q = w_qkv.transpose(0, 2, 1).reshape(3, size, -1, d).transpose(1, 0, 2, 3)
+    sent_q = w_qkv.reshape(3, d, size, -1).transpose(2, 0, 3, 1)
     sent_q = jnp.concatenate(
         [sent_q.reshape(size, -1, d), jnp.broadcast_to(gain_rows, (size, GAIN_ROWS, d))], axis=1
     )
     sent_o = w_out.reshape(size, -1, d)
-    sent_g = w_gate_up.transpose(0, 2, 1).reshape(2, size, -1, d).transpose(1, 0, 2, 3)
-    sent_g = sent_g.reshape(size, -1, d)
+    sent_g = w_gate_up.reshape(2, d, size, -1).transpose(2, 0, 3, 1).reshape(size, -1, d)
     sent_d = w_down.reshape(size, -1, d)
     tokens_full, moved_q, moved_o = gather_call(
         tokens_own, [], [], no_block, 1, size, [sent_q, sent_o], PLAN
@@ -1400,9 +1433,7 @@
         wide = grad.astype(full).reshape(size, d, count, -1).transpose(2, 1, 0, 3)
         return wide.reshape(count, d, -1)
 
-    grad_gu = natural(out_gu, 2)
-    grad_out = out_out.astype(full).transpose(0, 2, 1).reshape(-1, d)
-    grad_down = out_down.astype(full).transpose(0, 2, 1).reshape(-1, d)
+    grad_gu, grad_down, grad_out, g_tokens = finish_call(out_gu, out_down, out_out, g_tokens, size)
     grad_qkv = natural(out_qkv, 3)
 
     mine = lax.axis_index("fsdp") * size + lax.axis_index("ctx")

time: 1160 us -> 1070 us (0.922)
  the two profiles are of different devices: /device:TPU:15 before, /device:TPU:0 now
where the time goes in v3:
time: 1070 us; the launch traced here: 1060 us
  Pallas kernels  739 us (69%)
  waiting for transfers between devices  113 us (11%)
  matrix products  60.2 us (6%)
  starting transfers between devices  58.3 us (5%)
  local copies, waits for them, and re-layouts  57.3 us (5%)
  other arithmetic  19.9 us (2%)
  between operations  14.6 us (1%)
    pallas_call x3, Pallas kernels, reduce_call(): pl.pallas_call(functools.partial(reduce_kernel, size, groups, last, plan...  351 us
    pallas_call x3, Pallas kernels, gather_call(): pl.pallas_call(functools.partial(gather_kernel, size, groups, plan or {},...  283 us
    ppermute x3, waiting for transfers between devices, cross(): lax.ppermute(piece, 'ctx', [(i, (i + s) % size) for i in range(size)])  110 us
    dot_general x4, matrix products, tn(): lax.dot_general(left, right, (((0,), (0,)), ((), ())), preferred_element_...  48.5 us
    pallas_call x1, Pallas kernels, attend_back_call(): pl.pallas_call(functools.partial(attend_back_kernel, heads, scale), out_s...  37 us
    ppermute x9, starting transfers between devices, hand_out(): lax.ppermute(piece, 'ctx', [(i, (i + s) % size) for i in range(size)])  33.4 us
    pallas_call x1, Pallas kernels, attend_call(): pl.pallas_call(functools.partial(attend_kernel, heads, scale), out_shape=...  23.5 us
  transfers between devices with their start and end apart: 22, of which 3 were waited for; matrix products, arithmetic and copies ran while one was open for 10% of the time, Pallas kernels for 51%

profile of v3, /device:TPU:0, one launch (start us, length us, event | category | flops | bytes accessed | tf_op | source)
XLA Modules:
  0.0 1062.9 jit_solution(12728133185819036155)
XLA Ops:
  8.7 2.1 dynamic-slice_bitcast_fusion.4.refs_0_.refs_2_
  10.8 2.1 dynamic-slice_bitcast_fusion.5.refs_3_
  12.9 1.1 copy.44
  14.3 1.4 pad_maximum_fusion.refs_1_.refs_0_
  15.7 109.7 %shard_map.152 = (bf16[2048,3072]{1,0:T(8,128)(2,1)}, bf16[8,592,384]{2,1,0:T(8,128)(2,1)}, bf16[8,192,384]{2,1,0:T(8,128)(2,1)}) custom-call(bf16[128,3072]{1,0:T(8,128)(2,1)} %dynamic-slice_bitcast_fusion.4.refs_0_.refs_2_, bf16[4,592,384]{2,1,0:T(8,128)(2,1)} %pad_maximum_fusion.refs_1_.refs_0_, bf16[4,192,384]{2,1,0:T(8,128)(2,1)} %bitcast.67), custom_call_target="tpu_custom_call" | custom-call | bytes 225000000 | tf_op jit(solution)/shard_map/pallas_call | solution.py:367
  125.6 6.2 reshape.105
  131.7 5.1 copy.47
  136.9 1.7 dynamic-slice_bitcast_fusion
  138.6 1.0 collective-permute-start.2
  139.6 13.1 %collective-permute-start.1 = (bf16[1024,384]{1,0:T(8,128)(2,1)}, bf16[1024,384]{1,0:T(8,128)(2,1)}, u32[]{:S(2)}, u32[]{:S(2)}) collective-permute-start(bf16[1024,384]{1,0:T(8,128)(2,1)} %get-tuple-element.109), channel_id=1, source_target_pairs={{0,8},{4,12},{8,0},{12,4},{1,9},{5,13},{9,1},{13,5},{2,10},{6,14},... | collective-permute-start | bytes 2359304 | tf_op jit(solution)/shard_map/ppermute | solution.py:1128
  152.7 1.7 collective-permute-start
  155.7 3.7 fusion.2
  159.5 2.5 pad_maximum_fusion.1
  162.6 1.3 copy.46.col_ref
  163.9 2.6 shard_map.154.refs_1_
  166.6 5.2 shard_map.153.w_ref.refs_1_
  172.6 16.4 %collective-permute-done.2.refs_3_ = bf16[1024,384]{1,0:T(8,128)(2,1)} collective-permute-done((bf16[1024,384]{1,0:T(8,128)(2,1)}, bf16[1024,384]{1,0:T(8,128)(2,1)}, u32[]{:S(2)}, u32[]{:S(2)}) %collective-permute-start.2) | collective-permute-done | bytes 786464 | tf_op jit(solution)/shard_map/ppermute | solution.py:1128
  189.0 1.0 collective-permute-start.6
  190.0 93.3 %collective-permute-done.1.refs_2_ = bf16[1024,384]{1,0:T(8,128)(2,1)} collective-permute-done((bf16[1024,384]{1,0:T(8,128)(2,1)}, bf16[1024,384]{1,0:T(8,128)(2,1)}, u32[]{:S(2)}, u32[]{:S(2)}) %collective-permute-start.1) | collective-permute-done | bytes 786464 | tf_op jit(solution)/shard_map/ppermute | solution.py:1128
  283.4 1.5 collective-permute-start.5
  286.0 19.0 %qkv.1 = (bf16[2048,768]{1,0:T(8,128)(2,1)}, bf16[2048,3072]{1,0:T(8,128)(2,1)}) custom-call(bf16[2048,3072]{1,0:T(8,128)(2,1)} %get-tuple-element.44.x_ref, bf16[784,3072]{1,0:T(8,128)(2,1)} %shard_map.153.w_ref.refs_1_, f32[1,3072]{1,0:T(1,128)} %get-tuple-element.123.gain_ref.refs_4_, f32[2048,128]{1,0:T(8,128)} %get-tuple-element.117.cos_ref, ...), custom_call_target="tpu_custom_call" | custom-call | bytes 54000000 | tf_op jit(solution)/shard_map/qkv/pallas_call | solution.py:870
  305.0 1.2 and_select_fusion.low_ref
  306.2 23.5 %attend.1 = (bf16[2048,256]{1,0:T(8,128)(2,1)}, f32[2,2048]{1,0:T(2,128)}) custom-call(s32[8]{0:T(128)} %and_select_fusion.low_ref, bf16[2048,768]{1,0:T(8,128)(2,1)} %get-tuple-element.46.qkv_ref, s32[2048,1]{1,0:T(8,128)} %copy.46.col_ref, s32[1,2048]{1,0:T(1,128)} %row_ref.3), custom_call_target="tpu_custom_call" | custom-call | bytes 60000000 | tf_op jit(solution)/shard_map/attend/pallas_call | solution.py:946
  329.7 83.9 %shard_map.155 = (f32[128,3072]{1,0:T(8,128)}, bf16[128,3072]{1,0:T(8,128)(2,1)}, bf16[8,512,384]{2,1,0:T(8,128)(2,1)}) custom-call(bf16[2048,256]{1,0:T(8,128)(2,1)} %get-tuple-element.47.refs_0_.out_ref, bf16[256,3072]{1,0:T(8,128)(2,1)} %shard_map.154.refs_1_, bf16[128,3072]{1,0:T(8,128)(2,1)} %dynamic-slice_bitcast_fusion.4.refs_0_.refs_2_, ...), custom_call_target="tpu_custom_call" | custom-call | bytes 255000000 | tf_op jit(solution)/shard_map/pallas_call | solution.py:758
  413.6 3.6 shard_map.157.refs_2_
  417.3 5.6 shard_map.156.refs_1_
  422.9 84.4 %shard_map.158 = (bf16[2048,3072]{1,0:T(8,128)(2,1)}, bf16[2048,512]{1,0:T(8,128)(2,1)}, bf16[2048,512]{1,0:T(8,128)(2,1)}, bf16[2048,512]{1,0:T(8,128)(2,1)}) custom-call(bf16[128,3072]{1,0:T(8,128)(2,1)} %get-tuple-element.50.refs_0_, bf16[1024,3072]{1,0:T(8,128)(2,1)} %shard_map.156.refs_1_, bf16[512,3072]{1,0:T(8,128)(2,1)} %shard_map.157.refs_2_, ...), custom_call_target="tpu_custom_call" | custom-call | bytes 225000000 | tf_op jit(solution)/shard_map/pallas_call | solution.py:367
  507.2 11.7 %convolution_convert_fusion = bf16[2048,3072]{1,0:T(8,128)(2,1)} fusion(bf16[2048,512]{1,0:T(8,128)(2,1)} %get-tuple-element.53, bf16[512,3072]{1,0:T(8,128)(2,1)} %shard_map.157.refs_2_), kind=kOutput, calls=%fused_computation | convolution fusion | flops 6448742400 | bytes 17825792 | tf_op jit(solution)/shard_map/dot_general | solution.py:845
  519.5 2.0 constant_dynamic-update-slice_fusion.1
  521.9 1.2 copy-done.13
  523.2 12.6 %convolution_convert_fusion.3 = bf16[3072,512]{1,0:T(8,128)(2,1)} fusion(bf16[2048,3072]{1,0:T(8,128)(2,1)} %all-gather.3.cloned.1.call-done.refs_3_, bf16[2048,512]{1,0:T(8,128)(2,1)S(1)} %copy-done.13), kind=kOutput, calls=%fused_computation.4 | convolution fusion | flops 6444023808 | bytes 17825792 | tf_op jit(solution)/shard_map/dot_general | solution.py:849
  535.8 14.4 %convolution_convert_fusion.1 = bf16[3072,1024]{1,0:T(8,128)(2,1)S(1)} fusion(bf16[2048,3072]{1,0:T(8,128)(2,1)S(1)} %bitcast.72, bf16[2048,1024]{1,0:T(8,128)(2,1)S(1)} %constant_dynamic-update-slice_fusion.refs_0_), kind=kOutput, calls=%fused_computation.2 | convolution fusion | flops 12888047616 | bytes 23068672 | tf_op jit(solution)/shard_map/dot_general | solution.py:849
  550.2 2.2 constant_dynamic-slice_fusion.15
  552.4 1.4 copy-done.2
  553.8 2.5 collective-permute-start.7
  556.3 110.9 %shard_map.159 = (f32[128,3072]{1,0:T(8,128)}, bf16[128,3072]{1,0:T(8,128)(2,1)}, f32[16,3072]{1,0:T(8,128)}) custom-call(bf16[2048,1024]{1,0:T(8,128)(2,1)} %copy-done.1, bf16[1024,3072]{1,0:T(8,128)(2,1)} %shard_map.156.refs_1_, f32[128,3072]{1,0:T(8,128)} %get-tuple-element.49.refs_2_, bf16[128,3072]{1,0:T(8,128)(2,1)} %dynamic-slice_bitcast_fusion.5.refs_3_, ...), custom_call_target="tpu_custom_call" | custom-call | bytes 255000000 | tf_op jit(solution)/shard_map/pallas_call | solution.py:758
  667.3 88.5 %shard_map.160 = (bf16[2048,3072]{1,0:T(8,128)(2,1)}, bf16[2048,256]{1,0:T(8,128)(2,1)}) custom-call(bf16[128,3072]{1,0:T(8,128)(2,1)} %get-tuple-element.60.refs_0_, bf16[256,3072]{1,0:T(8,128)(2,1)} %shard_map.154.refs_1_), custom_call_target="tpu_custom_call" | custom-call | bytes 225000000 | tf_op jit(solution)/shard_map/pallas_call | solution.py:367
  755.8 8.3 convolution_convert_fusion.4
  765.1 1.6 collective-permute-start.15
  766.8 1.3 constant_dynamic-slice_fusion.10
  768.0 1.0 collective-permute-start.11
  769.6 1.6 copy.48
  771.2 37.0 %attend_back.1.refs_0_ = bf16[2048,768]{1,0:T(8,128)(2,1)} custom-call(s32[8]{0:T(128)} %broadcast_add_fusion.high_ref, bf16[2048,768]{1,0:T(8,128)(2,1)} %get-tuple-element.46.qkv_ref, bf16[2048,256]{1,0:T(8,128)(2,1)} %get-tuple-element.47.refs_0_.out_ref, bf16[2048,256]{1,0:T(8,128)(2,1)} %get-tuple-element.64.grad_ref, ...), custom_call_target="tpu_custom_call" | custom-call | bytes 96000000 | tf_op jit(solution)/shard_map/attend_back/pallas_call | solution.py:1040
  808.2 1.5 copy.49
  809.7 2.6 add_convert_fusion.3
  813.3 2.4 collective-permute-start.18
  816.3 2.7 add_convert_fusion.1
  819.0 1.1 constant_dynamic-slice_fusion.6
  820.1 3.0 collective-permute-start.14
  823.2 1.2 collective-permute-start.13
  824.4 3.4 add_convert_fusion
  827.8 1.7 constant_dynamic-slice_fusion.11
  829.6 3.3 collective-permute-done.17.refs_10_
  833.4 19.6 %collective-permute-start.9 = (bf16[384,1024]{1,0:T(8,128)(2,1)}, bf16[384,1024]{1,0:T(8,128)(2,1)}, u32[]{:S(2)}, u32[]{:S(2)}) collective-permute-start(bf16[384,1024]{1,0:T(8,128)(2,1)} %get-tuple-element.105), channel_id=1, source_target_pairs={{0,8},{4,12},{8,0},{12,4},{1,9},{5,13},{9,1},{13,5},{2,10},{6,14},... | collective-permute-start | bytes 2359304 | tf_op jit(solution)/shard_map/ppermute | solution.py:1155
  853.0 5.9 collective-permute-start.8
  859.0 13.1 %convolution_convert_fusion.2 = bf16[3072,768]{0,1:T(8,128)(2,1)S(1)} fusion(bf16[2048,3072]{1,0:T(8,128)(2,1)} %get-tuple-element.66, bf16[2048,768]{1,0:T(8,128)(2,1)S(1)} %copy-done), kind=kOutput, calls=%fused_computation.3 | convolution fusion | flops 9666035712 | bytes 20447232 | tf_op jit(solution)/shard_map/dot_general | solution.py:849
  872.4 3.7 copy.51.refs_6_
  876.1 156.3 %shard_map.161 = (bf16[4,128,3072]{2,1,0:T(8,128)(2,1)}, f32[8,3072]{1,0:T(8,128)}, bf16[4,384,576]{2,1,0:T(8,128)(2,1)}) custom-call(bf16[2048,768]{1,0:T(8,128)(2,1)} %attend_back.1.refs_0_, bf16[784,3072]{1,0:T(8,128)(2,1)} %shard_map.153.w_ref.refs_1_, bf16[128,3072]{1,0:T(8,128)(2,1)} %dynamic-slice_bitcast_fusion.4.refs_0_.refs_2_, ...), custom_call_target="tpu_custom_call" | custom-call | bytes 255000000 | tf_op jit(solution)/shard_map/pallas_call | solution.py:758
  1032.4 4.2 copy.52
  1036.5 2.2 copy.53
  1038.8 2.9 copy.54
  1041.7 1.4 dynamic-slice_reduce_fusion
  1043.2 9.2 finish.1
  1052.4 3.8 copy.57
  (96 shorter events, 10.7 us)
Async XLA Ops:
  7.2 5.7 copy-start.6
  7.2 415.7 %all-gather.3.cloned.1.call-start = ((), (), s32[]{:S(2)}) async-start(), calls=%async_computation.1 | async-start | bytes 13369344 | tf_op jit(solution)/shard_map/all_gather | solution.py:1196
  125.5 684.2 %reduce-scatter.2.cloned.1.call-start = ((), (), s32[]{:S(2)}) async-start(), calls=%async_computation.2 | async-start | bytes 13369344 | tf_op jit(solution)/shard_map/reduce_scatter | solution.py:1391
  136.8 18.0 %copy-start.8 = (s32[1,2048]{1,0:T(1,128)S(1)}, s32[1,2048]{1,0:T(1,128)}, u32[]{:S(2)}) copy-start(s32[1,2048]{1,0:T(1,128)} %row_ref.3) | copy-start | bytes 24580
  138.6 50.4 %collective-permute-start.2 = (bf16[1024,384]{1,0:T(8,128)(2,1)}, bf16[1024,384]{1,0:T(8,128)(2,1)}, u32[]{:S(2)}, u32[]{:S(2)}) collective-permute-start(bf16[1024,384]{1,0:T(8,128)(2,1)} %get-tuple-element.108), channel_id=1, source_target_pairs={{0,12},{4,0},{8,4},{12,8},{1,13},{5,1},{9,5},{13,9},{2,14},{6,2},{... | collective-permute-start | bytes 2359304 | tf_op jit(solution)/shard_map/ppermute | solution.py:1128
  139.6 143.8 %collective-permute-start.1 = (bf16[1024,384]{1,0:T(8,128)(2,1)}, bf16[1024,384]{1,0:T(8,128)(2,1)}, u32[]{:S(2)}, u32[]{:S(2)}) collective-permute-start(bf16[1024,384]{1,0:T(8,128)(2,1)} %get-tuple-element.109), channel_id=1, source_target_pairs={{0,8},{4,12},{8,0},{12,4},{1,9},{5,13},{9,1},{13,5},{2,10},{6,14},... | collective-permute-start | bytes 2359304 | tf_op jit(solution)/shard_map/ppermute | solution.py:1128
  152.7 132.2 %collective-permute-start = (bf16[1024,384]{1,0:T(8,128)(2,1)}, bf16[1024,384]{1,0:T(8,128)(2,1)}, u32[]{:S(2)}, u32[]{:S(2)}) collective-permute-start(bf16[1024,384]{1,0:T(8,128)(2,1)} %get-tuple-element.110), channel_id=1, source_target_pairs={{0,4},{4,8},{8,12},{12,0},{1,5},{5,9},{9,13},{13,1},{2,6},{6,10},{... | collective-permute-start | bytes 2359304 | tf_op jit(solution)/shard_map/ppermute | solution.py:1128
  154.3 262.9 %collective-permute-start.3 = (bf16[1024,384]{1,0:T(8,128)(2,1)}, bf16[1024,384]{1,0:T(8,128)(2,1)}, u32[]{:S(2)}, u32[]{:S(2)}) collective-permute-start(bf16[1024,384]{1,0:T(8,128)(2,1)} %get-tuple-element.111.refs_0_), channel_id=1, source_target_pairs={{0,16},{16,0},{1,17},{17,1},{2,18},{18,2},{3,19},{19,3},{4,20},{20... | collective-permute-start | bytes 2359304 | tf_op jit(solution)/shard_map/ppermute | solution.py:1133
  189.0 228.2 %collective-permute-start.6 = (bf16[1024,384]{1,0:T(8,128)(2,1)}, bf16[1024,384]{1,0:T(8,128)(2,1)}, u32[]{:S(2)}, u32[]{:S(2)}) collective-permute-start(bf16[1024,384]{1,0:T(8,128)(2,1)} %collective-permute-done.2.refs_3_), channel_id=1, source_target_pairs={{0,16},{16,0},{1,17},{17,1},{2,18},{18,2},{3,19},{19,3},{4,20},{20... | collective-permute-start | bytes 2359304 | tf_op jit(solution)/shard_map/ppermute | solution.py:1133
  283.4 133.9 %collective-permute-start.5 = (bf16[1024,384]{1,0:T(8,128)(2,1)}, bf16[1024,384]{1,0:T(8,128)(2,1)}, u32[]{:S(2)}, u32[]{:S(2)}) collective-permute-start(bf16[1024,384]{1,0:T(8,128)(2,1)} %collective-permute-done.1.refs_2_), channel_id=1, source_target_pairs={{0,16},{16,0},{1,17},{17,1},{2,18},{18,2},{3,19},{19,3},{4,20},{20... | collective-permute-start | bytes 2359304 | tf_op jit(solution)/shard_map/ppermute | solution.py:1133
  284.8 132.4 %collective-permute-start.4 = (bf16[1024,384]{1,0:T(8,128)(2,1)}, bf16[1024,384]{1,0:T(8,128)(2,1)}, u32[]{:S(2)}, u32[]{:S(2)}) collective-permute-start(bf16[1024,384]{1,0:T(8,128)(2,1)} %collective-permute-done.refs_1_), channel_id=1, source_target_pairs={{0,16},{16,0},{1,17},{17,1},{2,18},{18,2},{3,19},{19,3},{4,20},{20... | collective-permute-start | bytes 2359304 | tf_op jit(solution)/shard_map/ppermute | solution.py:1133
  519.0 2.6 copy-start.5
  519.0 533.4 %all-gather.5.cloned.1.call-start = ((), (), s32[]{:S(2)}) async-start(), calls=%async_computation.3 | async-start | bytes 3932160 | tf_op jit(solution)/shard_map/all_gather | solution.py:1393
  521.6 1.6 copy-start.13
  521.6 14.2 %slice-start.2 = ((s8[12582912]{0:T(1024)(128)(4,1)}), s8[4194304]{0:T(1024)(128)(4,1)S(1)}, s32[]{:S(2)}) async-start(s8[12582912]{0:T(1024)(128)(4,1)} %bitcast.71), calls=%async_computation.6 | async-start | bytes 8388608
  523.2 12.6 %copy-start.1 = (bf16[2048,1024]{1,0:T(8,128)(2,1)}, bf16[2048,1024]{1,0:T(8,128)(2,1)S(1)}, u32[]{:S(2)}) copy-start(bf16[2048,1024]{1,0:T(8,128)(2,1)S(1)} %constant_dynamic-update-slice_fusion.refs_0_) | copy-start | bytes 12582916
  523.2 12.7 %slice-start.3 = ((s8[12582912]{0:T(1024)(128)(4,1)}), s8[4194304]{0:T(1024)(128)(4,1)S(1)}, s32[]{:S(2)}) async-start(s8[12582912]{0:T(1024)(128)(4,1)} %bitcast.71), calls=%async_computation.7 | async-start | bytes 8388608
  523.2 12.7 %slice-start.4 = ((s8[12582912]{0:T(1024)(128)(4,1)}), s8[4194304]{0:T(1024)(128)(4,1)S(1)}, s32[]{:S(2)}) async-start(s8[12582912]{0:T(1024)(128)(4,1)} %bitcast.71), calls=%async_computation.8 | async-start | bytes 8388608
  550.2 3.6 copy-start.2
  553.8 269.3 %collective-permute-start.7 = (bf16[1536,1024]{1,0:T(8,128)(2,1)}, bf16[1536,1024]{1,0:T(8,128)(2,1)}, u32[]{:S(2)}, u32[]{:S(2)}) collective-permute-start(bf16[1536,1024]{1,0:T(8,128)(2,1)} %constant_dynamic-slice_fusion.15), channel_id=1, source_target_pairs={{0,16},{16,0},{1,17},{17,1},{2,18},{18,2},{3,19},{19,3},{4,20},{20... | collective-permute-start | bytes 9437192 | tf_op jit(solution)/shard_map/ppermute | solution.py:1148
  764.1 2.5 copy-start.12
  764.1 2.6 copy-start.4
  765.1 43.1 %collective-permute-start.15 = (bf16[1536,192]{0,1:T(8,128)(2,1)}, bf16[1536,192]{0,1:T(8,128)(2,1)}, u32[]{:S(2)}, u32[]{:S(2)}) collective-permute-start(bf16[1536,192]{0,1:T(8,128)(2,1)} %constant_dynamic-slice_fusion.5), channel_id=1, source_target_pairs={{0,16},{16,0},{1,17},{17,1},{2,18},{18,2},{3,19},{19,3},{4,20},{20... | collective-permute-start | bytes 1769480 | tf_op jit(solution)/shard_map/ppermute | solution.py:1148
  768.0 48.2 %collective-permute-start.11 = (bf16[1536,512]{1,0:T(8,128)(2,1)}, bf16[1536,512]{1,0:T(8,128)(2,1)}, u32[]{:S(2)}, u32[]{:S(2)}) collective-permute-start(bf16[1536,512]{1,0:T(8,128)(2,1)} %constant_dynamic-slice_fusion.10), channel_id=1, source_target_pairs={{0,16},{16,0},{1,17},{17,1},{2,18},{18,2},{3,19},{19,3},{4,20},{20... | collective-permute-start | bytes 4718600 | tf_op jit(solution)/shard_map/ppermute | solution.py:1148
  808.2 4.2 copy-start.3
  812.3 12.0 %slice-start = ((s8[6291456]{0:T(1024)(128)(4,1)}), s8[4194304]{0:T(1024)(128)(4,1)S(1)}, s32[]{:S(2)}) async-start(s8[6291456]{0:T(1024)(128)(4,1)} %bitcast.60), calls=%async_computation.4 | async-start | bytes 8388608
  813.3 16.2 %collective-permute-start.18 = (bf16[384,192]{1,0:T(8,128)(2,1)S(1)}, bf16[384,192]{1,0:T(8,128)(2,1)S(1)}, u32[]{:S(2)}, u32[]{:S(2)}) collective-permute-start(bf16[384,192]{1,0:T(8,128)(2,1)S(1)} %get-tuple-element.118), channel_id=1, source_target_pairs={{0,12},{4,0},{8,4},{12,8},{1,13},{5,1},{9,5},{13,9},{2,14},{6,2},{... | collective-permute-start | bytes 442376 | tf_op jit(solution)/shard_map/ppermute | solution.py:1155
  815.7 17.2 %collective-permute-start.17 = (bf16[384,192]{1,0:T(8,128)(2,1)S(1)}, bf16[384,192]{1,0:T(8,128)(2,1)S(1)}, u32[]{:S(2)}, u32[]{:S(2)}) collective-permute-start(bf16[384,192]{1,0:T(8,128)(2,1)S(1)} %get-tuple-element.119), channel_id=1, source_target_pairs={{0,8},{4,12},{8,0},{12,4},{1,9},{5,13},{9,1},{13,5},{2,10},{6,14},... | collective-permute-start | bytes 442376 | tf_op jit(solution)/shard_map/ppermute | solution.py:1155
  815.7 8.7 slice-start.1
  815.7 17.7 %collective-permute-start.16 = (bf16[384,192]{1,0:T(8,128)(2,1)S(1)}, bf16[384,192]{1,0:T(8,128)(2,1)S(1)}, u32[]{:S(2)}, u32[]{:S(2)}) collective-permute-start(bf16[384,192]{1,0:T(8,128)(2,1)S(1)} %get-tuple-element.120), channel_id=1, source_target_pairs={{0,4},{4,8},{8,12},{12,0},{1,5},{5,9},{9,13},{13,1},{2,6},{6,10},{... | collective-permute-start | bytes 442376 | tf_op jit(solution)/shard_map/ppermute | solution.py:1155
  820.1 32.9 %collective-permute-start.14 = (bf16[384,512]{1,0:T(8,128)(2,1)S(1)}, bf16[384,512]{1,0:T(8,128)(2,1)S(1)}, u32[]{:S(2)}, u32[]{:S(2)}) collective-permute-start(bf16[384,512]{1,0:T(8,128)(2,1)S(1)} %get-tuple-element.112), channel_id=1, source_target_pairs={{0,12},{4,0},{8,4},{12,8},{1,13},{5,1},{9,5},{13,9},{2,14},{6,2},{... | collective-permute-start | bytes 1179656 | tf_op jit(solution)/shard_map/ppermute | solution.py:1155
  823.2 220.0 %collective-permute-start.13 = (bf16[384,512]{1,0:T(8,128)(2,1)}, bf16[384,512]{1,0:T(8,128)(2,1)}, u32[]{:S(2)}, u32[]{:S(2)}) collective-permute-start(bf16[384,512]{1,0:T(8,128)(2,1)} %get-tuple-element.113), channel_id=1, source_target_pairs={{0,8},{4,12},{8,0},{12,4},{1,9},{5,13},{9,1},{13,5},{2,10},{6,14},... | collective-permute-start | bytes 1179656 | tf_op jit(solution)/shard_map/ppermute | solution.py:1155
  827.8 31.2 %copy-start = (bf16[2048,768]{1,0:T(8,128)(2,1)S(1)}, bf16[2048,768]{1,0:T(8,128)(2,1)}, u32[]{:S(2)}) copy-start(bf16[2048,768]{1,0:T(8,128)(2,1)} %attend_back.1.refs_0_) | copy-start | bytes 9437188
  829.5 29.4 %copy-start.9 = (bf16[384,192]{1,0:T(8,128)(2,1)}, bf16[384,192]{1,0:T(8,128)(2,1)S(1)}, u32[]{:S(2)}) copy-start(bf16[384,192]{1,0:T(8,128)(2,1)S(1)} %collective-permute-done.18.refs_11_) | copy-start | bytes 442372
  829.5 213.6 %collective-permute-start.12 = (bf16[384,512]{1,0:T(8,128)(2,1)}, bf16[384,512]{1,0:T(8,128)(2,1)}, u32[]{:S(2)}, u32[]{:S(2)}) collective-permute-start(bf16[384,512]{1,0:T(8,128)(2,1)} %get-tuple-element.114), channel_id=1, source_target_pairs={{0,4},{4,8},{8,12},{12,0},{1,5},{5,9},{9,13},{13,1},{2,6},{6,10},{... | collective-permute-start | bytes 1179656 | tf_op jit(solution)/shard_map/ppermute | solution.py:1155
  832.9 26.0 %copy-start.10 = (bf16[384,192]{1,0:T(8,128)(2,1)}, bf16[384,192]{1,0:T(8,128)(2,1)S(1)}, u32[]{:S(2)}) copy-start(bf16[384,192]{1,0:T(8,128)(2,1)S(1)} %collective-permute-done.17.refs_10_) | copy-start | bytes 442372
  832.9 210.3 %collective-permute-start.10 = (bf16[384,1024]{1,0:T(8,128)(2,1)}, bf16[384,1024]{1,0:T(8,128)(2,1)}, u32[]{:S(2)}, u32[]{:S(2)}) collective-permute-start(bf16[384,1024]{1,0:T(8,128)(2,1)} %get-tuple-element.104), channel_id=1, source_target_pairs={{0,12},{4,0},{8,4},{12,8},{1,13},{5,1},{9,5},{13,9},{2,14},{6,2},{... | collective-permute-start | bytes 2359304 | tf_op jit(solution)/shard_map/ppermute | solution.py:1155
  833.4 25.6 %copy-start.11 = (bf16[384,192]{1,0:T(8,128)(2,1)}, bf16[384,192]{1,0:T(8,128)(2,1)S(1)}, u32[]{:S(2)}) copy-start(bf16[384,192]{1,0:T(8,128)(2,1)S(1)} %collective-permute-done.16.refs_9_) | copy-start | bytes 442372
  833.4 209.8 %collective-permute-start.9 = (bf16[384,1024]{1,0:T(8,128)(2,1)}, bf16[384,1024]{1,0:T(8,128)(2,1)}, u32[]{:S(2)}, u32[]{:S(2)}) collective-permute-start(bf16[384,1024]{1,0:T(8,128)(2,1)} %get-tuple-element.105), channel_id=1, source_target_pairs={{0,8},{4,12},{8,0},{12,4},{1,9},{5,13},{9,1},{13,5},{2,10},{6,14},... | collective-permute-start | bytes 2359304 | tf_op jit(solution)/shard_map/ppermute | solution.py:1155
  853.0 5.9 copy-start.7
  853.0 190.1 %collective-permute-start.8 = (bf16[384,1024]{1,0:T(8,128)(2,1)}, bf16[384,1024]{1,0:T(8,128)(2,1)}, u32[]{:S(2)}, u32[]{:S(2)}) collective-permute-start(bf16[384,1024]{1,0:T(8,128)(2,1)} %get-tuple-element.106), channel_id=1, source_target_pairs={{0,4},{4,8},{8,12},{12,0},{1,5},{5,9},{9,13},{13,1},{2,6},{6,10},{... | collective-permute-start | bytes 2359304 | tf_op jit(solution)/shard_map/ppermute | solution.py:1155
Sparse Core Ops, SparseCore 0:
  125.6 168.5 all-gather.2
  519.1 187.9 reduce-scatter.1
  812.5 27.1 all-gather.4

commit v4 on v3

--- a/solution.py
+++ b/solution.py
@@ -471,6 +471,10 @@
         r = pl.ds(s * sub, sub)
         return remote(zsend.at[cc, r], zrecv.at[1, cc, r], z_sems.at[1, cc, s], {"ctx": c - 1})
 
+    def z_got(into, cc, s):
+        r = pl.ds(s * sub, sub)
+        remote(zsend.at[cc, r], zrecv.at[into, cc, r], z_sems.at[into, cc, s], ydev).wait_recv()
+
     if last or moves:
         greet_all(c, y, k, size, groups)
     else:
@@ -538,7 +542,7 @@
     def pass_on(cc, s, into, edge, send):
         @pl.when(jnp.logical_not(edge))
         def _():
-            send(cc, s).wait_recv()
+            z_got(into, cc, s)
 
             def add(r):
                 part_sum = qown[cc, r, :] + yrecv[cc, r, :].astype(jnp.float32)
@@ -620,11 +624,11 @@
 
         @pl.when(c > 0)
         def _():
-            z_up(c, s).wait_recv()
+            z_got(0, c, s)
 
         @pl.when(c < size - 1)
         def _():
-            z_down(c, s).wait_recv()
+            z_got(1, c, s)
 
         def close(r):
             sum_up(r)

time: 1070 us -> 1070 us (level)
  no operation moved by 1% of the time
where the time goes in v4:
time: 1070 us; the launch traced here: 1060 us
  Pallas kernels  739 us (69%)
  waiting for transfers between devices  113 us (11%)
  matrix products  60.2 us (6%)
  starting transfers between devices  58.3 us (5%)
  local copies, waits for them, and re-layouts  57.3 us (5%)
  other arithmetic  19.9 us (2%)
  between operations  14.6 us (1%)
    pallas_call x3, Pallas kernels, reduce_call(): pl.pallas_call(functools.partial(reduce_kernel, size, groups, last, plan...  351 us
    pallas_call x3, Pallas kernels, gather_call(): pl.pallas_call(functools.partial(gather_kernel, size, groups, plan or {},...  283 us
    ppermute x3, waiting for transfers between devices, cross(): lax.ppermute(piece, 'ctx', [(i, (i + s) % size) for i in range(size)])  110 us
    dot_general x4, matrix products, tn(): lax.dot_general(left, right, (((0,), (0,)), ((), ())), preferred_element_...  48.5 us
    pallas_call x1, Pallas kernels, attend_back_call(): pl.pallas_call(functools.partial(attend_back_kernel, heads, scale), out_s...  37 us
    ppermute x9, starting transfers between devices, hand_out(): lax.ppermute(piece, 'ctx', [(i, (i + s) % size) for i in range(size)])  33.4 us
    pallas_call x1, Pallas kernels, attend_call(): pl.pallas_call(functools.partial(attend_kernel, heads, scale), out_shape=...  23.5 us
  transfers between devices with their start and end apart: 22, of which 3 were waited for; matrix products, arithmetic and copies ran while one was open for 10% of the time, Pallas kernels for 51%

profile of v4, /device:TPU:0, one launch (start us, length us, event | category | flops | bytes accessed | tf_op | source)
XLA Modules:
  0.0 1062.9 jit_solution(12728133185819036155)
XLA Ops:
  8.7 2.1 dynamic-slice_bitcast_fusion.4.refs_0_.refs_2_
  10.8 2.1 dynamic-slice_bitcast_fusion.5.refs_3_
  12.9 1.1 copy.44
  14.3 1.4 pad_maximum_fusion.refs_1_.refs_0_
  15.7 109.7 %shard_map.152 = (bf16[2048,3072]{1,0:T(8,128)(2,1)}, bf16[8,592,384]{2,1,0:T(8,128)(2,1)}, bf16[8,192,384]{2,1,0:T(8,128)(2,1)}) custom-call(bf16[128,3072]{1,0:T(8,128)(2,1)} %dynamic-slice_bitcast_fusion.4.refs_0_.refs_2_, bf16[4,592,384]{2,1,0:T(8,128)(2,1)} %pad_maximum_fusion.refs_1_.refs_0_, bf16[4,192,384]{2,1,0:T(8,128)(2,1)} %bitcast.67), custom_call_target="tpu_custom_call" | custom-call | bytes 225000000 | tf_op jit(solution)/shard_map/pallas_call | solution.py:367
  125.6 6.2 reshape.105
  131.7 5.1 copy.47
  136.9 1.7 dynamic-slice_bitcast_fusion
  138.6 1.0 collective-permute-start.2
  139.6 13.1 %collective-permute-start.1 = (bf16[1024,384]{1,0:T(8,128)(2,1)}, bf16[1024,384]{1,0:T(8,128)(2,1)}, u32[]{:S(2)}, u32[]{:S(2)}) collective-permute-start(bf16[1024,384]{1,0:T(8,128)(2,1)} %get-tuple-element.109), channel_id=1, source_target_pairs={{0,8},{4,12},{8,0},{12,4},{1,9},{5,13},{9,1},{13,5},{2,10},{6,14},... | collective-permute-start | bytes 2359304 | tf_op jit(solution)/shard_map/ppermute | solution.py:1132
  152.7 1.7 collective-permute-start
  155.7 3.7 fusion.2
  159.5 2.5 pad_maximum_fusion.1
  162.6 1.3 copy.46.col_ref
  163.9 2.6 shard_map.154.refs_1_
  166.6 5.2 shard_map.153.w_ref.refs_1_
  172.6 16.4 %collective-permute-done.2.refs_3_ = bf16[1024,384]{1,0:T(8,128)(2,1)} collective-permute-done((bf16[1024,384]{1,0:T(8,128)(2,1)}, bf16[1024,384]{1,0:T(8,128)(2,1)}, u32[]{:S(2)}, u32[]{:S(2)}) %collective-permute-start.2) | collective-permute-done | bytes 786464 | tf_op jit(solution)/shard_map/ppermute | solution.py:1132
  189.0 1.0 collective-permute-start.6
  190.0 93.3 %collective-permute-done.1.refs_2_ = bf16[1024,384]{1,0:T(8,128)(2,1)} collective-permute-done((bf16[1024,384]{1,0:T(8,128)(2,1)}, bf16[1024,384]{1,0:T(8,128)(2,1)}, u32[]{:S(2)}, u32[]{:S(2)}) %collective-permute-start.1) | collective-permute-done | bytes 786464 | tf_op jit(solution)/shard_map/ppermute | solution.py:1132
  283.4 1.5 collective-permute-start.5
  286.0 19.0 %qkv.1 = (bf16[2048,768]{1,0:T(8,128)(2,1)}, bf16[2048,3072]{1,0:T(8,128)(2,1)}) custom-call(bf16[2048,3072]{1,0:T(8,128)(2,1)} %get-tuple-element.44.x_ref, bf16[784,3072]{1,0:T(8,128)(2,1)} %shard_map.153.w_ref.refs_1_, f32[1,3072]{1,0:T(1,128)} %get-tuple-element.123.gain_ref.refs_4_, f32[2048,128]{1,0:T(8,128)} %get-tuple-element.117.cos_ref, ...), custom_call_target="tpu_custom_call" | custom-call | bytes 54000000 | tf_op jit(solution)/shard_map/qkv/pallas_call | solution.py:874
  305.0 1.2 and_select_fusion.low_ref
  306.2 23.5 %attend.1 = (bf16[2048,256]{1,0:T(8,128)(2,1)}, f32[2,2048]{1,0:T(2,128)}) custom-call(s32[8]{0:T(128)} %and_select_fusion.low_ref, bf16[2048,768]{1,0:T(8,128)(2,1)} %get-tuple-element.46.qkv_ref, s32[2048,1]{1,0:T(8,128)} %copy.46.col_ref, s32[1,2048]{1,0:T(1,128)} %row_ref.3), custom_call_target="tpu_custom_call" | custom-call | bytes 60000000 | tf_op jit(solution)/shard_map/attend/pallas_call | solution.py:950
  329.7 83.9 %shard_map.155 = (f32[128,3072]{1,0:T(8,128)}, bf16[128,3072]{1,0:T(8,128)(2,1)}, bf16[8,512,384]{2,1,0:T(8,128)(2,1)}) custom-call(bf16[2048,256]{1,0:T(8,128)(2,1)} %get-tuple-element.47.refs_0_.out_ref, bf16[256,3072]{1,0:T(8,128)(2,1)} %shard_map.154.refs_1_, bf16[128,3072]{1,0:T(8,128)(2,1)} %dynamic-slice_bitcast_fusion.4.refs_0_.refs_2_, ...), custom_call_target="tpu_custom_call" | custom-call | bytes 255000000 | tf_op jit(solution)/shard_map/pallas_call | solution.py:762
  413.6 3.6 shard_map.157.refs_2_
  417.3 5.6 shard_map.156.refs_1_
  422.9 84.4 %shard_map.158 = (bf16[2048,3072]{1,0:T(8,128)(2,1)}, bf16[2048,512]{1,0:T(8,128)(2,1)}, bf16[2048,512]{1,0:T(8,128)(2,1)}, bf16[2048,512]{1,0:T(8,128)(2,1)}) custom-call(bf16[128,3072]{1,0:T(8,128)(2,1)} %get-tuple-element.50.refs_0_, bf16[1024,3072]{1,0:T(8,128)(2,1)} %shard_map.156.refs_1_, bf16[512,3072]{1,0:T(8,128)(2,1)} %shard_map.157.refs_2_, ...), custom_call_target="tpu_custom_call" | custom-call | bytes 225000000 | tf_op jit(solution)/shard_map/pallas_call | solution.py:367
  507.2 11.7 %convolution_convert_fusion = bf16[2048,3072]{1,0:T(8,128)(2,1)} fusion(bf16[2048,512]{1,0:T(8,128)(2,1)} %get-tuple-element.53, bf16[512,3072]{1,0:T(8,128)(2,1)} %shard_map.157.refs_2_), kind=kOutput, calls=%fused_computation | convolution fusion | flops 6448742400 | bytes 17825792 | tf_op jit(solution)/shard_map/dot_general | solution.py:849
  519.5 2.0 constant_dynamic-update-slice_fusion.1
  521.9 1.2 copy-done.13
  523.2 12.6 %convolution_convert_fusion.3 = bf16[3072,512]{1,0:T(8,128)(2,1)} fusion(bf16[2048,3072]{1,0:T(8,128)(2,1)} %all-gather.3.cloned.1.call-done.refs_3_, bf16[2048,512]{1,0:T(8,128)(2,1)S(1)} %copy-done.13), kind=kOutput, calls=%fused_computation.4 | convolution fusion | flops 6444023808 | bytes 17825792 | tf_op jit(solution)/shard_map/dot_general | solution.py:853
  535.8 14.4 %convolution_convert_fusion.1 = bf16[3072,1024]{1,0:T(8,128)(2,1)S(1)} fusion(bf16[2048,3072]{1,0:T(8,128)(2,1)S(1)} %bitcast.72, bf16[2048,1024]{1,0:T(8,128)(2,1)S(1)} %constant_dynamic-update-slice_fusion.refs_0_), kind=kOutput, calls=%fused_computation.2 | convolution fusion | flops 12888047616 | bytes 23068672 | tf_op jit(solution)/shard_map/dot_general | solution.py:853
  550.2 2.2 constant_dynamic-slice_fusion.15
  552.4 1.4 copy-done.2
  553.8 2.5 collective-permute-start.7
  556.3 110.9 %shard_map.159 = (f32[128,3072]{1,0:T(8,128)}, bf16[128,3072]{1,0:T(8,128)(2,1)}, f32[16,3072]{1,0:T(8,128)}) custom-call(bf16[2048,1024]{1,0:T(8,128)(2,1)} %copy-done.1, bf16[1024,3072]{1,0:T(8,128)(2,1)} %shard_map.156.refs_1_, f32[128,3072]{1,0:T(8,128)} %get-tuple-element.49.refs_2_, bf16[128,3072]{1,0:T(8,128)(2,1)} %dynamic-slice_bitcast_fusion.5.refs_3_, ...), custom_call_target="tpu_custom_call" | custom-call | bytes 255000000 | tf_op jit(solution)/shard_map/pallas_call | solution.py:762
  667.3 88.5 %shard_map.160 = (bf16[2048,3072]{1,0:T(8,128)(2,1)}, bf16[2048,256]{1,0:T(8,128)(2,1)}) custom-call(bf16[128,3072]{1,0:T(8,128)(2,1)} %get-tuple-element.60.refs_0_, bf16[256,3072]{1,0:T(8,128)(2,1)} %shard_map.154.refs_1_), custom_call_target="tpu_custom_call" | custom-call | bytes 225000000 | tf_op jit(solution)/shard_map/pallas_call | solution.py:367
  755.8 8.3 convolution_convert_fusion.4
  765.1 1.6 collective-permute-start.15
  766.8 1.3 constant_dynamic-slice_fusion.10
  768.0 1.0 collective-permute-start.11
  769.6 1.6 copy.48
  771.2 37.0 %attend_back.1.refs_0_ = bf16[2048,768]{1,0:T(8,128)(2,1)} custom-call(s32[8]{0:T(128)} %broadcast_add_fusion.high_ref, bf16[2048,768]{1,0:T(8,128)(2,1)} %get-tuple-element.46.qkv_ref, bf16[2048,256]{1,0:T(8,128)(2,1)} %get-tuple-element.47.refs_0_.out_ref, bf16[2048,256]{1,0:T(8,128)(2,1)} %get-tuple-element.64.grad_ref, ...), custom_call_target="tpu_custom_call" | custom-call | bytes 96000000 | tf_op jit(solution)/shard_map/attend_back/pallas_call | solution.py:1044
  808.2 1.5 copy.49
  809.7 2.6 add_convert_fusion.3
  813.3 2.4 collective-permute-start.18
  816.3 2.7 add_convert_fusion.1
  819.0 1.1 constant_dynamic-slice_fusion.6
  820.1 3.0 collective-permute-start.14
  823.2 1.2 collective-permute-start.13
  824.4 3.4 add_convert_fusion
  827.8 1.7 constant_dynamic-slice_fusion.11
  829.6 3.3 collective-permute-done.17.refs_10_
  833.4 19.6 %collective-permute-start.9 = (bf16[384,1024]{1,0:T(8,128)(2,1)}, bf16[384,1024]{1,0:T(8,128)(2,1)}, u32[]{:S(2)}, u32[]{:S(2)}) collective-permute-start(bf16[384,1024]{1,0:T(8,128)(2,1)} %get-tuple-element.105), channel_id=1, source_target_pairs={{0,8},{4,12},{8,0},{12,4},{1,9},{5,13},{9,1},{13,5},{2,10},{6,14},... | collective-permute-start | bytes 2359304 | tf_op jit(solution)/shard_map/ppermute | solution.py:1159
  853.0 5.9 collective-permute-start.8
  859.0 13.1 %convolution_convert_fusion.2 = bf16[3072,768]{0,1:T(8,128)(2,1)S(1)} fusion(bf16[2048,3072]{1,0:T(8,128)(2,1)} %get-tuple-element.66, bf16[2048,768]{1,0:T(8,128)(2,1)S(1)} %copy-done), kind=kOutput, calls=%fused_computation.3 | convolution fusion | flops 9666035712 | bytes 20447232 | tf_op jit(solution)/shard_map/dot_general | solution.py:853
  872.4 3.7 copy.51.refs_6_
  876.1 156.3 %shard_map.161 = (bf16[4,128,3072]{2,1,0:T(8,128)(2,1)}, f32[8,3072]{1,0:T(8,128)}, bf16[4,384,576]{2,1,0:T(8,128)(2,1)}) custom-call(bf16[2048,768]{1,0:T(8,128)(2,1)} %attend_back.1.refs_0_, bf16[784,3072]{1,0:T(8,128)(2,1)} %shard_map.153.w_ref.refs_1_, bf16[128,3072]{1,0:T(8,128)(2,1)} %dynamic-slice_bitcast_fusion.4.refs_0_.refs_2_, ...), custom_call_target="tpu_custom_call" | custom-call | bytes 255000000 | tf_op jit(solution)/shard_map/pallas_call | solution.py:762
  1032.4 4.2 copy.52
  1036.5 2.2 copy.53
  1038.8 2.9 copy.54
  1041.7 1.4 dynamic-slice_reduce_fusion
  1043.2 9.2 finish.1
  1052.4 3.8 copy.57
  (96 shorter events, 10.7 us)
Async XLA Ops:
  7.2 5.7 copy-start.6
  7.2 415.7 %all-gather.3.cloned.1.call-start = ((), (), s32[]{:S(2)}) async-start(), calls=%async_computation.1 | async-start | bytes 13369344 | tf_op jit(solution)/shard_map/all_gather | solution.py:1200
  125.5 684.2 %reduce-scatter.2.cloned.1.call-start = ((), (), s32[]{:S(2)}) async-start(), calls=%async_computation.2 | async-start | bytes 13369344 | tf_op jit(solution)/shard_map/reduce_scatter | solution.py:1395
  136.8 18.0 %copy-start.8 = (s32[1,2048]{1,0:T(1,128)S(1)}, s32[1,2048]{1,0:T(1,128)}, u32[]{:S(2)}) copy-start(s32[1,2048]{1,0:T(1,128)} %row_ref.3) | copy-start | bytes 24580
  138.6 50.4 %collective-permute-start.2 = (bf16[1024,384]{1,0:T(8,128)(2,1)}, bf16[1024,384]{1,0:T(8,128)(2,1)}, u32[]{:S(2)}, u32[]{:S(2)}) collective-permute-start(bf16[1024,384]{1,0:T(8,128)(2,1)} %get-tuple-element.108), channel_id=1, source_target_pairs={{0,12},{4,0},{8,4},{12,8},{1,13},{5,1},{9,5},{13,9},{2,14},{6,2},{... | collective-permute-start | bytes 2359304 | tf_op jit(solution)/shard_map/ppermute | solution.py:1132
  139.6 143.8 %collective-permute-start.1 = (bf16[1024,384]{1,0:T(8,128)(2,1)}, bf16[1024,384]{1,0:T(8,128)(2,1)}, u32[]{:S(2)}, u32[]{:S(2)}) collective-permute-start(bf16[1024,384]{1,0:T(8,128)(2,1)} %get-tuple-element.109), channel_id=1, source_target_pairs={{0,8},{4,12},{8,0},{12,4},{1,9},{5,13},{9,1},{13,5},{2,10},{6,14},... | collective-permute-start | bytes 2359304 | tf_op jit(solution)/shard_map/ppermute | solution.py:1132
  152.7 132.2 %collective-permute-start = (bf16[1024,384]{1,0:T(8,128)(2,1)}, bf16[1024,384]{1,0:T(8,128)(2,1)}, u32[]{:S(2)}, u32[]{:S(2)}) collective-permute-start(bf16[1024,384]{1,0:T(8,128)(2,1)} %get-tuple-element.110), channel_id=1, source_target_pairs={{0,4},{4,8},{8,12},{12,0},{1,5},{5,9},{9,13},{13,1},{2,6},{6,10},{... | collective-permute-start | bytes 2359304 | tf_op jit(solution)/shard_map/ppermute | solution.py:1132
  154.3 262.9 %collective-permute-start.3 = (bf16[1024,384]{1,0:T(8,128)(2,1)}, bf16[1024,384]{1,0:T(8,128)(2,1)}, u32[]{:S(2)}, u32[]{:S(2)}) collective-permute-start(bf16[1024,384]{1,0:T(8,128)(2,1)} %get-tuple-element.111.refs_0_), channel_id=1, source_target_pairs={{0,16},{16,0},{1,17},{17,1},{2,18},{18,2},{3,19},{19,3},{4,20},{20... | collective-permute-start | bytes 2359304 | tf_op jit(solution)/shard_map/ppermute | solution.py:1137
  189.0 228.2 %collective-permute-start.6 = (bf16[1024,384]{1,0:T(8,128)(2,1)}, bf16[1024,384]{1,0:T(8,128)(2,1)}, u32[]{:S(2)}, u32[]{:S(2)}) collective-permute-start(bf16[1024,384]{1,0:T(8,128)(2,1)} %collective-permute-done.2.refs_3_), channel_id=1, source_target_pairs={{0,16},{16,0},{1,17},{17,1},{2,18},{18,2},{3,19},{19,3},{4,20},{20... | collective-permute-start | bytes 2359304 | tf_op jit(solution)/shard_map/ppermute | solution.py:1137
  283.4 133.9 %collective-permute-start.5 = (bf16[1024,384]{1,0:T(8,128)(2,1)}, bf16[1024,384]{1,0:T(8,128)(2,1)}, u32[]{:S(2)}, u32[]{:S(2)}) collective-permute-start(bf16[1024,384]{1,0:T(8,128)(2,1)} %collective-permute-done.1.refs_2_), channel_id=1, source_target_pairs={{0,16},{16,0},{1,17},{17,1},{2,18},{18,2},{3,19},{19,3},{4,20},{20... | collective-permute-start | bytes 2359304 | tf_op jit(solution)/shard_map/ppermute | solution.py:1137
  284.8 132.4 %collective-permute-start.4 = (bf16[1024,384]{1,0:T(8,128)(2,1)}, bf16[1024,384]{1,0:T(8,128)(2,1)}, u32[]{:S(2)}, u32[]{:S(2)}) collective-permute-start(bf16[1024,384]{1,0:T(8,128)(2,1)} %collective-permute-done.refs_1_), channel_id=1, source_target_pairs={{0,16},{16,0},{1,17},{17,1},{2,18},{18,2},{3,19},{19,3},{4,20},{20... | collective-permute-start | bytes 2359304 | tf_op jit(solution)/shard_map/ppermute | solution.py:1137
  519.0 2.6 copy-start.5
  519.0 533.4 %all-gather.5.cloned.1.call-start = ((), (), s32[]{:S(2)}) async-start(), calls=%async_computation.3 | async-start | bytes 3932160 | tf_op jit(solution)/shard_map/all_gather | solution.py:1397
  521.6 1.6 copy-start.13
  521.6 14.2 %slice-start.2 = ((s8[12582912]{0:T(1024)(128)(4,1)}), s8[4194304]{0:T(1024)(128)(4,1)S(1)}, s32[]{:S(2)}) async-start(s8[12582912]{0:T(1024)(128)(4,1)} %bitcast.71), calls=%async_computation.6 | async-start | bytes 8388608
  523.2 12.6 %copy-start.1 = (bf16[2048,1024]{1,0:T(8,128)(2,1)}, bf16[2048,1024]{1,0:T(8,128)(2,1)S(1)}, u32[]{:S(2)}) copy-start(bf16[2048,1024]{1,0:T(8,128)(2,1)S(1)} %constant_dynamic-update-slice_fusion.refs_0_) | copy-start | bytes 12582916
  523.2 12.7 %slice-start.3 = ((s8[12582912]{0:T(1024)(128)(4,1)}), s8[4194304]{0:T(1024)(128)(4,1)S(1)}, s32[]{:S(2)}) async-start(s8[12582912]{0:T(1024)(128)(4,1)} %bitcast.71), calls=%async_computation.7 | async-start | bytes 8388608
  523.2 12.7 %slice-start.4 = ((s8[12582912]{0:T(1024)(128)(4,1)}), s8[4194304]{0:T(1024)(128)(4,1)S(1)}, s32[]{:S(2)}) async-start(s8[12582912]{0:T(1024)(128)(4,1)} %bitcast.71), calls=%async_computation.8 | async-start | bytes 8388608
  550.2 3.6 copy-start.2
  553.8 269.3 %collective-permute-start.7 = (bf16[1536,1024]{1,0:T(8,128)(2,1)}, bf16[1536,1024]{1,0:T(8,128)(2,1)}, u32[]{:S(2)}, u32[]{:S(2)}) collective-permute-start(bf16[1536,1024]{1,0:T(8,128)(2,1)} %constant_dynamic-slice_fusion.15), channel_id=1, source_target_pairs={{0,16},{16,0},{1,17},{17,1},{2,18},{18,2},{3,19},{19,3},{4,20},{20... | collective-permute-start | bytes 9437192 | tf_op jit(solution)/shard_map/ppermute | solution.py:1152
  764.1 2.5 copy-start.12
  764.1 2.6 copy-start.4
  765.1 43.1 %collective-permute-start.15 = (bf16[1536,192]{0,1:T(8,128)(2,1)}, bf16[1536,192]{0,1:T(8,128)(2,1)}, u32[]{:S(2)}, u32[]{:S(2)}) collective-permute-start(bf16[1536,192]{0,1:T(8,128)(2,1)} %constant_dynamic-slice_fusion.5), channel_id=1, source_target_pairs={{0,16},{16,0},{1,17},{17,1},{2,18},{18,2},{3,19},{19,3},{4,20},{20... | collective-permute-start | bytes 1769480 | tf_op jit(solution)/shard_map/ppermute | solution.py:1152
  768.0 48.2 %collective-permute-start.11 = (bf16[1536,512]{1,0:T(8,128)(2,1)}, bf16[1536,512]{1,0:T(8,128)(2,1)}, u32[]{:S(2)}, u32[]{:S(2)}) collective-permute-start(bf16[1536,512]{1,0:T(8,128)(2,1)} %constant_dynamic-slice_fusion.10), channel_id=1, source_target_pairs={{0,16},{16,0},{1,17},{17,1},{2,18},{18,2},{3,19},{19,3},{4,20},{20... | collective-permute-start | bytes 4718600 | tf_op jit(solution)/shard_map/ppermute | solution.py:1152
  808.2 4.2 copy-start.3
  812.3 12.0 %slice-start = ((s8[6291456]{0:T(1024)(128)(4,1)}), s8[4194304]{0:T(1024)(128)(4,1)S(1)}, s32[]{:S(2)}) async-start(s8[6291456]{0:T(1024)(128)(4,1)} %bitcast.60), calls=%async_computation.4 | async-start | bytes 8388608
  813.3 16.2 %collective-permute-start.18 = (bf16[384,192]{1,0:T(8,128)(2,1)S(1)}, bf16[384,192]{1,0:T(8,128)(2,1)S(1)}, u32[]{:S(2)}, u32[]{:S(2)}) collective-permute-start(bf16[384,192]{1,0:T(8,128)(2,1)S(1)} %get-tuple-element.118), channel_id=1, source_target_pairs={{0,12},{4,0},{8,4},{12,8},{1,13},{5,1},{9,5},{13,9},{2,14},{6,2},{... | collective-permute-start | bytes 442376 | tf_op jit(solution)/shard_map/ppermute | solution.py:1159
  815.7 17.2 %collective-permute-start.17 = (bf16[384,192]{1,0:T(8,128)(2,1)S(1)}, bf16[384,192]{1,0:T(8,128)(2,1)S(1)}, u32[]{:S(2)}, u32[]{:S(2)}) collective-permute-start(bf16[384,192]{1,0:T(8,128)(2,1)S(1)} %get-tuple-element.119), channel_id=1, source_target_pairs={{0,8},{4,12},{8,0},{12,4},{1,9},{5,13},{9,1},{13,5},{2,10},{6,14},... | collective-permute-start | bytes 442376 | tf_op jit(solution)/shard_map/ppermute | solution.py:1159
  815.7 8.7 slice-start.1
  815.7 17.7 %collective-permute-start.16 = (bf16[384,192]{1,0:T(8,128)(2,1)S(1)}, bf16[384,192]{1,0:T(8,128)(2,1)S(1)}, u32[]{:S(2)}, u32[]{:S(2)}) collective-permute-start(bf16[384,192]{1,0:T(8,128)(2,1)S(1)} %get-tuple-element.120), channel_id=1, source_target_pairs={{0,4},{4,8},{8,12},{12,0},{1,5},{5,9},{9,13},{13,1},{2,6},{6,10},{... | collective-permute-start | bytes 442376 | tf_op jit(solution)/shard_map/ppermute | solution.py:1159
  820.1 32.9 %collective-permute-start.14 = (bf16[384,512]{1,0:T(8,128)(2,1)S(1)}, bf16[384,512]{1,0:T(8,128)(2,1)S(1)}, u32[]{:S(2)}, u32[]{:S(2)}) collective-permute-start(bf16[384,512]{1,0:T(8,128)(2,1)S(1)} %get-tuple-element.112), channel_id=1, source_target_pairs={{0,12},{4,0},{8,4},{12,8},{1,13},{5,1},{9,5},{13,9},{2,14},{6,2},{... | collective-permute-start | bytes 1179656 | tf_op jit(solution)/shard_map/ppermute | solution.py:1159
  823.2 220.0 %collective-permute-start.13 = (bf16[384,512]{1,0:T(8,128)(2,1)}, bf16[384,512]{1,0:T(8,128)(2,1)}, u32[]{:S(2)}, u32[]{:S(2)}) collective-permute-start(bf16[384,512]{1,0:T(8,128)(2,1)} %get-tuple-element.113), channel_id=1, source_target_pairs={{0,8},{4,12},{8,0},{12,4},{1,9},{5,13},{9,1},{13,5},{2,10},{6,14},... | collective-permute-start | bytes 1179656 | tf_op jit(solution)/shard_map/ppermute | solution.py:1159
  827.8 31.2 %copy-start = (bf16[2048,768]{1,0:T(8,128)(2,1)S(1)}, bf16[2048,768]{1,0:T(8,128)(2,1)}, u32[]{:S(2)}) copy-start(bf16[2048,768]{1,0:T(8,128)(2,1)} %attend_back.1.refs_0_) | copy-start | bytes 9437188
  829.5 29.4 %copy-start.9 = (bf16[384,192]{1,0:T(8,128)(2,1)}, bf16[384,192]{1,0:T(8,128)(2,1)S(1)}, u32[]{:S(2)}) copy-start(bf16[384,192]{1,0:T(8,128)(2,1)S(1)} %collective-permute-done.18.refs_11_) | copy-start | bytes 442372
  829.5 213.6 %collective-permute-start.12 = (bf16[384,512]{1,0:T(8,128)(2,1)}, bf16[384,512]{1,0:T(8,128)(2,1)}, u32[]{:S(2)}, u32[]{:S(2)}) collective-permute-start(bf16[384,512]{1,0:T(8,128)(2,1)} %get-tuple-element.114), channel_id=1, source_target_pairs={{0,4},{4,8},{8,12},{12,0},{1,5},{5,9},{9,13},{13,1},{2,6},{6,10},{... | collective-permute-start | bytes 1179656 | tf_op jit(solution)/shard_map/ppermute | solution.py:1159
  832.9 26.0 %copy-start.10 = (bf16[384,192]{1,0:T(8,128)(2,1)}, bf16[384,192]{1,0:T(8,128)(2,1)S(1)}, u32[]{:S(2)}) copy-start(bf16[384,192]{1,0:T(8,128)(2,1)S(1)} %collective-permute-done.17.refs_10_) | copy-start | bytes 442372
  832.9 210.3 %collective-permute-start.10 = (bf16[384,1024]{1,0:T(8,128)(2,1)}, bf16[384,1024]{1,0:T(8,128)(2,1)}, u32[]{:S(2)}, u32[]{:S(2)}) collective-permute-start(bf16[384,1024]{1,0:T(8,128)(2,1)} %get-tuple-element.104), channel_id=1, source_target_pairs={{0,12},{4,0},{8,4},{12,8},{1,13},{5,1},{9,5},{13,9},{2,14},{6,2},{... | collective-permute-start | bytes 2359304 | tf_op jit(solution)/shard_map/ppermute | solution.py:1159
  833.4 25.6 %copy-start.11 = (bf16[384,192]{1,0:T(8,128)(2,1)}, bf16[384,192]{1,0:T(8,128)(2,1)S(1)}, u32[]{:S(2)}) copy-start(bf16[384,192]{1,0:T(8,128)(2,1)S(1)} %collective-permute-done.16.refs_9_) | copy-start | bytes 442372
  833.4 209.8 %collective-permute-start.9 = (bf16[384,1024]{1,0:T(8,128)(2,1)}, bf16[384,1024]{1,0:T(8,128)(2,1)}, u32[]{:S(2)}, u32[]{:S(2)}) collective-permute-start(bf16[384,1024]{1,0:T(8,128)(2,1)} %get-tuple-element.105), channel_id=1, source_target_pairs={{0,8},{4,12},{8,0},{12,4},{1,9},{5,13},{9,1},{13,5},{2,10},{6,14},... | collective-permute-start | bytes 2359304 | tf_op jit(solution)/shard_map/ppermute | solution.py:1159
  853.0 5.9 copy-start.7
  853.0 190.1 %collective-permute-start.8 = (bf16[384,1024]{1,0:T(8,128)(2,1)}, bf16[384,1024]{1,0:T(8,128)(2,1)}, u32[]{:S(2)}, u32[]{:S(2)}) collective-permute-start(bf16[384,1024]{1,0:T(8,128)(2,1)} %get-tuple-element.106), channel_id=1, source_target_pairs={{0,4},{4,8},{8,12},{12,0},{1,5},{5,9},{9,13},{13,1},{2,6},{6,10},{... | collective-permute-start | bytes 2359304 | tf_op jit(solution)/shard_map/ppermute | solution.py:1159
Sparse Core Ops, SparseCore 0:
  125.6 168.5 all-gather.2
  519.1 187.9 reduce-scatter.1
  812.5 27.1 all-gather.4
